TPU v7x, 32 devices: a whole 2x2x4 slice. The times are simulated.
32 devices in a mesh: dom: 32 (over z, y, x, core).
Axes of the slice: x: 2, y: 2, z: 4, core: 2. Of those that a mesh axis runs over, the one named last changes fastest.
Arguments:
- features: bfloat16 [32768, 512], P('dom'), may hold values from -6 to 6
- embeddings: bfloat16 [32768, 128], P('dom'), may hold values from -6 to 6
- tile_values: bfloat16 [256, 4, 128, 128], P('dom'), may hold values from -4 to 4
- tile_columns: int32 [256, 4], P('dom'), may hold values from 0 to 11
- send_blocks: int32 [32, 2, 2], P('dom'), may hold values from 0 to 7
- send_count: int32 [32, 2], P('dom'), may hold values from 1 to 2, as said below
- hub_rows: int32 [64], P('dom'), may hold values from 0 to 1023, as said below
- hub_weight: bfloat16 [32768, 64], P('dom'), may hold values from -4 to 4
- degree: int32 [32768], P('dom'), may hold values from 16 to 64
Outputs:
- hop_features: bfloat16 [3, 32768, 512], P(None, 'dom')
- hop_embeddings: bfloat16 [3, 32768, 128], P(None, 'dom')
Inputs may be any that keep to these rules, and one draw needn't show every extreme that they name: `send_count`: some partition sends 2 blocks to its right and some to its left. `hub_rows`: the 2 hub rows of each partition are distinct local row numbers.
All inputs are finite; a program needn't handle non-finite values.
Results may differ from a plain program's by a relative error of at most 0.012.
Values may be sent and summed in bfloat16 or wider, within the bound.
No kernel may reach another device: no remote copies, remote signals or barrier semaphores. Data moves between devices by JAX's collectives and lax.ppermute only.
A program may use at most 64 MiB of HBM per device.

v0:
```python
import jax
import jax.numpy as jnp
from jax import lax
from jax.sharding import PartitionSpec as P

HOPS = 3


def shifted(value, axis, steps):
    count = lax.axis_size(axis)
    initial, last = (max(0, -steps), min(count, count - steps))
    return lax.ppermute(value, axis, [(source, source + steps) for source in range(initial, last)])


def body(
    features,
    embeddings,
    tile_values,
    tile_columns,
    send_blocks,
    send_count,
    hub_rows,
    hub_weight,
    degree,
):
    row_count = features.shape[0]
    tile_size = tile_values.shape[2]
    block_count = row_count // tile_size
    send_most = send_blocks.shape[2]
    feature_width = features.shape[1] + embeddings.shape[1]
    rim_rows = send_most * tile_size
    inverse_root = lax.rsqrt(degree.astype(jnp.float32))[:, None]
    current = jnp.concatenate([features, embeddings], axis=1)
    listed = send_blocks[0].reshape(-1)
    live_slots = (jnp.arange(send_most, dtype=jnp.int32)[None, :] < send_count[0][:, None]).reshape(
        -1
    )
    results = []
    for hop_index in range(HOPS):
        scaled = (current.astype(jnp.float32) * inverse_root).astype(jnp.bfloat16)
        blocked = scaled.reshape(block_count, tile_size, feature_width)
        outgoing = blocked[listed]
        outgoing = jnp.where(live_slots[:, None, None], outgoing, jnp.zeros_like(outgoing))
        outgoing = outgoing.reshape(2 * rim_rows, feature_width)
        hub_local = scaled[hub_rows]
        gathered_hubs = lax.all_gather(hub_local, "dom", axis=0, tiled=True)
        hub_sum = jnp.dot(hub_weight, gathered_hubs, preferred_element_type=jnp.float32)
        from_left = shifted(outgoing[rim_rows:], "dom", 1)
        from_right = shifted(outgoing[:rim_rows], "dom", -1)
        extended = jnp.concatenate(
            [
                blocked,
                from_left.reshape(send_most, tile_size, feature_width),
                from_right.reshape(send_most, tile_size, feature_width),
            ],
            axis=0,
        )
        picked = extended[tile_columns]
        local_part = jnp.einsum(
            "bkij,bkjw->biw", tile_values, picked, preferred_element_type=jnp.float32
        )
        summed = local_part.reshape(row_count, feature_width) + hub_sum
        current = (summed * inverse_root).astype(jnp.bfloat16)
        results.append(current)
    stacked = jnp.stack(results)
    split_at = features.shape[1]
    return (stacked[:, :, :split_at], stacked[:, :, split_at:])


def solution(mesh):
    placed = (
        P("dom", None),
        P("dom", None),
        P("dom", None, None, None),
        P("dom", None),
        P("dom", None, None),
        P("dom", None),
        P("dom"),
        P("dom", None),
        P("dom"),
    )
    return jax.shard_map(
        body,
        mesh=mesh,
        in_specs=placed,
        out_specs=(P(None, "dom", None), P(None, "dom", None)),
        check_vma=False,
    )
```

profile of v0, /device:TPU:0, one launch (start us, length us, event | category | flops | bytes accessed | tf_op | source)
XLA Modules:
  0.0 219.1 jit_solution(10857633315471224269)
XLA Ops:
  0.6 0.8 reshape_squeeze.3
  1.5 0.7 iota_compare_fusion
  2.3 0.7 convert_rsqrt_fusion
  3.0 1.6 multiply_convert_fusion.3
  4.7 1.5 gather_fusion
  6.1 1.2 broadcast_select_fusion.2
  7.4 0.9 fusion.11
  8.3 1.3 collective-permute-start.1
  9.6 3.8 %collective-permute-start = (bf16[256,640]{1,0:T(8,128)(2,1)}, bf16[256,640]{1,0:T(8,128)(2,1)}, u32[]{:S(2)}, u32[]{:S(2)}) collective-permute-start(bf16[256,640]{1,0:T(8,128)(2,1)} %bitcast.5), channel_id=1, source_target_pairs={{0,1},{1,2},{2,3},{3,4},{4,5},{5,6},{6,7},{7,8},{8,9},{9,10},{10,1... | collective-permute-start | bytes 983048 | tf_op jit(solution)/shard_map/ppermute | solution.py:12
  13.3 1.8 copy.43
  15.1 1.3 copy.42
  16.4 1.6 multiply_convert_fusion.2
  18.3 1.5 copy.44
  19.7 2.0 gather_fusion.2
  21.8 43.6 %all-gather.3 = bf16[32,2,640]{2,1,0:T(2,128)(2,1)S(1)} all-gather(bf16[1,2,640]{2,1,0:T(2,128)(2,1)S(1)} %bitcast.103), channel_id=2, replica_groups=mesh['dom'=32] {'dom'}, dimensions={0}, use_global_device_ids=true | all-gather | bytes 84480 | tf_op jit(solution)/shard_map/all_gather | solution.py:46
  65.5 1.8 pad_maximum_fusion.1
  67.3 3.5 %gather_fusion.1 = bf16[32,128,640]{2,1,0:T(8,128)(2,1)} fusion(bf16[12,128,640]{2,1,0:T(8,128)(2,1)S(1)} %pad_maximum_fusion.1, s32[1024]{0:T(1024)S(1)} %pad_clamp_fusion.1), kind=kCustom, calls=%fused_computation.1 | custom fusion | bytes 10485888 | tf_op jit(solution)/shard_map/gather | solution.py:58
  70.8 5.0 %fusion.12 = f32[8,640,128,1]{1,2,3,0:T(8,128)} fusion(bf16[8,4,128,128]{3,2,1,0:T(8,128)(2,1)S(1)} %copy-done, bf16[8,4,128,640]{3,2,1,0:T(8,128)(2,1)} %bitcast.82), kind=kOutput, calls=%fused_computation.44 | convolution fusion | flops 671088640 | bytes 8912896 | tf_op jit(solution)/shard_map/bkij,bkjw->biw/dot_general | solution.py:59
  75.8 3.3 %copy.45 = f32[1024,640]{0,1:T(8,128)} copy(f32[1024,640]{1,0:T(8,128)} %bitcast.88) | data formatting | bytes 5242880 | tf_op jit(solution)/shard_map/reshape | solution.py:62
  79.1 3.8 %multiply_convert_fusion.1 = (bf16[1024,640]{0,1:T(8,128)(2,1)}, bf16[1024,640]{0,1:T(8,128)(2,1)}) fusion(f32[1024]{0:T(1024)S(1)} %get-tuple-element.14, f32[1024,640]{0,1:T(8,128)} %copy.45, bf16[64,640]{1,0:T(8,128)(2,1)S(1)} %reshape.194, bf16[1024,64]{0,1:T(8,128)(2,1)S(1)} %copy-done.7), kind=kOutput, calls=%fused_computation.20 | convolution fusion | flops 87818240 | bytes 5459968 | tf_op jit(solution)/shard_map/dot_general | solution.py:47
  82.8 1.7 copy.61
  84.6 0.7 gather_fusion.3
  85.5 1.3 collective-permute-start.3
  86.8 3.8 %collective-permute-start.2 = (bf16[256,640]{1,0:T(8,128)(2,1)S(1)}, bf16[256,640]{1,0:T(8,128)(2,1)}, u32[]{:S(2)}, u32[]{:S(2)}) collective-permute-start(bf16[256,640]{1,0:T(8,128)(2,1)S(1)} %bitcast.98), channel_id=1, source_target_pairs={{0,1},{1,2},{2,3},{3,4},{4,5},{5,6},{6,7},{7,8},{8,9},{9,10},{10,1... | collective-permute-start | bytes 983048 | tf_op jit(solution)/shard_map/ppermute | solution.py:12
  90.5 1.3 gather_fusion.5
  91.8 37.6 %all-gather.4 = bf16[32,2,640]{2,1,0:T(2,128)(2,1)S(1)} all-gather(bf16[1,2,640]{2,1,0:T(2,128)(2,1)} %bitcast.105), channel_id=3, replica_groups=mesh['dom'=32] {'dom'}, dimensions={0}, use_global_device_ids=true | all-gather | bytes 84480 | tf_op jit(solution)/shard_map/all_gather | solution.py:46
  129.4 0.7 reshape.196
  130.1 1.7 pad_maximum_fusion.2
  131.8 3.5 %gather_fusion.4 = bf16[32,128,640]{2,1,0:T(8,128)(2,1)} fusion(bf16[12,128,640]{2,1,0:T(8,128)(2,1)S(1)} %pad_maximum_fusion.2, s32[1024]{0:T(1024)S(1)} %copy-done.14), kind=kCustom, calls=%fused_computation.4 | custom fusion | bytes 10485888 | tf_op jit(solution)/shard_map/gather | solution.py:58
  135.3 5.0 %fusion.13 = f32[8,640,128,1]{1,2,3,0:T(8,128)} fusion(bf16[8,4,128,128]{3,2,1,0:T(8,128)(2,1)S(1)} %copy-done, bf16[8,4,128,640]{3,2,1,0:T(8,128)(2,1)} %bitcast.83), kind=kOutput, calls=%fused_computation.45 | convolution fusion | flops 671088640 | bytes 8912896 | tf_op jit(solution)/shard_map/bkij,bkjw->biw/dot_general | solution.py:59
  140.3 3.3 %copy.59 = f32[1024,640]{0,1:T(8,128)} copy(f32[1024,640]{1,0:T(8,128)} %bitcast.89) | data formatting | bytes 5242880 | tf_op jit(solution)/shard_map/reshape | solution.py:62
  143.5 3.8 %multiply_convert_fusion = (bf16[1024,640]{0,1:T(8,128)(2,1)}, bf16[1024,640]{0,1:T(8,128)(2,1)}) fusion(f32[1024]{0:T(1024)S(1)} %copy-done.11, f32[1024,640]{0,1:T(8,128)} %copy.59, bf16[64,640]{1,0:T(8,128)(2,1)S(1)} %copy-done.8, bf16[1024,64]{0,1:T(8,128)(2,1)S(1)} %copy-done.7), kind=kOutput, calls=%fused_computation.19 | convolution fusion | flops 87818240 | bytes 5459968 | tf_op jit(solution)/shard_map/dot_general | solution.py:47
  147.3 1.7 copy.62
  149.0 0.8 gather_fusion.6
  150.0 1.3 collective-permute-start.5
  151.3 3.8 %collective-permute-start.4 = (bf16[256,640]{1,0:T(8,128)(2,1)S(1)}, bf16[256,640]{1,0:T(8,128)(2,1)}, u32[]{:S(2)}, u32[]{:S(2)}) collective-permute-start(bf16[256,640]{1,0:T(8,128)(2,1)S(1)} %bitcast.97), channel_id=1, source_target_pairs={{0,1},{1,2},{2,3},{3,4},{4,5},{5,6},{6,7},{7,8},{8,9},{9,10},{10,1... | collective-permute-start | bytes 983048 | tf_op jit(solution)/shard_map/ppermute | solution.py:12
  155.1 1.3 gather_fusion.8
  156.4 37.8 %all-gather.5 = bf16[32,2,640]{2,1,0:T(2,128)(2,1)S(1)} all-gather(bf16[1,2,640]{2,1,0:T(2,128)(2,1)} %bitcast.104), channel_id=4, replica_groups=mesh['dom'=32] {'dom'}, dimensions={0}, use_global_device_ids=true | all-gather | bytes 84480 | tf_op jit(solution)/shard_map/all_gather | solution.py:46
  194.1 0.7 reshape.198
  194.8 1.7 pad_maximum_fusion.3
  196.5 3.5 %gather_fusion.7 = bf16[32,128,640]{2,1,0:T(8,128)(2,1)} fusion(bf16[12,128,640]{2,1,0:T(8,128)(2,1)S(1)} %pad_maximum_fusion.3, s32[1024]{0:T(1024)S(1)} %copy-done.15), kind=kCustom, calls=%fused_computation.7 | custom fusion | bytes 10485888 | tf_op jit(solution)/shard_map/gather | solution.py:58
  200.1 5.0 %fusion.14 = f32[8,640,128,1]{1,2,3,0:T(8,128)} fusion(bf16[8,4,128,128]{3,2,1,0:T(8,128)(2,1)S(1)} %copy-done, bf16[8,4,128,640]{3,2,1,0:T(8,128)(2,1)} %bitcast.81), kind=kOutput, calls=%fused_computation.46 | convolution fusion | flops 671088640 | bytes 8912896 | tf_op jit(solution)/shard_map/bkij,bkjw->biw/dot_general | solution.py:59
  205.0 3.3 %copy.60 = f32[1024,640]{0,1:T(8,128)} copy(f32[1024,640]{1,0:T(8,128)} %bitcast.90) | data formatting | bytes 5242880 | tf_op jit(solution)/shard_map/reshape | solution.py:62
  208.3 2.4 %fusion.6 = bf16[1,1024,640]{1,2,0:T(8,128)(2,1)S(1)} fusion(f32[1024,640]{0,1:T(8,128)} %copy.60, bf16[64,640]{1,0:T(8,128)(2,1)S(1)} %copy-done.9, bf16[1024,64]{0,1:T(8,128)(2,1)S(1)} %copy-done.7, f32[1024]{0:T(1024)S(1)} %copy-done.12), kind=kOutput, calls=%fused_computation.26 | convolution fusion | flops 85852160 | bytes 4149248 | tf_op jit(solution)/shard_map/dot_general | solution.py:47
  210.9 0.5 pad_maximum_fusion
  211.4 1.9 slice.80
  213.3 4.6 %copy.54 = bf16[3,1024,512]{2,1,0:T(8,128)(2,1)} copy(bf16[3,1024,512]{1,2,0:T(8,128)(2,1)} %slice.80) | data formatting | bytes 6291456
  217.9 1.2 copy.55
  (65 shorter events, 0.9 us)
Async XLA Ops:
  0.6 70.2 %copy-start = (bf16[8,4,128,128]{3,2,1,0:T(8,128)(2,1)S(1)}, bf16[8,4,128,128]{3,2,1,0:T(8,128)(2,1)}, u32[]{:S(2)}) copy-start(bf16[8,4,128,128]{3,2,1,0:T(8,128)(2,1)} %param.11) | copy-start | bytes 3145732
  2.3 82.9 %copy-start.18 = (pred[4]{0:T(512)(128)(4,1)}, pred[4]{0:T(512)(128)(4,1)S(1)}, u32[]{:S(2)}) copy-start(pred[4]{0:T(512)(128)(4,1)S(1)} %lt.48) | copy-start | bytes 16
  2.3 82.2 %copy-start.16 = (s32[1024]{0:T(1024)}, s32[1024]{0:T(1024)S(1)}, u32[]{:S(2)}) copy-start(s32[1024]{0:T(1024)S(1)} %pad_clamp_fusion.2) | copy-start | bytes 12292
  3.0 76.0 %copy-start.10 = (f32[1024]{0:T(1024)}, f32[1024]{0:T(1024)S(1)}, u32[]{:S(2)}) copy-start(f32[1024]{0:T(1024)S(1)} %get-tuple-element.14) | copy-start | bytes 12292
  4.6 11.8 %copy-start.5 = (bf16[8,128,640]{2,1,0:T(8,128)(2,1)}, bf16[8,128,640]{2,1,0:T(8,128)(2,1)S(1)}, u32[]{:S(2)}) copy-start(bf16[8,128,640]{2,1,0:T(8,128)(2,1)S(1)} %multiply_convert_fusion.3) | copy-start | bytes 3932164
  4.7 10.4 %copy-start.6 = (bf16[1024,512]{1,0:T(8,128)(2,1)S(1)}, bf16[1024,512]{1,0:T(8,128)(2,1)}, u32[]{:S(2)}) copy-start(bf16[1024,512]{1,0:T(8,128)(2,1)} %param.9) | copy-start | bytes 3145732
  6.1 10.3 %copy-start.20 = (s32[8,4]{0,1:T(4,128)S(1)}, s32[8,4]{0,1:T(4,128)}, u32[]{:S(2)}) copy-start(s32[8,4]{0,1:T(4,128)} %param.12) | copy-start | bytes 388
  8.3 57.2 %collective-permute-start.1 = (bf16[256,640]{1,0:T(8,128)(2,1)}, bf16[256,640]{1,0:T(8,128)(2,1)}, u32[]{:S(2)}, u32[]{:S(2)}) collective-permute-start(bf16[256,640]{1,0:T(8,128)(2,1)} %bitcast.7), channel_id=1, source_target_pairs={{1,0},{2,1},{3,2},{4,3},{5,4},{6,5},{7,6},{8,7},{9,8},{10,9},{11,1... | collective-permute-start | bytes 983048 | tf_op jit(solution)/shard_map/ppermute | solution.py:12
  9.5 8.5 %copy-start.21 = (s32[2]{0:T(128)S(1)}, s32[2]{0:T(128)}, u32[]{:S(2)}) copy-start(s32[2]{0:T(128)} %param.15) | copy-start | bytes 28
  9.6 55.9 %collective-permute-start = (bf16[256,640]{1,0:T(8,128)(2,1)}, bf16[256,640]{1,0:T(8,128)(2,1)}, u32[]{:S(2)}, u32[]{:S(2)}) collective-permute-start(bf16[256,640]{1,0:T(8,128)(2,1)} %bitcast.5), channel_id=1, source_target_pairs={{0,1},{1,2},{2,3},{3,4},{4,5},{5,6},{6,7},{7,8},{8,9},{9,10},{10,1... | collective-permute-start | bytes 983048 | tf_op jit(solution)/shard_map/ppermute | solution.py:12
  19.7 2.1 copy-start.17
  65.4 5.3 %copy-start.13 = (s32[1024]{0:T(1024)}, s32[1024]{0:T(1024)S(1)}, u32[]{:S(2)}) copy-start(s32[1024]{0:T(1024)S(1)} %pad_clamp_fusion.1) | copy-start | bytes 12292
  75.8 3.3 %copy-start.7 = (bf16[1024,64]{0,1:T(8,128)(2,1)S(1)}, bf16[1024,64]{0,1:T(8,128)(2,1)}, u32[]{:S(2)}) copy-start(bf16[1024,64]{0,1:T(8,128)(2,1)} %param.16) | copy-start | bytes 393220
  84.5 45.5 %copy-start.4 = (bf16[1024,640]{1,0:T(8,128)(2,1)}, bf16[1024,640]{1,0:T(8,128)(2,1)S(1)}, u32[]{:S(2)}) copy-start(bf16[1024,640]{1,0:T(8,128)(2,1)S(1)} %copy.61) | copy-start | bytes 3932164
  85.5 44.6 %collective-permute-start.3 = (bf16[256,640]{1,0:T(8,128)(2,1)S(1)}, bf16[256,640]{1,0:T(8,128)(2,1)S(1)}, u32[]{:S(2)}, u32[]{:S(2)}) collective-permute-start(bf16[256,640]{1,0:T(8,128)(2,1)S(1)} %bitcast.100), channel_id=1, source_target_pairs={{1,0},{2,1},{3,2},{4,3},{5,4},{6,5},{7,6},{8,7},{9,8},{10,9},{11,1... | collective-permute-start | bytes 983048 | tf_op jit(solution)/shard_map/ppermute | solution.py:12
  86.8 43.3 %collective-permute-start.2 = (bf16[256,640]{1,0:T(8,128)(2,1)S(1)}, bf16[256,640]{1,0:T(8,128)(2,1)}, u32[]{:S(2)}, u32[]{:S(2)}) collective-permute-start(bf16[256,640]{1,0:T(8,128)(2,1)S(1)} %bitcast.98), channel_id=1, source_target_pairs={{0,1},{1,2},{2,3},{3,4},{4,5},{5,6},{6,7},{7,8},{8,9},{9,10},{10,1... | collective-permute-start | bytes 983048 | tf_op jit(solution)/shard_map/ppermute | solution.py:12
  130.0 1.7 copy-start.14
  140.3 3.3 %copy-start.8 = (bf16[64,640]{1,0:T(8,128)(2,1)S(1)}, bf16[64,640]{1,0:T(8,128)(2,1)}, u32[]{:S(2)}) copy-start(bf16[64,640]{1,0:T(8,128)(2,1)} %reshape.196) | copy-start | bytes 245764
  140.3 3.3 %copy-start.11 = (f32[1024]{0:T(1024)S(1)}, f32[1024]{0:T(1024)}, u32[]{:S(2)}) copy-start(f32[1024]{0:T(1024)} %copy-done.10) | copy-start | bytes 12292
  147.3 2.5 %copy-start.19 = (pred[4]{0:T(512)(128)(4,1)S(1)}, pred[4]{0:T(512)(128)(4,1)}, u32[]{:S(2)}) copy-start(pred[4]{0:T(512)(128)(4,1)} %copy-done.18) | copy-start | bytes 16
  149.0 45.8 %copy-start.3 = (bf16[1024,640]{1,0:T(8,128)(2,1)}, bf16[1024,640]{1,0:T(8,128)(2,1)S(1)}, u32[]{:S(2)}) copy-start(bf16[1024,640]{1,0:T(8,128)(2,1)S(1)} %copy.62) | copy-start | bytes 3932164
  150.0 44.8 %collective-permute-start.5 = (bf16[256,640]{1,0:T(8,128)(2,1)S(1)}, bf16[256,640]{1,0:T(8,128)(2,1)S(1)}, u32[]{:S(2)}, u32[]{:S(2)}) collective-permute-start(bf16[256,640]{1,0:T(8,128)(2,1)S(1)} %bitcast.99), channel_id=1, source_target_pairs={{1,0},{2,1},{3,2},{4,3},{5,4},{6,5},{7,6},{8,7},{9,8},{10,9},{11,1... | collective-permute-start | bytes 983048 | tf_op jit(solution)/shard_map/ppermute | solution.py:12
  151.3 43.5 %collective-permute-start.4 = (bf16[256,640]{1,0:T(8,128)(2,1)S(1)}, bf16[256,640]{1,0:T(8,128)(2,1)}, u32[]{:S(2)}, u32[]{:S(2)}) collective-permute-start(bf16[256,640]{1,0:T(8,128)(2,1)S(1)} %bitcast.97), channel_id=1, source_target_pairs={{0,1},{1,2},{2,3},{3,4},{4,5},{5,6},{6,7},{7,8},{8,9},{9,10},{10,1... | collective-permute-start | bytes 983048 | tf_op jit(solution)/shard_map/ppermute | solution.py:12
  194.8 1.7 copy-start.15
  205.0 3.3 %copy-start.9 = (bf16[64,640]{1,0:T(8,128)(2,1)S(1)}, bf16[64,640]{1,0:T(8,128)(2,1)}, u32[]{:S(2)}) copy-start(bf16[64,640]{1,0:T(8,128)(2,1)} %reshape.198) | copy-start | bytes 245764
  205.0 3.3 %copy-start.12 = (f32[1024]{0:T(1024)S(1)}, f32[1024]{0:T(1024)}, u32[]{:S(2)}) copy-start(f32[1024]{0:T(1024)} %copy-done.10) | copy-start | bytes 12292
  208.3 2.4 %copy-start.1 = (bf16[1024,640]{0,1:T(8,128)(2,1)S(1)}, bf16[1024,640]{0,1:T(8,128)(2,1)}, u32[]{:S(2)}) copy-start(bf16[1024,640]{0,1:T(8,128)(2,1)} %get-tuple-element.17) | copy-start | bytes 3932164
  208.3 2.5 %copy-start.2 = (bf16[1024,640]{0,1:T(8,128)(2,1)S(1)}, bf16[1024,640]{0,1:T(8,128)(2,1)}, u32[]{:S(2)}) copy-start(bf16[1024,640]{0,1:T(8,128)(2,1)} %get-tuple-element.19) | copy-start | bytes 3932164
where the time goes:
time: 220 us; the launch traced here: 219 us
  blocking collectives  119 us (54%)
  local copies, waits for them, and re-layouts  47.2 us (21%)
  matrix products  24.9 us (11%)
  starting transfers between devices  15.1 us (7%)
  other arithmetic  11.9 us (5%)
    all_gather x3, blocking collectives, body(): gathered_hubs = lax.all_gather(hub_local, 'dom', axis=0, tiled=True)  119 us
    ppermute x6, starting transfers between devices, shifted(): lax.ppermute(value, axis, [(source, source + steps) for source in range(i...  15.1 us
    dot_general x3, matrix products, body(): jnp.einsum('bkij,bkjw->biw', tile_values, picked, preferred_element_type=...  14.9 us
    gather x3, local copies, waits for them, and re-layouts, body(): picked = extended[tile_columns]  10.5 us
    unnamed x51, local copies, waits for them, and re-layouts  10.4 us
    dot_general x3, matrix products, body(): jnp.dot(hub_weight, gathered_hubs, preferred_element_type=jnp.float32)  9.96 us
    reshape x3, local copies, waits for them, and re-layouts, body(): summed = local_part.reshape(row_count, feature_width) + hub_sum  9.84 us
    concatenate x3, other arithmetic, body(): jnp.concatenate([blocked, from_left.reshape(send_most, tile_size, feature...  5.18 us
  transfers between devices with their start and end apart: 6, of which 0 were waited for; matrix products, arithmetic and copies ran while one was open for 6% of the time, Pallas kernels for 0%

commit v1 on v0

v1 whole, which is shorter than its diff:
```python
import functools

import jax
import jax.numpy as jnp
from jax import lax
from jax.experimental import pallas as pl
from jax.experimental.pallas import tpu as pltpu
from jax.sharding import PartitionSpec as P

HOPS = 3
VMEM = pltpu.VMEM
SMEM = pltpu.SMEM


def scale_rows(value, dmat):
    lanes = dmat.shape[1]
    pieces = [value[:, i : i + lanes] * dmat for i in range(0, value.shape[1], lanes)]
    return pieces[0] if len(pieces) == 1 else jnp.concatenate(pieces, axis=1)


def pack(parity, z_ref, blocks_ref, count_ref, hubs_ref, chip_ref, core_ref, hub_ref):
    send_most, tile, _ = chip_ref.shape
    for side, out_ref in ((parity, chip_ref), (1 - parity, core_ref)):
        for slot in range(send_most):
            block = z_ref[blocks_ref[0, side, slot]]
            live = slot < count_ref[0, side]
            out_ref[slot] = jnp.where(live, block, jnp.zeros_like(block))
    group = 16
    rows = []
    for i in range(hub_ref.shape[0]):
        row = hubs_ref[i]
        inside = row % tile
        base = pl.multiple_of(inside // group * group, group)
        near = z_ref[row // tile, pl.ds(base, group), :].astype(jnp.float32)
        at = lax.broadcasted_iota(jnp.int32, near.shape, 0) == inside % group
        rows.append(jnp.sum(jnp.where(at, near, 0.0), axis=0, keepdims=True))
    hub_ref[...] = jnp.concatenate(rows, axis=0).astype(jnp.bfloat16)


def prologue_kernel(
    index_ref, blocks_ref, count_ref, hubs_ref, degree_ref, features_ref, embeddings_ref,
    z_ref, dmat_ref, chip_ref, core_ref, hub_ref,
):
    blocks, tile, _ = z_ref.shape
    split = features_ref.shape[2]
    for b in range(blocks):
        root = lax.rsqrt(degree_ref[b : b + 1, :].astype(jnp.float32))
        dmat = jnp.broadcast_to(root, (tile, tile)).T
        dmat_ref[b] = dmat
        z_ref[b, :, :split] = scale_rows(features_ref[b].astype(jnp.float32), dmat).astype(jnp.bfloat16)
        z_ref[b, :, split:] = scale_rows(embeddings_ref[b].astype(jnp.float32), dmat).astype(jnp.bfloat16)
    pack(index_ref[0] % 2, z_ref, blocks_ref, count_ref, hubs_ref, chip_ref, core_ref, hub_ref)


def hop_kernel(
    index_ref, blocks_ref, count_ref, hubs_ref, columns_ref, tiles_ref, weight_ref, dmat_ref,
    z_ref, from_chip_ref, from_core_ref, gathered_ref, *refs, hop, last, write_at,
):
    refs = list(refs)
    if write_at:
        old_features, old_embeddings = refs[:2]
        refs = refs[2:]
        if write_at > 1:
            refs = refs[2:]
        all_features, all_embeddings = refs[:2]
        refs = refs[2:]
    if last:
        new_features, new_embeddings, extended, hub_sum, sems = refs
    else:
        new_features, new_embeddings, z_next, chip_ref, core_ref, hub_ref, extended, hub_sum, sems = refs
    copies = []
    if write_at:
        copies = [
            pltpu.make_async_copy(old_features, all_features.at[write_at - 1], sems.at[0]),
            pltpu.make_async_copy(old_embeddings, all_embeddings.at[write_at - 1], sems.at[1]),
        ]
        for copy in copies:
            copy.start()
    blocks, tile, width = z_ref.shape
    split = new_features.shape[2]
    per_block = columns_ref.shape[1]
    send_most = from_chip_ref.shape[0]
    parity = index_ref[0] % 2
    for b in range(blocks):
        extended[b] = z_ref[b]
    for slot in range(send_most):
        extended[blocks + parity * send_most + slot] = from_chip_ref[slot]
        extended[blocks + (1 - parity) * send_most + slot] = from_core_ref[slot]
    gathered = gathered_ref[...]
    for b in range(blocks):
        values = jnp.concatenate([tiles_ref[b, k] for k in range(per_block)], axis=1)
        picked = jnp.concatenate([extended[columns_ref[b, k]] for k in range(per_block)], axis=0)
        total = jnp.dot(values, picked, preferred_element_type=jnp.float32)
        total = total + jnp.dot(weight_ref[b], gathered, preferred_element_type=jnp.float32)
        dmat = dmat_ref[b]
        fresh = scale_rows(total, dmat).astype(jnp.bfloat16)
        new_features[b] = fresh[:, :split]
        new_embeddings[b] = fresh[:, split:]
        if last:
            row = 2 + 2 * b
            pair = [
                pltpu.make_async_copy(new_features.at[b], all_features.at[hop, b], sems.at[row]),
                pltpu.make_async_copy(new_embeddings.at[b], all_embeddings.at[hop, b], sems.at[row + 1]),
            ]
            for copy in pair:
                copy.start()
            copies += pair
        else:
            z_next[b] = scale_rows(fresh.astype(jnp.float32), dmat).astype(jnp.bfloat16)
    if not last:
        pack(parity, z_next, blocks_ref, count_ref, hubs_ref, chip_ref, core_ref, hub_ref)
    for copy in copies:
        copy.wait()


def body(
    features, embeddings, tile_values, tile_columns, send_blocks, send_count, hub_rows, hub_weight, degree,
):
    row_count, split = features.shape
    blocks, per_block, tile, _ = tile_values.shape
    extra = embeddings.shape[1]
    width = split + extra
    send_most = send_blocks.shape[2]
    hub_dev = hub_rows.shape[0]
    hub_total = hub_weight.shape[1]
    count = lax.axis_size("dom")
    bf16 = jnp.bfloat16

    index = lax.axis_index("dom").reshape(1)
    vmem = pl.BlockSpec(memory_space=VMEM)
    smem = pl.BlockSpec(memory_space=SMEM)
    hbm = pl.BlockSpec(memory_space=pl.ANY)
    params = pltpu.CompilerParams(vmem_limit_bytes=24 * 2**20)

    sends = [
        jax.ShapeDtypeStruct((send_most, tile, width), bf16),
        jax.ShapeDtypeStruct((send_most, tile, width), bf16),
        jax.ShapeDtypeStruct((hub_dev, width), bf16),
    ]
    z_shape = jax.ShapeDtypeStruct((blocks, tile, width), bf16)
    z, dmat, to_chip, to_core, hub = pl.pallas_call(
        prologue_kernel,
        out_shape=[z_shape, jax.ShapeDtypeStruct((blocks, tile, tile), jnp.float32)] + sends,
        in_specs=[smem] * 4 + [vmem] * 3,
        out_specs=[vmem] * 5,
        compiler_params=params,
        name="prologue",
    )(
        index, send_blocks, send_count, hub_rows,
        degree.reshape(blocks, tile),
        features.reshape(blocks, tile, split),
        embeddings.reshape(blocks, tile, extra),
    )

    core_pairs = [(i, i ^ 1) for i in range(count) if i ^ 1 < count]
    chip_pairs = [p for i in range(1, count - 1, 2) for p in ((i, i + 1), (i + 1, i))]
    weight = hub_weight.reshape(blocks, tile, hub_total)
    old = None
    out = None
    for hop in range(HOPS):
        last = hop == HOPS - 1
        from_chip = lax.ppermute(to_chip, "dom", chip_pairs)
        from_core = lax.ppermute(to_core, "dom", core_pairs)
        spread = jnp.broadcast_to(hub[None], (count, hub_dev, width))
        gathered = lax.all_to_all(spread, "dom", 0, 0).reshape(hub_total, width)
        operands = [index, send_blocks, send_count, hub_rows, tile_columns, tile_values, weight, dmat,
                    z, from_chip, from_core, gathered]
        in_specs = [smem] * 5 + [vmem] * 7
        fresh_shapes = [
            jax.ShapeDtypeStruct((blocks, tile, split), bf16),
            jax.ShapeDtypeStruct((blocks, tile, extra), bf16),
        ]
        whole_shapes = [
            jax.ShapeDtypeStruct((HOPS, blocks, tile, split), bf16),
            jax.ShapeDtypeStruct((HOPS, blocks, tile, extra), bf16),
        ]
        out_shape, out_specs, scratch, aliases = [], [], [], {}
        if hop:
            operands += list(old)
            in_specs += [vmem] * 2
            if hop > 1:
                aliases = {len(operands): 0, len(operands) + 1: 1}
                operands += list(out)
                in_specs += [hbm] * 2
            out_shape += whole_shapes
            out_specs += [hbm] * 2
        if last:
            scratch += [VMEM((blocks, tile, split), bf16), VMEM((blocks, tile, extra), bf16)]
        else:
            out_shape += fresh_shapes + [z_shape] + sends
            out_specs += [vmem] * 6
        scratch += [
            VMEM((blocks + 2 * send_most, tile, width), bf16),
            VMEM((8, 128), jnp.float32),
            pltpu.SemaphoreType.DMA((2 + 2 * blocks,)),
        ]
        got = pl.pallas_call(
            functools.partial(hop_kernel, hop=hop, last=last, write_at=hop),
            out_shape=out_shape,
            in_specs=in_specs,
            out_specs=out_specs,
            scratch_shapes=scratch,
            input_output_aliases=aliases,
            compiler_params=params,
            name=f"hop{hop}",
        )(*operands)
        if hop:
            out = got[:2]
            got = got[2:]
        if not last:
            old = got[:2]
            z, to_chip, to_core, hub = got[2:]
    return out[0].reshape(HOPS, row_count, split), out[1].reshape(HOPS, row_count, extra)


def solution(mesh):
    placed = (
        P("dom", None),
        P("dom", None),
        P("dom", None, None, None),
        P("dom", None),
        P("dom", None, None),
        P("dom", None),
        P("dom"),
        P("dom", None),
        P("dom"),
    )
    return jax.shard_map(
        body,
        mesh=mesh,
        in_specs=placed,
        out_specs=(P(None, "dom", None), P(None, "dom", None)),
        check_vma=False,
    )
```

time: 220 us -> 86.3 us (0.39)
  blocking collectives: 119 us -> 21.6 us
  matrix products: 24.9 us -> 0 us
  local copies, waits for them, and re-layouts: 47.2 us -> 29.1 us
  Pallas kernels: 0 us -> 12.9 us
  other arithmetic: 11.9 us -> 0 us
  waiting for transfers between devices: 0.02 us -> 5.83 us
    all_gather x3 -> x0, blocking collectives: 119 us -> none  [body(): gathered_hubs = lax.all_gather(hub_local, 'dom', axis=0, tiled=True)]
    dot_general x6 -> x0, matrix products: 24.9 us -> none  [the longest x3 14.9 us: body(): jnp.einsum('bkij,bkjw->biw', tile_values, picked, preferred_element_type=...]
    all_to_all x0 -> x2, blocking collectives: none -> 21.6 us  [body(): gathered = lax.all_to_all(spread, 'dom', 0, 0).reshape(hub_total, width)]
    gather x9 -> x0, local copies, waits for them, and re-layouts: 18 us -> none  [the longest x3 10.5 us: body(): picked = extended[tile_columns]]
    unnamed x51 -> x66, local copies, waits for them, and re-layouts: 10.4 us -> 26.5 us
    pallas_call x0 -> x4, Pallas kernels: none -> 12.9 us  [the longest x3 11.2 us: body(): pl.pallas_call(functools.partial(hop_kernel, hop=hop, last=last, write_at...]
    reshape x5 -> x3, local copies, waits for them, and re-layouts: 13.2 us -> 1.88 us  [body(): gathered = lax.all_to_all(spread, 'dom', 0, 0).reshape(hub_total, width)]
    all_to_all x0 -> x1, waiting for transfers between devices: none -> 5.81 us  [body(): gathered = lax.all_to_all(spread, 'dom', 0, 0).reshape(hub_total, width)]
  transfers between devices with their start and end apart: 6 -> 7, of which waited for: 0 -> 1; matrix products, arithmetic and copies ran while one was open for 6% -> 5% of each run, Pallas kernels for 0% -> 0%
where the time goes in v1:
time: 86.3 us; the launch traced here: 85.3 us
  local copies, waits for them, and re-layouts  29.1 us (34%)
  blocking collectives  21.6 us (25%)
  starting transfers between devices  15 us (17%)
  Pallas kernels  12.9 us (15%)
  waiting for transfers between devices  5.83 us (7%)
    unnamed x66, local copies, waits for them, and re-layouts  26.5 us
    all_to_all x2, blocking collectives, body(): gathered = lax.all_to_all(spread, 'dom', 0, 0).reshape(hub_total, width)  21.6 us
    pallas_call x3, Pallas kernels, body(): pl.pallas_call(functools.partial(hop_kernel, hop=hop, last=last, write_at...  11.2 us
    ppermute x3, starting transfers between devices, body(): from_core = lax.ppermute(to_core, 'dom', core_pairs)  7.98 us
    all_to_all x1, waiting for transfers between devices, body(): gathered = lax.all_to_all(spread, 'dom', 0, 0).reshape(hub_total, width)  5.81 us
    all_to_all x1, starting transfers between devices, body(): gathered = lax.all_to_all(spread, 'dom', 0, 0).reshape(hub_total, width)  5.04 us
    ppermute x3, starting transfers between devices, body(): from_chip = lax.ppermute(to_chip, 'dom', chip_pairs)  2.01 us
    reshape x3, local copies, waits for them, and re-layouts, body(): gathered = lax.all_to_all(spread, 'dom', 0, 0).reshape(hub_total, width)  1.88 us
  transfers between devices with their start and end apart: 7, of which 1 were waited for; matrix products, arithmetic and copies ran while one was open for 5% of the time, Pallas kernels for 0%

profile of v1, /device:TPU:0, one launch (start us, length us, event | category | flops | bytes accessed | tf_op | source)
XLA Modules:
  0.0 85.3 jit_solution(17403912932430216300)
XLA Ops:
  0.7 1.3 %copy-done.5 = bf16[1024,512]{1,0:T(8,128)(2,1)S(1)} copy-done((bf16[1024,512]{1,0:T(8,128)(2,1)S(1)}, bf16[1024,512]{1,0:T(8,128)(2,1)}, u32[]{:S(2)}) %copy-start.5) | copy-done | bytes 1048600
  2.0 0.9 %copy-done.10 = bf16[1024,128]{1,0:T(8,128)(2,1)S(1)} copy-done((bf16[1024,128]{1,0:T(8,128)(2,1)S(1)}, bf16[1024,128]{1,0:T(8,128)(2,1)}, u32[]{:S(2)}) %copy-start.10) | copy-done | bytes 262168
  2.9 0.7 copy-done.18
  3.6 0.7 copy-done.22
  4.2 0.7 copy-done.26
  4.9 0.7 copy-done.30
  5.6 1.7 %prologue.1 = (bf16[8,128,640]{2,1,0:T(8,128)(2,1)S(1)}, f32[8,128,128]{2,1,0:T(8,128)S(1)}, bf16[2,128,640]{2,1,0:T(8,128)(2,1)}, bf16[2,128,640]{2,1,0:T(8,128)(2,1)}, bf16[2,640]{1,0:T(2,128)(2,1)S(1)}) custom-call(s32[1]{0:T(128)} %bitcast.index_ref, s32[1,2,2]{2,1,0:T(2,128)S(1)} %copy-done.18, s32[1,2]{1,0:T(1,128)S(1)} %copy-done.22, ...), custom_call_target="tpu_custom_call" | custom-call | tf_op jit(solution)/shard_map/prologue/pallas_call | solution.py:141
  7.3 0.7 collective-permute-start
  8.0 4.4 %collective-permute-start.1 = (bf16[2,128,640]{2,1,0:T(8,128)(2,1)}, bf16[2,128,640]{2,1,0:T(8,128)(2,1)}, u32[]{:S(2)}, u32[]{:S(2)}) collective-permute-start(bf16[2,128,640]{2,1,0:T(8,128)(2,1)} %get-tuple-element.26), channel_id=1, source_target_pairs={{0,1},{1,0},{2,3},{3,2},{4,5},{5,4},{6,7},{7,6},{8,9},{9,8},{10,11... | collective-permute-start | bytes 983048 | tf_op jit(solution)/shard_map/ppermute | solution.py:163
  12.4 0.7 broadcast_in_dim.6
  13.0 5.0 %all-to-all-start = ((bf16[32,2,640]{2,1,0:T(2,128)(2,1)}), bf16[32,2,640]{2,1,0:T(2,128)(2,1)}, u32[]{:S(2)}, u32[]{:S(2)}) async-start(bf16[32,2,640]{2,1,0:T(2,128)(2,1)} %broadcast_in_dim.6), calls=%async_computation | async-start | bytes 163840 | tf_op jit(solution)/shard_map/all_to_all | solution.py:165
  18.1 0.7 copy.16.columns_ref
  18.8 1.1 %copy.13 = bf16[1024,64]{1,0:T(8,128)(2,1)S(1)} copy(bf16[1024,64]{0,1:T(8,128)(2,1)} %param.16) | data formatting | bytes 262144 | tf_op args[7]
  19.8 5.8 %all-to-all-done = bf16[32,2,640]{2,1,0:T(2,128)(2,1)} async-done(((bf16[32,2,640]{2,1,0:T(2,128)(2,1)}), bf16[32,2,640]{2,1,0:T(2,128)(2,1)}, u32[]{:S(2)}, u32[]{:S(2)}) %all-to-all-start) | async-done | bytes 81952 | tf_op jit(solution)/shard_map/all_to_all | solution.py:165
  25.6 0.9 %reshape.42.gathered_ref = bf16[64,640]{1,0:T(8,128)(2,1)S(1)} reshape(bf16[32,2,640]{2,1,0:T(2,128)(2,1)} %all-to-all-done) | data formatting | bytes 163840 | tf_op jit(solution)/shard_map/reshape | solution.py:165
  26.6 0.7 copy-done.15
  27.3 0.7 copy-done.19
  28.0 0.7 copy-done.23
  28.6 0.7 copy-done.27
  29.3 3.6 %hop0.1 = (bf16[8,128,512]{2,1,0:T(8,128)(2,1)S(1)}, bf16[8,128,128]{2,1,0:T(8,128)(2,1)S(1)}, bf16[8,128,640]{2,1,0:T(8,128)(2,1)S(1)}, bf16[2,128,640]{2,1,0:T...) custom-call(s32[1]{0:T(128)} %bitcast.index_ref, s32[1,2,2]{2,1,0:T(2,128)S(1)} %copy-done.19, ...), custom_call_target="tpu_custom_call" | custom-call | tf_op jit(solution)/shard_map/hop0/pallas_call | solution.py:197
  32.9 1.0 %copy-done.1 = bf16[8,128,640]{2,1,0:T(8,128)(2,1)} copy-done((bf16[8,128,640]{2,1,0:T(8,128)(2,1)}, bf16[8,128,640]{2,1,0:T(8,128)(2,1)S(1)}, u32[]{:S(2)}) %copy-start.1) | copy-done | bytes 1310744
  33.9 1.0 %copy-done.6 = bf16[8,128,512]{2,1,0:T(8,128)(2,1)} copy-done((bf16[8,128,512]{2,1,0:T(8,128)(2,1)}, bf16[8,128,512]{2,1,0:T(8,128)(2,1)S(1)}, u32[]{:S(2)}) %copy-start.6) | copy-done | bytes 1048600
  34.9 0.7 copy-done.13
  35.6 0.7 collective-permute-start.2
  36.3 1.8 %collective-permute-start.3 = (bf16[2,128,640]{2,1,0:T(8,128)(2,1)}, bf16[2,128,640]{2,1,0:T(8,128)(2,1)S(1)}, u32[]{:S(2)}, u32[]{:S(2)}) collective-permute-start(bf16[2,128,640]{2,1,0:T(8,128)(2,1)} %get-tuple-element.30), channel_id=1, source_target_pairs={{0,1},{1,0},{2,3},{3,2},{4,5},{5,4},{6,7},{7,6},{8,9},{9,8},{10,11... | collective-permute-start | bytes 983048 | tf_op jit(solution)/shard_map/ppermute | solution.py:163
  38.2 10.7 %all_to_all.15 = bf16[32,2,640]{2,1,0:T(2,128)(2,1)S(1)} all-to-all(bf16[32,2,640]{2,1,0:T(2,128)(2,1)S(1)} %broadcast_in_dim.7), channel_id=1, replica_groups=mesh['dom'=32] {'dom'}, dimensions={0} | all-to-all | bytes 163840 | tf_op jit(solution)/shard_map/all_to_all | solution.py:165
  49.0 0.7 copy-done.8
  49.7 1.3 %copy-done.2 = bf16[8,128,640]{2,1,0:T(8,128)(2,1)S(1)} copy-done((bf16[8,128,640]{2,1,0:T(8,128)(2,1)S(1)}, bf16[8,128,640]{2,1,0:T(8,128)(2,1)}, u32[]{:S(2)}) %copy-start.2) | copy-done | bytes 1310744
  51.0 1.2 %copy-done.7 = bf16[8,128,512]{2,1,0:T(8,128)(2,1)S(1)} copy-done((bf16[8,128,512]{2,1,0:T(8,128)(2,1)S(1)}, bf16[8,128,512]{2,1,0:T(8,128)(2,1)}, u32[]{:S(2)}) %copy-start.7) | copy-done | bytes 1048600
  52.2 1.0 %copy-done.9 = bf16[2,128,640]{2,1,0:T(8,128)(2,1)S(1)} copy-done((bf16[2,128,640]{2,1,0:T(8,128)(2,1)S(1)}, bf16[2,128,640]{2,1,0:T(8,128)(2,1)}, u32[]{:S(2)}) %copy-start.9) | copy-done | bytes 327704
  53.2 0.9 %copy-done.14 = bf16[8,128,128]{2,1,0:T(8,128)(2,1)S(1)} copy-done((bf16[8,128,128]{2,1,0:T(8,128)(2,1)S(1)}, bf16[8,128,128]{2,1,0:T(8,128)(2,1)}, u32[]{:S(2)}) %copy-start.14) | copy-done | bytes 262168
  54.2 0.7 copy-done.16
  54.8 0.7 copy-done.20
  55.5 0.7 copy-done.24
  56.2 0.7 copy-done.28
  56.8 4.3 %hop1.1 = (bf16[3,8,128,512]{3,2,1,0:T(8,128)(2,1)}, bf16[3,8,128,128]{3,2,1,0:T(8,128)(2,1)}, bf16[8,128,512]{2,1,0:T(8,128)(2,1)S(1)}, bf16[8,128,128]{2,1,0:T...) custom-call(s32[1]{0:T(128)} %bitcast.index_ref, ...), custom_call_target="tpu_custom_call" | custom-call | tf_op jit(solution)/shard_map/hop1/pallas_call | solution.py:197
  61.2 1.0 %copy-done.3 = bf16[8,128,512]{2,1,0:T(8,128)(2,1)} copy-done((bf16[8,128,512]{2,1,0:T(8,128)(2,1)}, bf16[8,128,512]{2,1,0:T(8,128)(2,1)S(1)}, u32[]{:S(2)}) %copy-start.3) | copy-done | bytes 1048600
  62.1 0.7 copy-done.11
  62.8 0.7 collective-permute-start.4
  63.5 1.8 %collective-permute-start.5 = (bf16[2,128,640]{2,1,0:T(8,128)(2,1)}, bf16[2,128,640]{2,1,0:T(8,128)(2,1)}, u32[]{:S(2)}, u32[]{:S(2)}) collective-permute-start(bf16[2,128,640]{2,1,0:T(8,128)(2,1)} %get-tuple-element.36), channel_id=1, source_target_pairs={{0,1},{1,0},{2,3},{3,2},{4,5},{5,4},{6,7},{7,6},{8,9},{9,8},{10,11... | collective-permute-start | bytes 983048 | tf_op jit(solution)/shard_map/ppermute | solution.py:163
  65.4 10.9 %all_to_all.16 = bf16[32,2,640]{2,1,0:T(2,128)(2,1)} all-to-all(bf16[32,2,640]{2,1,0:T(2,128)(2,1)S(1)} %broadcast_in_dim.8), channel_id=1, replica_groups=mesh['dom'=32] {'dom'}, dimensions={0} | all-to-all | bytes 163840 | tf_op jit(solution)/shard_map/all_to_all | solution.py:165
  76.2 0.9 %reshape.44.gathered_ref = bf16[64,640]{1,0:T(8,128)(2,1)S(1)} reshape(bf16[32,2,640]{2,1,0:T(2,128)(2,1)} %all_to_all.16) | data formatting | bytes 163840 | tf_op jit(solution)/shard_map/reshape | solution.py:165
  77.2 1.2 %copy-done.4 = bf16[8,128,512]{2,1,0:T(8,128)(2,1)S(1)} copy-done((bf16[8,128,512]{2,1,0:T(8,128)(2,1)S(1)}, bf16[8,128,512]{2,1,0:T(8,128)(2,1)}, u32[]{:S(2)}) %copy-start.4) | copy-done | bytes 1048600
  78.4 0.9 %copy-done.12 = bf16[8,128,128]{2,1,0:T(8,128)(2,1)S(1)} copy-done((bf16[8,128,128]{2,1,0:T(8,128)(2,1)S(1)}, bf16[8,128,128]{2,1,0:T(8,128)(2,1)}, u32[]{:S(2)}) %copy-start.12) | copy-done | bytes 262168
  79.4 0.7 copy-done.17
  80.0 0.7 copy-done.21
  81.4 0.7 copy-done.29
  82.0 3.3 %hop2.1 = (bf16[3,8,128,512]{3,2,1,0:T(8,128)(2,1)}, bf16[3,8,128,128]{3,2,1,0:T(8,128)(2,1)}) custom-call(s32[1]{0:T(128)} %bitcast.index_ref, s32[1,2,2]{2,1,0:T(2,128)S(1)} %copy-done.21, s32[1,2]{1,0:T(1,128)S(1)} %copy-done.25, s32[2]{0:T(128)S(1)} %copy-done.29, s32[8,4]{1,0:T(8,128)S(1)} %copy-done.17, ...), custom_call_target="tpu_custom_call", output_to_operand_aliasing={{0}: (14, {}), {1}: (15, {})} | custom-call | tf_op jit(solution)/shard_map/hop2/pallas_call | solution.py:197
  (44 shorter events, 0.9 us)
Async XLA Ops:
  0.6 26.0 %copy-start = (bf16[8,4,128,128]{3,2,1,0:T(8,128)(2,1)S(1)}, bf16[8,4,128,128]{3,2,1,0:T(8,128)(2,1)}, u32[]{:S(2)}) copy-start(bf16[8,4,128,128]{3,2,1,0:T(8,128)(2,1)} %tiles_ref.5) | copy-start | bytes 3145732
  0.6 1.3 %copy-start.5 = (bf16[1024,512]{1,0:T(8,128)(2,1)S(1)}, bf16[1024,512]{1,0:T(8,128)(2,1)}, u32[]{:S(2)}) copy-start(bf16[1024,512]{1,0:T(8,128)(2,1)} %param.9) | copy-start | bytes 3145732
  2.0 0.9 %copy-start.10 = (bf16[1024,128]{1,0:T(8,128)(2,1)S(1)}, bf16[1024,128]{1,0:T(8,128)(2,1)}, u32[]{:S(2)}) copy-start(bf16[1024,128]{1,0:T(8,128)(2,1)} %param.10) | copy-start | bytes 786436
  2.9 0.7 copy-start.18
  3.6 0.7 copy-start.22
  4.2 0.7 copy-start.26
  4.9 0.7 copy-start.30
  5.6 12.5 %copy-start.31 = (s32[8,4]{0,1:T(4,128)S(1)}, s32[8,4]{0,1:T(4,128)}, u32[]{:S(2)}) copy-start(s32[8,4]{0,1:T(4,128)} %param.12) | copy-start | bytes 388
  7.3 19.3 %collective-permute-start = (bf16[2,128,640]{2,1,0:T(8,128)(2,1)}, bf16[2,128,640]{2,1,0:T(8,128)(2,1)S(1)}, u32[]{:S(2)}, u32[]{:S(2)}) collective-permute-start(bf16[2,128,640]{2,1,0:T(8,128)(2,1)} %get-tuple-element.25), channel_id=1, source_target_pairs={{1,2},{2,1},{3,4},{4,3},{5,6},{6,5},{7,8},{8,7},{9,10},{10,9},{11,... | collective-permute-start | bytes 983048 | tf_op jit(solution)/shard_map/ppermute | solution.py:162
  8.0 18.6 %collective-permute-start.1 = (bf16[2,128,640]{2,1,0:T(8,128)(2,1)}, bf16[2,128,640]{2,1,0:T(8,128)(2,1)}, u32[]{:S(2)}, u32[]{:S(2)}) collective-permute-start(bf16[2,128,640]{2,1,0:T(8,128)(2,1)} %get-tuple-element.26), channel_id=1, source_target_pairs={{0,1},{1,0},{2,3},{3,2},{4,5},{5,4},{6,7},{7,6},{8,9},{9,8},{10,11... | collective-permute-start | bytes 983048 | tf_op jit(solution)/shard_map/ppermute | solution.py:163
  13.0 12.6 %all-to-all-start = ((bf16[32,2,640]{2,1,0:T(2,128)(2,1)}), bf16[32,2,640]{2,1,0:T(2,128)(2,1)}, u32[]{:S(2)}, u32[]{:S(2)}) async-start(bf16[32,2,640]{2,1,0:T(2,128)(2,1)} %broadcast_in_dim.6), calls=%async_computation | async-start | bytes 163840 | tf_op jit(solution)/shard_map/all_to_all | solution.py:165
  26.6 0.7 copy-start.15
  27.3 0.7 copy-start.19
  28.0 0.7 copy-start.23
  28.6 0.7 copy-start.27
  32.9 1.1 %copy-start.1 = (bf16[8,128,640]{2,1,0:T(8,128)(2,1)}, bf16[8,128,640]{2,1,0:T(8,128)(2,1)S(1)}, u32[]{:S(2)}) copy-start(bf16[8,128,640]{2,1,0:T(8,128)(2,1)S(1)} %get-tuple-element.28.z_ref) | copy-start | bytes 3932164
  33.9 1.0 %copy-start.6 = (bf16[8,128,512]{2,1,0:T(8,128)(2,1)}, bf16[8,128,512]{2,1,0:T(8,128)(2,1)S(1)}, u32[]{:S(2)}) copy-start(bf16[8,128,512]{2,1,0:T(8,128)(2,1)S(1)} %get-tuple-element.32.refs_0_) | copy-start | bytes 3145732
  34.9 0.7 copy-start.13
  35.6 13.3 %collective-permute-start.2 = (bf16[2,128,640]{2,1,0:T(8,128)(2,1)}, bf16[2,128,640]{2,1,0:T(8,128)(2,1)S(1)}, u32[]{:S(2)}, u32[]{:S(2)}) collective-permute-start(bf16[2,128,640]{2,1,0:T(8,128)(2,1)} %get-tuple-element.29), channel_id=1, source_target_pairs={{1,2},{2,1},{3,4},{4,3},{5,6},{6,5},{7,8},{8,7},{9,10},{10,9},{11,... | collective-permute-start | bytes 983048 | tf_op jit(solution)/shard_map/ppermute | solution.py:162
  36.3 12.6 %collective-permute-start.3 = (bf16[2,128,640]{2,1,0:T(8,128)(2,1)}, bf16[2,128,640]{2,1,0:T(8,128)(2,1)S(1)}, u32[]{:S(2)}, u32[]{:S(2)}) collective-permute-start(bf16[2,128,640]{2,1,0:T(8,128)(2,1)} %get-tuple-element.30), channel_id=1, source_target_pairs={{0,1},{1,0},{2,3},{3,2},{4,5},{5,4},{6,7},{7,6},{8,9},{9,8},{10,11... | collective-permute-start | bytes 983048 | tf_op jit(solution)/shard_map/ppermute | solution.py:163
  49.0 0.7 copy-start.8
  49.7 1.3 %copy-start.2 = (bf16[8,128,640]{2,1,0:T(8,128)(2,1)S(1)}, bf16[8,128,640]{2,1,0:T(8,128)(2,1)}, u32[]{:S(2)}) copy-start(bf16[8,128,640]{2,1,0:T(8,128)(2,1)} %copy-done.1) | copy-start | bytes 3932164
  51.0 1.2 %copy-start.7 = (bf16[8,128,512]{2,1,0:T(8,128)(2,1)S(1)}, bf16[8,128,512]{2,1,0:T(8,128)(2,1)}, u32[]{:S(2)}) copy-start(bf16[8,128,512]{2,1,0:T(8,128)(2,1)} %copy-done.6) | copy-start | bytes 3145732
  52.2 1.0 %copy-start.9 = (bf16[2,128,640]{2,1,0:T(8,128)(2,1)S(1)}, bf16[2,128,640]{2,1,0:T(8,128)(2,1)}, u32[]{:S(2)}) copy-start(bf16[2,128,640]{2,1,0:T(8,128)(2,1)} %copy-done.8) | copy-start | bytes 983044
  53.2 0.9 %copy-start.14 = (bf16[8,128,128]{2,1,0:T(8,128)(2,1)S(1)}, bf16[8,128,128]{2,1,0:T(8,128)(2,1)}, u32[]{:S(2)}) copy-start(bf16[8,128,128]{2,1,0:T(8,128)(2,1)} %copy-done.13) | copy-start | bytes 786436
  54.2 0.7 copy-start.16
  54.8 0.7 copy-start.20
  55.5 0.7 copy-start.24
  56.2 0.7 copy-start.28
  61.1 1.0 %copy-start.3 = (bf16[8,128,512]{2,1,0:T(8,128)(2,1)}, bf16[8,128,512]{2,1,0:T(8,128)(2,1)S(1)}, u32[]{:S(2)}) copy-start(bf16[8,128,512]{2,1,0:T(8,128)(2,1)S(1)} %get-tuple-element.38.refs_0_) | copy-start | bytes 3145732
  62.1 0.7 copy-start.11
  62.8 14.3 %collective-permute-start.4 = (bf16[2,128,640]{2,1,0:T(8,128)(2,1)}, bf16[2,128,640]{2,1,0:T(8,128)(2,1)S(1)}, u32[]{:S(2)}, u32[]{:S(2)}) collective-permute-start(bf16[2,128,640]{2,1,0:T(8,128)(2,1)} %get-tuple-element.35), channel_id=1, source_target_pairs={{1,2},{2,1},{3,4},{4,3},{5,6},{6,5},{7,8},{8,7},{9,10},{10,9},{11,... | collective-permute-start | bytes 983048 | tf_op jit(solution)/shard_map/ppermute | solution.py:162
  63.5 13.6 %collective-permute-start.5 = (bf16[2,128,640]{2,1,0:T(8,128)(2,1)}, bf16[2,128,640]{2,1,0:T(8,128)(2,1)}, u32[]{:S(2)}, u32[]{:S(2)}) collective-permute-start(bf16[2,128,640]{2,1,0:T(8,128)(2,1)} %get-tuple-element.36), channel_id=1, source_target_pairs={{0,1},{1,0},{2,3},{3,2},{4,5},{5,4},{6,7},{7,6},{8,9},{9,8},{10,11... | collective-permute-start | bytes 983048 | tf_op jit(solution)/shard_map/ppermute | solution.py:163
  77.2 1.2 %copy-start.4 = (bf16[8,128,512]{2,1,0:T(8,128)(2,1)S(1)}, bf16[8,128,512]{2,1,0:T(8,128)(2,1)}, u32[]{:S(2)}) copy-start(bf16[8,128,512]{2,1,0:T(8,128)(2,1)} %copy-done.3) | copy-start | bytes 3145732
  78.4 0.9 %copy-start.12 = (bf16[8,128,128]{2,1,0:T(8,128)(2,1)S(1)}, bf16[8,128,128]{2,1,0:T(8,128)(2,1)}, u32[]{:S(2)}) copy-start(bf16[8,128,128]{2,1,0:T(8,128)(2,1)} %copy-done.11) | copy-start | bytes 786436
  79.3 0.7 copy-start.17
  80.0 0.7 copy-start.21
  80.7 0.7 copy-start.25
  81.4 0.7 copy-start.29

commit v2 on v1

v2 whole, which is shorter than its diff:
```python
import functools

import jax
import jax.numpy as jnp
from jax import lax
from jax.experimental import pallas as pl
from jax.experimental.pallas import tpu as pltpu
from jax.sharding import PartitionSpec as P

HOPS = 3
VMEM = pltpu.VMEM
SMEM = pltpu.SMEM
BF16 = jnp.bfloat16
F32 = jnp.float32


def scale_rows(value, dmat):
    lanes = dmat.shape[1]
    pieces = [value[:, i : i + lanes] * dmat for i in range(0, value.shape[1], lanes)]
    return pieces[0] if len(pieces) == 1 else jnp.concatenate(pieces, axis=1)


def begin(copies):
    for copy in copies:
        copy.start()
    return copies


def finish(copies):
    for copy in copies:
        copy.wait()


def fetch(sources, targets, sems, first):
    return begin(
        [
            pltpu.make_async_copy(source, target, sems.at[first + i])
            for i, (source, target) in enumerate(zip(sources, targets))
        ]
    )


def pack(parity, z_ref, blocks_ref, count_ref, hubs_ref, chip_ref, core_ref, hub_ref):
    send_most, tile, _ = chip_ref.shape
    for side, out_ref in ((parity, chip_ref), (1 - parity, core_ref)):
        for slot in range(send_most):
            block = z_ref[blocks_ref[0, side, slot]]
            live = slot < count_ref[0, side]
            out_ref[slot] = jnp.where(live, block, jnp.zeros_like(block))
    group = 16
    rows = []
    for i in range(hub_ref.shape[0]):
        row = hubs_ref[i]
        inside = row % tile
        base = pl.multiple_of(inside // group * group, group)
        near = z_ref[row // tile, pl.ds(base, group), :].astype(F32)
        at = lax.broadcasted_iota(jnp.int32, near.shape, 0) == inside % group
        rows.append(jnp.sum(jnp.where(at, near, 0.0), axis=0, keepdims=True))
    hub_ref[...] = jnp.concatenate(rows, axis=0).astype(BF16)


def prologue_kernel(
    blocks_hbm, count_hbm, hubs_hbm, degree_hbm, features_hbm, embeddings_hbm,
    z_hbm, dmat_ref, chip_ref, core_ref, hub_ref,
    blocks_ref, count_ref, hubs_ref, degree_ref, features_ref, embeddings_ref, z_ref, sems,
):
    blocks, tile, _ = z_ref.shape
    split = features_ref.shape[2]
    writes = []
    degree_copy = fetch([degree_hbm], [degree_ref], sems, 0)
    row_copies = []
    for b in range(blocks):
        row_copies.append(
            fetch([features_hbm.at[b], embeddings_hbm.at[b]], [features_ref.at[b], embeddings_ref.at[b]],
                  sems, 4 + 2 * b)
        )
    tables = fetch([blocks_hbm, count_hbm, hubs_hbm], [blocks_ref, count_ref, hubs_ref], sems, 1)
    finish(degree_copy)
    for b in range(blocks):
        root = lax.rsqrt(degree_ref[b : b + 1, :].astype(F32))
        dmat = jnp.broadcast_to(root, (tile, tile)).T
        dmat_ref[b] = dmat
        finish(row_copies[b])
        z_ref[b, :, :split] = scale_rows(features_ref[b].astype(F32), dmat).astype(BF16)
        z_ref[b, :, split:] = scale_rows(embeddings_ref[b].astype(F32), dmat).astype(BF16)
        writes += fetch([z_ref.at[b]], [z_hbm.at[b]], sems, 4 + 2 * blocks + b)
    finish(tables)
    pack(lax.axis_index("dom") % 2, z_ref, blocks_ref, count_ref, hubs_ref, chip_ref, core_ref, hub_ref)
    finish(writes)


def own_kernel(columns_hbm, tiles_hbm, z_hbm, *refs, first):
    if first:
        weight_hbm, own_hbm, mixed_ref, columns_ref, tiles_ref, z_ref, weight_ref, own_ref, sems = refs
    else:
        own_hbm, columns_ref, tiles_ref, z_ref, own_ref, sems = refs
    blocks, tile, _ = z_ref.shape
    per_block = columns_ref.shape[0]
    table = fetch([columns_hbm], [columns_ref], sems, 0)
    rows = fetch([z_hbm], [z_ref], sems, 1)
    reads = [fetch([tiles_hbm.at[b]], [tiles_ref.at[b]], sems, 3 + b) for b in range(blocks)]
    if first:
        finish(fetch([weight_hbm], [weight_ref], sems, 2))
    finish(table)
    finish(rows)
    writes = []
    for b in range(blocks):
        finish(reads[b])
        columns = [columns_ref[k, b] for k in range(per_block)]
        tiles = [tiles_ref[b, k] for k in range(per_block)]
        values = jnp.concatenate(
            [jnp.where(c < blocks, t, jnp.zeros_like(t)) for c, t in zip(columns, tiles)], axis=1
        )
        picked = jnp.concatenate([z_ref[jnp.minimum(c, blocks - 1)] for c in columns], axis=0)
        own_ref[b] = jnp.dot(values, picked, preferred_element_type=F32)
        writes += fetch([own_ref.at[b]], [own_hbm.at[b]], sems, 3 + blocks + b)
        if first:
            rim = (mixed_ref.shape[2] - weight_ref.shape[0]) // tile
            for slot in range(rim):
                total = jnp.zeros((tile, tile), F32)
                for c, t in zip(columns, tiles):
                    total += jnp.where(c == blocks + slot, t, jnp.zeros_like(t)).astype(F32)
                mixed_ref[b, :, slot * tile : (slot + 1) * tile] = total.astype(BF16)
            mixed_ref[b, :, rim * tile :] = weight_ref[:, b * tile : (b + 1) * tile].astype(F32).T.astype(BF16)
    finish(writes)


def merge_kernel(
    blocks_hbm, count_hbm, hubs_hbm, own_hbm, mixed_ref, dmat_ref, from_chip_ref, from_core_ref, gathered_ref,
    *refs, hop, last,
):
    refs = list(refs)
    if hop:
        del refs[:2]
    all_features, all_embeddings = refs[:2]
    if last:
        new_features, new_embeddings, own_ref, received, sems = refs[2:]
    else:
        (z_hbm, chip_ref, core_ref, hub_ref, blocks_ref, count_ref, hubs_ref, z_next,
         new_features, new_embeddings, own_ref, received, sems) = refs[2:]
    blocks, tile, width = own_ref.shape
    reads = [fetch([own_hbm.at[b]], [own_ref.at[b]], sems, 3 + b) for b in range(blocks)]
    if not last:
        tables = fetch([blocks_hbm, count_hbm, hubs_hbm], [blocks_ref, count_ref, hubs_ref], sems, 0)
    split = new_features.shape[2]
    send_most = from_chip_ref.shape[0]
    rim_rows = send_most * tile
    parity = lax.axis_index("dom") % 2
    for slot in range(send_most):
        chip_at = pl.multiple_of(parity * rim_rows + slot * tile, tile)
        core_at = pl.multiple_of((1 - parity) * rim_rows + slot * tile, tile)
        received[pl.ds(chip_at, tile), :] = from_chip_ref[slot]
        received[pl.ds(core_at, tile), :] = from_core_ref[slot]
    received[2 * rim_rows :, :] = gathered_ref[...]
    writes = []
    for b in range(blocks):
        total = jnp.dot(mixed_ref[b], received[...], preferred_element_type=F32)
        finish(reads[b])
        total = own_ref[b] + total
        dmat = dmat_ref[b]
        fresh = scale_rows(total, dmat).astype(BF16)
        new_features[b] = fresh[:, :split]
        new_embeddings[b] = fresh[:, split:]
        sources = [new_features.at[b], new_embeddings.at[b]]
        targets = [all_features.at[hop, b], all_embeddings.at[hop, b]]
        if not last:
            z_next[b] = scale_rows(fresh.astype(F32), dmat).astype(BF16)
            sources.append(z_next.at[b])
            targets.append(z_hbm.at[b])
        writes += fetch(sources, targets, sems, 3 + blocks + 3 * b)
    if not last:
        finish(tables)
        pack(parity, z_next, blocks_ref, count_ref, hubs_ref, chip_ref, core_ref, hub_ref)
    finish(writes)


def body(
    features, embeddings, tile_values, tile_columns, send_blocks, send_count, hub_rows, hub_weight, degree,
):
    row_count, split = features.shape
    blocks, per_block, tile, _ = tile_values.shape
    extra = embeddings.shape[1]
    width = split + extra
    send_most = send_blocks.shape[2]
    hub_dev = hub_rows.shape[0]
    hub_total = hub_weight.shape[1]
    count = lax.axis_size("dom")
    rim_rows = 2 * send_most * tile

    vmem = pl.BlockSpec(memory_space=VMEM)
    hbm = pl.BlockSpec(memory_space=pltpu.HBM)
    shape = jax.ShapeDtypeStruct

    def pin(*values):
        return [pltpu.with_memory_space_constraint(value, pltpu.HBM) for value in values]

    def call(kernel, name, flops, **kwargs):
        return pl.pallas_call(
            kernel,
            name=name,
            compiler_params=pltpu.CompilerParams(vmem_limit_bytes=24 * 2**20),
            cost_estimate=pl.CostEstimate(flops=flops, bytes_accessed=0, transcendentals=0),
            **kwargs,
        )

    int32 = jnp.int32
    tables = [SMEM(send_blocks.shape, int32), SMEM(send_count.shape, int32), SMEM(hub_rows.shape, int32)]
    sends = [
        shape((send_most, tile, width), BF16), shape((send_most, tile, width), BF16), shape((hub_dev, width), BF16),
    ]
    whole = [pltpu.HBM((HOPS, blocks, tile, split), BF16), pltpu.HBM((HOPS, blocks, tile, extra), BF16)]
    z_like = (blocks, tile, width)
    lists = pin(send_blocks, send_count, hub_rows)
    z, dmat, to_chip, to_core, hub = call(
        prologue_kernel, "prologue", 10**8,
        out_shape=[pltpu.HBM(z_like, BF16), shape((blocks, tile, tile), F32)] + sends,
        in_specs=[hbm] * 6,
        out_specs=[hbm] + [vmem] * 4,
        scratch_shapes=tables + [
            VMEM((blocks, tile), int32), VMEM((blocks, tile, split), BF16), VMEM((blocks, tile, extra), BF16),
            VMEM(z_like, BF16), pltpu.SemaphoreType.DMA((4 + 3 * blocks,)),
        ],
    )(
        *lists,
        *pin(degree.reshape(blocks, tile), features.reshape(blocks, tile, split),
             embeddings.reshape(blocks, tile, extra)),
    )

    core_pairs = [(i, i ^ 1) for i in range(count) if i ^ 1 < count]
    chip_pairs = [p for i in range(1, count - 1, 2) for p in ((i, i + 1), (i + 1, i))]
    fixed = pin(tile_columns.T, tile_values)
    mixed = out = None
    for hop in range(HOPS):
        first, last = hop == 0, hop == HOPS - 1
        from_chip = lax.ppermute(to_chip, "dom", chip_pairs)
        from_core = lax.ppermute(to_core, "dom", core_pairs)
        spread = jnp.broadcast_to(hub[None], (count, hub_dev, width))
        gathered = lax.all_to_all(spread, "dom", 0, 0).reshape(hub_total, width)

        operands = fixed + pin(z)
        out_shape, out_specs = [pltpu.HBM(z_like, F32)], [hbm]
        scratch = [
            SMEM((per_block, blocks), int32), VMEM(tile_values.shape, BF16), VMEM(z_like, BF16),
            VMEM(z_like, F32), pltpu.SemaphoreType.DMA((3 + 2 * blocks,)),
        ]
        if first:
            operands += pin(hub_weight.T)
            out_shape += [shape((blocks, tile, rim_rows + hub_total), BF16)]
            out_specs += [vmem]
            scratch.insert(3, VMEM((hub_total, row_count), BF16))
        own, *rest = call(
            functools.partial(own_kernel, first=first), f"own{hop}", 2 * row_count * per_block * tile * width,
            out_shape=out_shape, in_specs=[hbm] * len(operands), out_specs=out_specs, scratch_shapes=scratch,
        )(*operands)
        if first:
            (mixed,) = rest

        operands = lists + pin(own) + [mixed, dmat, from_chip, from_core, gathered]
        in_specs = [hbm] * 4 + [vmem] * 5
        aliases = {}
        if hop:
            aliases = {len(operands): 0, len(operands) + 1: 1}
            operands += pin(*out)
            in_specs += [hbm] * 2
        out_shape, out_specs = list(whole), [hbm] * 2
        scratch = [
            VMEM((blocks, tile, split), BF16), VMEM((blocks, tile, extra), BF16), VMEM(z_like, F32),
            VMEM((rim_rows + hub_total, width), BF16), pltpu.SemaphoreType.DMA((3 + 4 * blocks,)),
        ]
        if not last:
            out_shape += [pltpu.HBM(z_like, BF16)] + sends
            out_specs += [hbm] + [vmem] * 3
            scratch = tables + [VMEM(z_like, BF16)] + scratch
        got = call(
            functools.partial(merge_kernel, hop=hop, last=last), f"merge{hop}",
            2 * row_count * (rim_rows + hub_total) * width,
            out_shape=out_shape, in_specs=in_specs, out_specs=out_specs, input_output_aliases=aliases,
            scratch_shapes=scratch,
        )(*operands)
        out = got[:2]
        if not last:
            z, to_chip, to_core, hub = got[2:]
    return out[0].reshape(HOPS, row_count, split), out[1].reshape(HOPS, row_count, extra)


def solution(mesh):
    placed = (
        P("dom", None),
        P("dom", None),
        P("dom", None, None, None),
        P("dom", None),
        P("dom", None, None),
        P("dom", None),
        P("dom"),
        P("dom", None),
        P("dom"),
    )
    return jax.shard_map(
        body,
        mesh=mesh,
        in_specs=placed,
        out_specs=(P(None, "dom", None), P(None, "dom", None)),
        check_vma=False,
    )
```

time: 86.3 us -> 64.2 us (0.74)
  local copies, waits for them, and re-layouts: 29.1 us -> 2.16 us
  blocking collectives: 21.6 us -> 0 us
  Pallas kernels: 12.9 us -> 30 us
  starting transfers between devices: 15 us -> 21.9 us
  waiting for transfers between devices: 5.83 us -> 8.72 us
    unnamed x66 -> x0, local copies, waits for them, and re-layouts: 26.5 us -> none
    all_to_all x2 -> x0, blocking collectives: 21.6 us -> none  [body(): gathered = lax.all_to_all(spread, 'dom', 0, 0).reshape(hub_total, width)]
    pallas_call x4 -> x7, Pallas kernels: 12.9 us -> 30 us  [the longest x3 13.8 us: body(): call(functools.partial(own_kernel, first=first), f'own{hop}', 2 * row_cou...]
    all_to_all x1 -> x3, starting transfers between devices: 5.04 us -> 11.9 us  [body(): gathered = lax.all_to_all(spread, 'dom', 0, 0).reshape(hub_total, width)]
    all_to_all x1 -> x3, waiting for transfers between devices: 5.81 us -> 8.71 us  [body(): gathered = lax.all_to_all(spread, 'dom', 0, 0).reshape(hub_total, width)]
    reshape x3, local copies, waits for them, and re-layouts: 1.88 us -> 0.1 us  [body(): gathered = lax.all_to_all(spread, 'dom', 0, 0).reshape(hub_total, width)]
    broadcast_in_dim x3, local copies, waits for them, and re-layouts: 0.76 us -> 2.05 us  [body(): spread = jnp.broadcast_to(hub[None], (count, hub_dev, width))]
  transfers between devices with their start and end apart: 7 -> 9, of which waited for: 1 -> 3; matrix products, arithmetic and copies ran while one was open for 5% -> 3% of each run, Pallas kernels for 0% -> 22%
where the time goes in v2:
time: 64.2 us; the launch traced here: 63.7 us
  Pallas kernels  30 us (47%)
  starting transfers between devices  21.9 us (34%)
  waiting for transfers between devices  8.72 us (14%)
  local copies, waits for them, and re-layouts  2.16 us (3%)
  between operations  0.94 us (1%)
    pallas_call x3, Pallas kernels, body(): call(functools.partial(own_kernel, first=first), f'own{hop}', 2 * row_cou...  13.8 us
    pallas_call x3, Pallas kernels, body(): call(functools.partial(merge_kernel, hop=hop, last=last), f'merge{hop}',...  13.5 us
    all_to_all x3, starting transfers between devices, body(): gathered = lax.all_to_all(spread, 'dom', 0, 0).reshape(hub_total, width)  11.9 us
    all_to_all x3, waiting for transfers between devices, body(): gathered = lax.all_to_all(spread, 'dom', 0, 0).reshape(hub_total, width)  8.71 us
    ppermute x3, starting transfers between devices, body(): from_core = lax.ppermute(to_core, 'dom', core_pairs)  7.99 us
    pallas_call x1, Pallas kernels, body(): call(prologue_kernel, 'prologue', 10 ** 8, out_shape=[pltpu.HBM(z_like, B...  2.64 us
    broadcast_in_dim x3, local copies, waits for them, and re-layouts, body(): spread = jnp.broadcast_to(hub[None], (count, hub_dev, width))  2.05 us
    ppermute x3, starting transfers between devices, body(): from_chip = lax.ppermute(to_chip, 'dom', chip_pairs)  2.04 us
  transfers between devices with their start and end apart: 9, of which 3 were waited for; matrix products, arithmetic and copies ran while one was open for 3% of the time, Pallas kernels for 22%

profile of v2, /device:TPU:0, one launch (start us, length us, event | category | flops | bytes accessed | tf_op | source)
XLA Modules:
  0.0 63.7 jit_solution(12405742639177675541)
XLA Ops:
  0.6 2.6 %prologue.1 = (bf16[8,128,640]{2,1,0:T(8,128)(2,1)}, f32[8,128,128]{2,1,0:T(8,128)S(1)}, bf16[2,128,640]{2,1,0:T(8,128)(2,1)S(1)}, bf16[2,128,640]{2,1,0:T(8,128)(2,1)S(1)}, bf16[2,640]{1,0:T(2,128)(2,1)S(1)}) custom-call(s32[1,2,2]{2,1,0:T(2,128)} %blocks_hbm.7, s32[1,2]{1,0:T(1,128)} %count_hbm.7, s32[2]{0:T(128)} %hubs_hbm.7, s32[8,128]{1,0:T(8,128)} %bitcast.15, ...), custom_call_target="tpu_custom_call" | custom-call | flops 100000000 | tf_op jit(solution)/shard_map/prologue/pallas_call | solution.py:214
  3.3 0.7 %collective-permute-start = (bf16[2,128,640]{2,1,0:T(8,128)(2,1)S(1)}, bf16[2,128,640]{2,1,0:T(8,128)(2,1)S(1)}, u32[]{:S(2)}, u32[]{:S(2)}) collective-permute-start(bf16[2,128,640]{2,1,0:T(8,128)(2,1)S(1)} %get-tuple-element.27), channel_id=1, source_target_pairs={{1,2},{2,1},{3,4},{4,3},{5,6},{6,5},{7,8},{8,7},{9,10},{10,9},{11,... | collective-permute-start | bytes 983048 | tf_op jit(solution)/shard_map/ppermute | solution.py:235
  4.0 4.4 %collective-permute-start.1 = (bf16[2,128,640]{2,1,0:T(8,128)(2,1)S(1)}, bf16[2,128,640]{2,1,0:T(8,128)(2,1)S(1)}, u32[]{:S(2)}, u32[]{:S(2)}) collective-permute-start(bf16[2,128,640]{2,1,0:T(8,128)(2,1)S(1)} %get-tuple-element.28), channel_id=1, source_target_pairs={{0,1},{1,0},{2,3},{3,2},{4,5},{5,4},{6,7},{7,6},{8,9},{9,8},{10,11... | collective-permute-start | bytes 983048 | tf_op jit(solution)/shard_map/ppermute | solution.py:236
  8.3 0.7 %broadcast_in_dim.6 = bf16[32,2,640]{2,1,0:T(2,128)(2,1)} broadcast(bf16[2,640]{1,0:T(2,128)(2,1)S(1)} %get-tuple-element.29), dimensions={1,2} | broadcast | bytes 84480 | tf_op jit(solution)/shard_map/broadcast_in_dim | solution.py:237
  9.0 4.9 %all-to-all-start = ((bf16[32,2,640]{2,1,0:T(2,128)(2,1)}), bf16[32,2,640]{2,1,0:T(2,128)(2,1)S(1)}, u32[]{:S(2)}, u32[]{:S(2)}) async-start(bf16[32,2,640]{2,1,0:T(2,128)(2,1)} %broadcast_in_dim.6), calls=%async_computation | async-start | bytes 163840 | tf_op jit(solution)/shard_map/all_to_all | solution.py:238
  14.0 5.0 %own0.1 = (f32[8,128,640]{2,1,0:T(8,128)}, bf16[8,128,576]{2,1,0:T(8,128)(2,1)S(1)}) custom-call(s32[4,8]{1,0:T(4,128)} %bitcast.12, bf16[8,4,128,128]{3,2,1,0:T(8,128)(2,1)} %tiles_hbm.5, bf16[8,128,640]{2,1,0:T(8,128)(2,1)} %get-tuple-element.23.z_hbm, bf16[64,1024]{1,0:T(8,128)(2,1)} %bitcast.11), custom_call_target="tpu_custom_call" | custom-call | flops 671088640 | tf_op jit(solution)/shard_map/own0/pallas_call | solution.py:251
  19.0 2.6 %all-to-all-done = bf16[32,2,640]{2,1,0:T(2,128)(2,1)S(1)} async-done(((bf16[32,2,640]{2,1,0:T(2,128)(2,1)}), bf16[32,2,640]{2,1,0:T(2,128)(2,1)S(1)}, u32[]{:S(2)}, u32[]{:S(2)}) %all-to-all-start) | async-done | bytes 81952 | tf_op jit(solution)/shard_map/all_to_all | solution.py:238
  21.6 0.0 collective-permute-done.from_chip_ref
  21.6 0.0 collective-permute-done.1.from_core_ref
  21.6 4.6 %merge0.1 = (bf16[3,8,128,512]{3,2,1,0:T(8,128)(2,1)}, bf16[3,8,128,128]{3,2,1,0:T(8,128)(2,1)}, bf16[8,128,640]{2,1,0:T(8,128)(2,1)}, bf16[2,128,640]{2,1,0:T(8...) custom-call(s32[1,2,2]{2,1,0:T(2,128)} %blocks_hbm.7, s32[1,2]{1,0:T(1,128)} %count_hbm.7, ...), custom_call_target="tpu_custom_call" | custom-call | flops 754974720 | tf_op jit(solution)/shard_map/merge0/pallas_call | solution.py:274
  26.2 0.7 %collective-permute-start.2 = (bf16[2,128,640]{2,1,0:T(8,128)(2,1)S(1)}, bf16[2,128,640]{2,1,0:T(8,128)(2,1)S(1)}, u32[]{:S(2)}, u32[]{:S(2)}) collective-permute-start(bf16[2,128,640]{2,1,0:T(8,128)(2,1)S(1)} %get-tuple-element.31), channel_id=1, source_target_pairs={{1,2},{2,1},{3,4},{4,3},{5,6},{6,5},{7,8},{8,7},{9,10},{10,9},{11,... | collective-permute-start | bytes 983048 | tf_op jit(solution)/shard_map/ppermute | solution.py:235
  26.9 1.8 %collective-permute-start.3 = (bf16[2,128,640]{2,1,0:T(8,128)(2,1)S(1)}, bf16[2,128,640]{2,1,0:T(8,128)(2,1)S(1)}, u32[]{:S(2)}, u32[]{:S(2)}) collective-permute-start(bf16[2,128,640]{2,1,0:T(8,128)(2,1)S(1)} %get-tuple-element.32), channel_id=1, source_target_pairs={{0,1},{1,0},{2,3},{3,2},{4,5},{5,4},{6,7},{7,6},{8,9},{9,8},{10,11... | collective-permute-start | bytes 983048 | tf_op jit(solution)/shard_map/ppermute | solution.py:236
  28.7 0.7 %broadcast_in_dim.7 = bf16[32,2,640]{2,1,0:T(2,128)(2,1)} broadcast(bf16[2,640]{1,0:T(2,128)(2,1)S(1)} %get-tuple-element.33), dimensions={1,2} | broadcast | bytes 84480 | tf_op jit(solution)/shard_map/broadcast_in_dim | solution.py:237
  29.4 3.4 %all-to-all-start.1 = ((bf16[32,2,640]{2,1,0:T(2,128)(2,1)}), bf16[32,2,640]{2,1,0:T(2,128)(2,1)S(1)}, u32[]{:S(2)}, u32[]{:S(2)}) async-start(bf16[32,2,640]{2,1,0:T(2,128)(2,1)} %broadcast_in_dim.7), calls=%async_computation.1 | async-start | bytes 163840 | tf_op jit(solution)/shard_map/all_to_all | solution.py:238
  32.9 4.4 %own1.1.own_hbm = f32[8,128,640]{2,1,0:T(8,128)} custom-call(s32[4,8]{1,0:T(4,128)} %bitcast.13, bf16[8,4,128,128]{3,2,1,0:T(8,128)(2,1)} %tiles_hbm.5, bf16[8,128,640]{2,1,0:T(8,128)(2,1)} %get-tuple-element.30.z_hbm), custom_call_target="tpu_custom_call" | custom-call | flops 671088640 | tf_op jit(solution)/shard_map/own1/pallas_call | solution.py:251
  37.3 3.2 %all-to-all-done.1 = bf16[32,2,640]{2,1,0:T(2,128)(2,1)S(1)} async-done(((bf16[32,2,640]{2,1,0:T(2,128)(2,1)}), bf16[32,2,640]{2,1,0:T(2,128)(2,1)S(1)}, u32[]{:S(2)}, u32[]{:S(2)}) %all-to-all-start.1) | async-done | bytes 81952 | tf_op jit(solution)/shard_map/all_to_all | solution.py:238
  40.5 0.0 collective-permute-done.2.from_chip_ref
  40.5 0.0 collective-permute-done.3.from_core_ref
  40.5 4.6 %merge1.1 = (bf16[3,8,128,512]{3,2,1,0:T(8,128)(2,1)}, bf16[3,8,128,128]{3,2,1,0:T(8,128)(2,1)}, bf16[8,128,640]{2,1,0:T(8,128)(2,1)}, bf16[2,128,640]{2,1,0:T(8...) custom-call(s32[1,2,2]{2,1,0:T(2,128)} %blocks_hbm.7, ...), custom_call_target="tpu_custom_call", output_to_operand_aliasing={{0}: (9, {}), {1}: (10, {})} | custom-call | flops 754974720 | tf_op jit(solution)/shard_map/merge1/pallas_call | solution.py:274
  45.2 0.7 %collective-permute-start.4 = (bf16[2,128,640]{2,1,0:T(8,128)(2,1)S(1)}, bf16[2,128,640]{2,1,0:T(8,128)(2,1)S(1)}, u32[]{:S(2)}, u32[]{:S(2)}) collective-permute-start(bf16[2,128,640]{2,1,0:T(8,128)(2,1)S(1)} %get-tuple-element.37), channel_id=1, source_target_pairs={{1,2},{2,1},{3,4},{4,3},{5,6},{6,5},{7,8},{8,7},{9,10},{10,9},{11,... | collective-permute-start | bytes 983048 | tf_op jit(solution)/shard_map/ppermute | solution.py:235
  45.8 1.8 %collective-permute-start.5 = (bf16[2,128,640]{2,1,0:T(8,128)(2,1)S(1)}, bf16[2,128,640]{2,1,0:T(8,128)(2,1)S(1)}, u32[]{:S(2)}, u32[]{:S(2)}) collective-permute-start(bf16[2,128,640]{2,1,0:T(8,128)(2,1)S(1)} %get-tuple-element.38), channel_id=1, source_target_pairs={{0,1},{1,0},{2,3},{3,2},{4,5},{5,4},{6,7},{7,6},{8,9},{9,8},{10,11... | collective-permute-start | bytes 983048 | tf_op jit(solution)/shard_map/ppermute | solution.py:236
  47.7 0.7 %broadcast_in_dim.8 = bf16[32,2,640]{2,1,0:T(2,128)(2,1)} broadcast(bf16[2,640]{1,0:T(2,128)(2,1)S(1)} %get-tuple-element.39), dimensions={1,2} | broadcast | bytes 84480 | tf_op jit(solution)/shard_map/broadcast_in_dim | solution.py:237
  48.3 3.5 %all-to-all-start.2 = ((bf16[32,2,640]{2,1,0:T(2,128)(2,1)}), bf16[32,2,640]{2,1,0:T(2,128)(2,1)S(1)}, u32[]{:S(2)}, u32[]{:S(2)}) async-start(bf16[32,2,640]{2,1,0:T(2,128)(2,1)} %broadcast_in_dim.8), calls=%async_computation.2 | async-start | bytes 163840 | tf_op jit(solution)/shard_map/all_to_all | solution.py:238
  51.9 4.4 %own2.1.own_hbm = f32[8,128,640]{2,1,0:T(8,128)} custom-call(s32[4,8]{1,0:T(4,128)} %bitcast.14, bf16[8,4,128,128]{3,2,1,0:T(8,128)(2,1)} %tiles_hbm.5, bf16[8,128,640]{2,1,0:T(8,128)(2,1)} %get-tuple-element.36.z_hbm), custom_call_target="tpu_custom_call" | custom-call | flops 671088640 | tf_op jit(solution)/shard_map/own2/pallas_call | solution.py:251
  56.3 3.0 %all-to-all-done.2 = bf16[32,2,640]{2,1,0:T(2,128)(2,1)S(1)} async-done(((bf16[32,2,640]{2,1,0:T(2,128)(2,1)}), bf16[32,2,640]{2,1,0:T(2,128)(2,1)S(1)}, u32[]{:S(2)}, u32[]{:S(2)}) %all-to-all-start.2) | async-done | bytes 81952 | tf_op jit(solution)/shard_map/all_to_all | solution.py:238
  59.3 0.0 collective-permute-done.4.from_chip_ref
  59.3 0.0 collective-permute-done.5.from_core_ref
  59.3 4.2 %merge2.1 = (bf16[3,8,128,512]{3,2,1,0:T(8,128)(2,1)}, bf16[3,8,128,128]{3,2,1,0:T(8,128)(2,1)}) custom-call(s32[1,2,2]{2,1,0:T(2,128)} %blocks_hbm.7, s32[1,2]{1,0:T(1,128)} %count_hbm.7, s32[2]{0:T(128)} %hubs_hbm.7, f32[8,128,640]{2,1,0:T(8,128)} %own2.1.own_hbm, ...), custom_call_target="tpu_custom_call", output_to_operand_aliasing={{0}: (9, {}), {1}: (10, {})} | custom-call | flops 754974720 | tf_op jit(solution)/shard_map/merge2/pallas_call | solution.py:274
  (3 shorter events, 0.1 us)
Async XLA Ops:
  3.3 18.3 %collective-permute-start = (bf16[2,128,640]{2,1,0:T(8,128)(2,1)S(1)}, bf16[2,128,640]{2,1,0:T(8,128)(2,1)S(1)}, u32[]{:S(2)}, u32[]{:S(2)}) collective-permute-start(bf16[2,128,640]{2,1,0:T(8,128)(2,1)S(1)} %get-tuple-element.27), channel_id=1, source_target_pairs={{1,2},{2,1},{3,4},{4,3},{5,6},{6,5},{7,8},{8,7},{9,10},{10,9},{11,... | collective-permute-start | bytes 983048 | tf_op jit(solution)/shard_map/ppermute | solution.py:235
  4.0 17.6 %collective-permute-start.1 = (bf16[2,128,640]{2,1,0:T(8,128)(2,1)S(1)}, bf16[2,128,640]{2,1,0:T(8,128)(2,1)S(1)}, u32[]{:S(2)}, u32[]{:S(2)}) collective-permute-start(bf16[2,128,640]{2,1,0:T(8,128)(2,1)S(1)} %get-tuple-element.28), channel_id=1, source_target_pairs={{0,1},{1,0},{2,3},{3,2},{4,5},{5,4},{6,7},{7,6},{8,9},{9,8},{10,11... | collective-permute-start | bytes 983048 | tf_op jit(solution)/shard_map/ppermute | solution.py:236
  9.0 12.5 %all-to-all-start = ((bf16[32,2,640]{2,1,0:T(2,128)(2,1)}), bf16[32,2,640]{2,1,0:T(2,128)(2,1)S(1)}, u32[]{:S(2)}, u32[]{:S(2)}) async-start(bf16[32,2,640]{2,1,0:T(2,128)(2,1)} %broadcast_in_dim.6), calls=%async_computation | async-start | bytes 163840 | tf_op jit(solution)/shard_map/all_to_all | solution.py:238
  26.2 14.2 %collective-permute-start.2 = (bf16[2,128,640]{2,1,0:T(8,128)(2,1)S(1)}, bf16[2,128,640]{2,1,0:T(8,128)(2,1)S(1)}, u32[]{:S(2)}, u32[]{:S(2)}) collective-permute-start(bf16[2,128,640]{2,1,0:T(8,128)(2,1)S(1)} %get-tuple-element.31), channel_id=1, source_target_pairs={{1,2},{2,1},{3,4},{4,3},{5,6},{6,5},{7,8},{8,7},{9,10},{10,9},{11,... | collective-permute-start | bytes 983048 | tf_op jit(solution)/shard_map/ppermute | solution.py:235
  26.9 13.6 %collective-permute-start.3 = (bf16[2,128,640]{2,1,0:T(8,128)(2,1)S(1)}, bf16[2,128,640]{2,1,0:T(8,128)(2,1)S(1)}, u32[]{:S(2)}, u32[]{:S(2)}) collective-permute-start(bf16[2,128,640]{2,1,0:T(8,128)(2,1)S(1)} %get-tuple-element.32), channel_id=1, source_target_pairs={{0,1},{1,0},{2,3},{3,2},{4,5},{5,4},{6,7},{7,6},{8,9},{9,8},{10,11... | collective-permute-start | bytes 983048 | tf_op jit(solution)/shard_map/ppermute | solution.py:236
  29.4 11.0 %all-to-all-start.1 = ((bf16[32,2,640]{2,1,0:T(2,128)(2,1)}), bf16[32,2,640]{2,1,0:T(2,128)(2,1)S(1)}, u32[]{:S(2)}, u32[]{:S(2)}) async-start(bf16[32,2,640]{2,1,0:T(2,128)(2,1)} %broadcast_in_dim.7), calls=%async_computation.1 | async-start | bytes 163840 | tf_op jit(solution)/shard_map/all_to_all | solution.py:238
  45.2 14.2 %collective-permute-start.4 = (bf16[2,128,640]{2,1,0:T(8,128)(2,1)S(1)}, bf16[2,128,640]{2,1,0:T(8,128)(2,1)S(1)}, u32[]{:S(2)}, u32[]{:S(2)}) collective-permute-start(bf16[2,128,640]{2,1,0:T(8,128)(2,1)S(1)} %get-tuple-element.37), channel_id=1, source_target_pairs={{1,2},{2,1},{3,4},{4,3},{5,6},{6,5},{7,8},{8,7},{9,10},{10,9},{11,... | collective-permute-start | bytes 983048 | tf_op jit(solution)/shard_map/ppermute | solution.py:235
  45.8 13.5 %collective-permute-start.5 = (bf16[2,128,640]{2,1,0:T(8,128)(2,1)S(1)}, bf16[2,128,640]{2,1,0:T(8,128)(2,1)S(1)}, u32[]{:S(2)}, u32[]{:S(2)}) collective-permute-start(bf16[2,128,640]{2,1,0:T(8,128)(2,1)S(1)} %get-tuple-element.38), channel_id=1, source_target_pairs={{0,1},{1,0},{2,3},{3,2},{4,5},{5,4},{6,7},{7,6},{8,9},{9,8},{10,11... | collective-permute-start | bytes 983048 | tf_op jit(solution)/shard_map/ppermute | solution.py:236
  48.3 10.9 %all-to-all-start.2 = ((bf16[32,2,640]{2,1,0:T(2,128)(2,1)}), bf16[32,2,640]{2,1,0:T(2,128)(2,1)S(1)}, u32[]{:S(2)}, u32[]{:S(2)}) async-start(bf16[32,2,640]{2,1,0:T(2,128)(2,1)} %broadcast_in_dim.8), calls=%async_computation.2 | async-start | bytes 163840 | tf_op jit(solution)/shard_map/all_to_all | solution.py:238

commit v3 on v0

v3 whole, which is shorter than its diff:
```python
import functools

import jax
import jax.numpy as jnp
from jax import lax
from jax.experimental import pallas as pl
from jax.experimental.pallas import tpu as pltpu
from jax.sharding import PartitionSpec as P

HOPS = 3
VMEM = pltpu.VMEM
SMEM = pltpu.SMEM
BF16 = jnp.bfloat16
F32 = jnp.float32
GROUP = 16


def scale_rows(value, dmat):
    lanes = dmat.shape[1]
    pieces = [value[:, i : i + lanes] * dmat for i in range(0, value.shape[1], lanes)]
    return pieces[0] if len(pieces) == 1 else jnp.concatenate(pieces, axis=1)


def finish(copies):
    for copy in copies:
        copy.wait()


class Copies:
    def __init__(self, sems):
        self.sems, self.used = sems, 0

    def start(self, *pairs):
        begun = []
        for source, target in pairs:
            copy = pltpu.make_async_copy(source, target, self.sems.at[self.used])
            copy.start()
            begun.append(copy)
            self.used += 1
        return begun


def block_rows(index, tile):
    return pl.ds(pl.multiple_of(index * tile, tile), tile)


def one_row(ref, row):
    base = pl.multiple_of(row // GROUP * GROUP, GROUP)
    near = ref[pl.ds(base, GROUP), :].astype(F32)
    at = lax.broadcasted_iota(jnp.int32, near.shape, 0) == row % GROUP
    return jnp.sum(jnp.where(at, near, 0.0), axis=0, keepdims=True)


def factor_block(degree_ref, index):
    tile = degree_ref.shape[1]
    root = lax.rsqrt(degree_ref[pl.ds(index, 1), :].astype(F32))
    return jnp.broadcast_to(root, (tile, tile)).T


def slots(blocks_ref, count_ref):
    parity = lax.axis_index("dom") % 2
    send_most = blocks_ref.shape[2]
    return [
        (blocks_ref[0, side, slot], slot < count_ref[0, side])
        for side in (parity, 1 - parity)
        for slot in range(send_most)
    ]


def gather_sent(source_ref, target_ref, listed, hubs_ref):
    tile = (target_ref.shape[0] - GROUP) // len(listed)
    width = source_ref.shape[1]
    for i, (index, live) in enumerate(listed):
        block = source_ref[block_rows(index, tile), :]
        target_ref[i * tile : (i + 1) * tile, :] = jnp.where(live, block, jnp.zeros_like(block))
    rows = [one_row(source_ref, hubs_ref[i]) for i in range(hubs_ref.shape[0])]
    rows.append(jnp.zeros((GROUP - len(rows), width), F32))
    target_ref[len(listed) * tile :, :] = jnp.concatenate(rows, axis=0).astype(target_ref.dtype)


def place_received(from_chip_ref, from_core_ref, gathered_ref, received):
    rim_rows = from_chip_ref.shape[0]
    parity = lax.axis_index("dom") % 2
    received[block_rows(parity, rim_rows), :] = from_chip_ref[...]
    received[block_rows(1 - parity, rim_rows), :] = from_core_ref[...]
    received[2 * rim_rows :, :] = gathered_ref[...]


def prologue_kernel(
    blocks_hbm, count_hbm, hubs_hbm, degree_hbm, features_hbm, embeddings_hbm,
    chip_ref, core_ref, spread_ref,
    blocks_ref, count_ref, hubs_ref, degree_ref, features_ref, embeddings_ref, sems,
):
    copies = Copies(sems)
    tile = degree_ref.shape[1]
    split = features_ref.shape[1]
    tables = copies.start(
        (blocks_hbm, blocks_ref), (count_hbm, count_ref), (hubs_hbm, hubs_ref), (degree_hbm, degree_ref)
    )
    rows = copies.start((features_hbm, features_ref), (embeddings_hbm, embeddings_ref))
    finish(tables)
    listed = slots(blocks_ref, count_ref)
    factors = [factor_block(degree_ref, index) for index, _ in listed]
    finish(rows)
    half = len(listed) // 2
    for i, (index, live) in enumerate(listed):
        target = (chip_ref, core_ref)[i // half]
        into = slice((i % half) * tile, (i % half + 1) * tile)
        for source, columns in ((features_ref, slice(0, split)), (embeddings_ref, slice(split, None))):
            block = scale_rows(source[block_rows(index, tile), :].astype(F32), factors[i])
            target[into, columns] = jnp.where(live, block, 0.0).astype(BF16)
    rows = []
    for i in range(hubs_ref.shape[0]):
        row = hubs_ref[i]
        degrees = degree_ref[pl.ds(row // tile, 1), :].astype(F32)
        at = lax.broadcasted_iota(jnp.int32, degrees.shape, 1) == row % tile
        factor = lax.rsqrt(jnp.broadcast_to(jnp.sum(jnp.where(at, degrees, 0.0), axis=1, keepdims=True), (1, tile)))
        whole = jnp.concatenate([one_row(features_ref, row), one_row(embeddings_ref, row)], axis=1)
        rows.append(scale_rows(whole, factor))
    hub = jnp.concatenate(rows, axis=0).astype(BF16)
    spread_ref[...] = jnp.broadcast_to(hub[None], spread_ref.shape)


def bulk_kernel(*refs, hop, rim, per_block):
    refs = list(refs)
    take = lambda n: [refs.pop(0) for _ in range(n)]
    blocks_hbm, count_hbm, hubs_hbm, columns_hbm, tiles_hbm = take(5)
    first, last = hop == 0, hop == HOPS - 1
    if first:
        degree_hbm, features_hbm, embeddings_hbm, weight_hbm = take(4)
        own_hbm, own_sent_hbm, mixed_out, dmat_out, mixed_sent, dmat_sent = take(6)
    else:
        old_own_hbm, mixed_hbm, dmat_hbm, received_hbm = take(4)
        if hop > 1:
            take(2)
        all_features, all_embeddings, own_hbm = take(3)
        if last:
            mixed_out, dmat_out = take(2)
        else:
            (own_sent_hbm,) = take(1)
    blocks_ref, count_ref, hubs_ref, columns_ref = take(4)
    tiles_ref, z_ref, own_ref, own_sent, mixed_ref, dmat_ref, features_ref, embeddings_ref = take(8)
    if first:
        degree_ref, weight_ref, sems = refs
    else:
        received, sems = refs
    copies = Copies(sems)
    blocks, _, tile, _ = tiles_ref.shape
    row_count, width = z_ref.shape
    split = features_ref.shape[1]
    half = row_count // 2
    halves = (slice(0, half), slice(half, row_count))

    tables = copies.start(
        (blocks_hbm, blocks_ref), (count_hbm, count_ref), (hubs_hbm, hubs_ref), (columns_hbm, columns_ref)
    )
    writes = []
    if first:
        inputs = copies.start((degree_hbm, degree_ref), (features_hbm, features_ref),
                              (embeddings_hbm, embeddings_ref))
        late = copies.start((tiles_hbm, tiles_ref), (weight_hbm, weight_ref))
        finish(inputs)
    else:
        inputs = copies.start((received_hbm, received), (mixed_hbm, mixed_ref), (dmat_hbm, dmat_ref))
        olds = [copies.start((old_own_hbm.at[h, :], own_ref.at[h, :])) for h in halves]
        late = copies.start((tiles_hbm, tiles_ref))
        finish(inputs)
    for b in range(blocks):
        rows = slice(b * tile, (b + 1) * tile)
        if first:
            dmat = factor_block(degree_ref, b)
            dmat_ref[rows, :] = dmat
            z_ref[rows, :split] = scale_rows(features_ref[rows, :].astype(F32), dmat).astype(BF16)
            z_ref[rows, split:] = scale_rows(embeddings_ref[rows, :].astype(F32), dmat).astype(BF16)
        else:
            total = jnp.dot(mixed_ref[rows, :], received[...], preferred_element_type=F32)
            if b * tile in (0, half):
                finish(olds[b * tile // half])
            dmat = dmat_ref[rows, :]
            fresh = scale_rows(own_ref[rows, :] + total, dmat).astype(BF16)
            features_ref[rows, :] = fresh[:, :split]
            embeddings_ref[rows, :] = fresh[:, split:]
            z_ref[rows, :] = scale_rows(fresh.astype(F32), dmat).astype(BF16)
    if not first:
        writes += copies.start(
            (features_ref, all_features.at[hop - 1]), (embeddings_ref, all_embeddings.at[hop - 1])
        )
    finish(late)
    finish(tables)
    for b in range(blocks):
        rows = slice(b * tile, (b + 1) * tile)
        columns = [columns_ref[k, b] for k in range(per_block)]
        tiles = [tiles_ref[b, k] for k in range(per_block)]
        values = jnp.concatenate(
            [jnp.where(c < blocks, t, jnp.zeros_like(t)) for c, t in zip(columns, tiles)], axis=1
        )
        picked = jnp.concatenate([z_ref[block_rows(jnp.minimum(c, blocks - 1), tile), :] for c in columns], axis=0)
        own_ref[rows, :] = jnp.dot(values, picked, preferred_element_type=F32)
        writes += copies.start((own_ref.at[rows, :], own_hbm.at[rows, :]))
        if first:
            for slot in range(rim):
                total = jnp.zeros((tile, tile), F32)
                for c, t in zip(columns, tiles):
                    total += jnp.where(c == blocks + slot, t, jnp.zeros_like(t)).astype(F32)
                mixed_ref[rows, slot * tile : (slot + 1) * tile] = total.astype(BF16)
            mixed_ref[rows, rim * tile :] = weight_ref[:, rows].astype(F32).T.astype(BF16)
    if not last:
        listed = slots(blocks_ref, count_ref)
        gather_sent(own_ref, own_sent, listed, hubs_ref)
        writes += copies.start((own_sent, own_sent_hbm))
    if first:
        writes += copies.start((mixed_ref, mixed_out), (dmat_ref, dmat_out))
        gather_sent(mixed_ref, mixed_sent, listed, hubs_ref)
        gather_sent(dmat_ref, dmat_sent, listed, hubs_ref)
    if last:
        mixed_out[...] = mixed_ref[...]
        dmat_out[...] = dmat_ref[...]
    finish(writes)


def edge_kernel(
    own_hbm, mixed_ref, dmat_ref, from_chip_ref, from_core_ref, gathered_ref,
    chip_ref, core_ref, spread_ref, received_hbm,
    own_ref, received, sems,
):
    copies = Copies(sems)
    rim_rows = chip_ref.shape[0]
    hub_dev = spread_ref.shape[1]
    parts = [slice(0, rim_rows), slice(rim_rows, own_ref.shape[0])]
    reads = [copies.start((own_hbm.at[part, :], own_ref.at[part, :])) for part in parts]
    place_received(from_chip_ref, from_core_ref, gathered_ref, received)
    writes = copies.start((received, received_hbm))
    for part, read in zip(parts, reads):
        total = jnp.dot(mixed_ref[part, :], received[...], preferred_element_type=F32)
        finish(read)
        dmat = dmat_ref[part, :]
        fresh = scale_rows(own_ref[part, :] + total, dmat).astype(BF16)
        sent = scale_rows(fresh.astype(F32), dmat)
        if part.start == 0:
            chip_ref[...] = sent.astype(BF16)
        else:
            core_ref[...] = sent[:rim_rows].astype(BF16)
            hub = sent[rim_rows : rim_rows + hub_dev].astype(BF16)
            spread_ref[...] = jnp.broadcast_to(hub[None], spread_ref.shape)
    finish(writes)


def final_kernel(
    own_hbm, mixed_ref, dmat_ref, from_chip_ref, from_core_ref, gathered_ref, _, __,
    all_features, all_embeddings,
    own_ref, features_ref, embeddings_ref, received, sems,
):
    copies = Copies(sems)
    tile = dmat_ref.shape[1]
    split = features_ref.shape[1]
    blocks = [slice(i, i + tile) for i in range(0, own_ref.shape[0], tile)]
    reads = [copies.start((own_hbm.at[rows, :], own_ref.at[rows, :])) for rows in blocks]
    place_received(from_chip_ref, from_core_ref, gathered_ref, received)
    writes = []
    for rows, read in zip(blocks, reads):
        total = jnp.dot(mixed_ref[rows, :], received[...], preferred_element_type=F32)
        finish(read)
        fresh = scale_rows(own_ref[rows, :] + total, dmat_ref[rows, :]).astype(BF16)
        features_ref[rows, :] = fresh[:, :split]
        embeddings_ref[rows, :] = fresh[:, split:]
        writes += copies.start(
            (features_ref.at[rows, :], all_features.at[HOPS - 1, rows, :]),
            (embeddings_ref.at[rows, :], all_embeddings.at[HOPS - 1, rows, :]),
        )
    finish(writes)


def body(
    features, embeddings, tile_values, tile_columns, send_blocks, send_count, hub_rows, hub_weight, degree,
):
    row_count, split = features.shape
    blocks, per_block, tile, _ = tile_values.shape
    extra = embeddings.shape[1]
    width = split + extra
    send_most = send_blocks.shape[2]
    hub_dev = hub_rows.shape[0]
    hub_total = hub_weight.shape[1]
    count = lax.axis_size("dom")
    rim = 2 * send_most
    deep = rim * tile + hub_total
    sent = rim * tile + GROUP

    vmem = pl.BlockSpec(memory_space=VMEM)
    hbm = pl.BlockSpec(memory_space=pltpu.HBM)
    shape = jax.ShapeDtypeStruct
    int32 = jnp.int32

    def pin(*values):
        return [pltpu.with_memory_space_constraint(value, pltpu.HBM) for value in values]

    def call(kernel, name, flops, out_shape, scratch, sems, in_hbm, operands, aliases={}):
        specs = [hbm] * in_hbm + [vmem] * (len(operands) - in_hbm)
        for source in aliases:
            specs[source] = hbm
        return pl.pallas_call(
            kernel,
            name=name,
            out_shape=out_shape,
            in_specs=specs,
            out_specs=[vmem if isinstance(out, shape) else hbm for out in out_shape],
            scratch_shapes=scratch + [pltpu.SemaphoreType.DMA((sems,))],
            input_output_aliases=aliases,
            compiler_params=pltpu.CompilerParams(vmem_limit_bytes=32 * 2**20),
            cost_estimate=pl.CostEstimate(flops=flops, bytes_accessed=0, transcendentals=0),
        )(*operands)

    tables = [SMEM(send_blocks.shape, int32), SMEM(send_count.shape, int32), SMEM(hub_rows.shape, int32)]
    sends = [
        shape((send_most * tile, width), BF16), shape((send_most * tile, width), BF16),
        shape((count, hub_dev, width), BF16),
    ]
    whole = [pltpu.HBM((HOPS, row_count, split), BF16), pltpu.HBM((HOPS, row_count, extra), BF16)]
    row_buffers = [VMEM((row_count, split), BF16), VMEM((row_count, extra), BF16)]
    lists = pin(send_blocks, send_count, hub_rows)
    rows = pin(degree.reshape(blocks, tile), features, embeddings)
    to_chip, to_core, spread = call(
        prologue_kernel, "prologue", 10**8, sends,
        tables + [VMEM((blocks, tile), int32)] + row_buffers, 6, 6, lists + rows,
    )

    core_pairs = [(i, i ^ 1) for i in range(count) if i ^ 1 < count]
    chip_pairs = [p for i in range(1, count - 1, 2) for p in ((i, i + 1), (i + 1, i))]
    fixed = lists + pin(tile_columns.T, tile_values)
    out = []
    for hop in range(HOPS):
        first, last = hop == 0, hop == HOPS - 1
        from_chip = lax.ppermute(to_chip, "dom", chip_pairs)
        from_core = lax.ppermute(to_core, "dom", core_pairs)
        gathered = lax.all_to_all(spread, "dom", 0, 0).reshape(hub_total, width)

        scratch = tables + [
            SMEM((per_block, blocks), int32), VMEM(tile_values.shape, BF16), VMEM((row_count, width), BF16),
            VMEM((row_count, width), F32), VMEM((sent, width), F32),
            VMEM((row_count, deep), BF16), VMEM((row_count, tile), F32),
        ] + row_buffers
        aliases = {}
        full_own = pltpu.HBM((row_count, width), F32)
        sent_own = pltpu.HBM((sent, width), F32)
        if first:
            operands = fixed + rows + pin(hub_weight.T)
            out_shape = [full_own, sent_own, pltpu.HBM((row_count, deep), BF16), pltpu.HBM((row_count, tile), F32),
                         shape((sent, deep), BF16), shape((sent, tile), F32)]
            scratch += [VMEM((blocks, tile), int32), VMEM((hub_total, row_count), BF16)]
        else:
            operands = fixed + pin(own, mixed, dmat, received)
            if out:
                aliases = {len(operands): 0, len(operands) + 1: 1}
                operands += pin(*out)
            out_shape = whole + [full_own]
            out_shape += [shape((row_count, deep), BF16), shape((row_count, tile), F32)] if last else [sent_own]
            scratch += [VMEM((deep, width), BF16)]
        got = call(
            functools.partial(bulk_kernel, hop=hop, rim=rim, per_block=per_block), f"bulk{hop}",
            4 * row_count * per_block * tile * width, out_shape, scratch, 16 + blocks,
            len(operands), operands, aliases,
        )
        if first:
            own, own_sent, mixed, dmat, mixed_sent, dmat_sent = got
        else:
            out, (own, *got) = got[:2], got[2:]
            if last:
                mixed_here, dmat_here = got
            else:
                (own_sent,) = got

        flops = 2 * row_count * deep * width
        if last:
            operands = pin(own) + [mixed_here, dmat_here, from_chip, from_core, gathered]
            aliases = {len(operands): 0, len(operands) + 1: 1}
            out = call(
                final_kernel, "final", flops, whole,
                [VMEM((row_count, width), F32)] + row_buffers + [VMEM((deep, width), BF16)], 3 * blocks,
                1, operands + pin(*out), aliases,
            )
        else:
            to_chip, to_core, spread, received = call(
                edge_kernel, f"edge{hop}", flops, sends + [pltpu.HBM((deep, width), BF16)],
                [VMEM((sent, width), F32), VMEM((deep, width), BF16)], 3,
                1, pin(own_sent) + [mixed_sent, dmat_sent, from_chip, from_core, gathered],
            )
    return out[0], out[1]


def solution(mesh):
    placed = (
        P("dom", None),
        P("dom", None),
        P("dom", None, None, None),
        P("dom", None),
        P("dom", None, None),
        P("dom", None),
        P("dom"),
        P("dom", None),
        P("dom"),
    )
    return jax.shard_map(
        body,
        mesh=mesh,
        in_specs=placed,
        out_specs=(P(None, "dom", None), P(None, "dom", None)),
        check_vma=False,
    )
```

time: 220 us -> 59.4 us (0.27)
  blocking collectives: 119 us -> 0 us
  local copies, waits for them, and re-layouts: 47.2 us -> 0.1 us
  Pallas kernels: 0 us -> 29.1 us
  matrix products: 24.9 us -> 0 us
  other arithmetic: 11.9 us -> 0 us
  starting transfers between devices: 15.1 us -> 23.5 us
  waiting for transfers between devices: 0.02 us -> 5.35 us
    all_gather x3 -> x0, blocking collectives: 119 us -> none  [body(): gathered_hubs = lax.all_gather(hub_local, 'dom', axis=0, tiled=True)]
    pallas_call x0 -> x7, Pallas kernels: none -> 29.1 us  [call(): pl.pallas_call(kernel, name=name, out_shape=out_shape, in_specs=specs, ou...]
    dot_general x6 -> x0, matrix products: 24.9 us -> none  [the longest x3 14.9 us: body(): jnp.einsum('bkij,bkjw->biw', tile_values, picked, preferred_element_type=...]
    gather x9 -> x0, local copies, waits for them, and re-layouts: 18 us -> none  [the longest x3 10.5 us: body(): picked = extended[tile_columns]]
    all_to_all x0 -> x3, starting transfers between devices: none -> 13.4 us  [body(): gathered = lax.all_to_all(spread, 'dom', 0, 0).reshape(hub_total, width)]
    reshape x5 -> x3, local copies, waits for them, and re-layouts: 13.2 us -> 0.1 us  [body(): gathered = lax.all_to_all(spread, 'dom', 0, 0).reshape(hub_total, width)]
    unnamed x51 -> x0, local copies, waits for them, and re-layouts: 10.4 us -> none
    all_to_all x0 -> x3, waiting for transfers between devices: none -> 5.34 us  [body(): gathered = lax.all_to_all(spread, 'dom', 0, 0).reshape(hub_total, width)]
  transfers between devices with their start and end apart: 6 -> 9, of which waited for: 0 -> 3; matrix products, arithmetic and copies ran while one was open for 6% -> 0% of each run, Pallas kernels for 0% -> 29%
where the time goes in v3:
time: 59.4 us; the launch traced here: 59 us
  Pallas kernels  29.1 us (49%)
  starting transfers between devices  23.5 us (40%)
  waiting for transfers between devices  5.35 us (9%)
  between operations  0.94 us (2%)
    pallas_call x7, Pallas kernels, call(): pl.pallas_call(kernel, name=name, out_shape=out_shape, in_specs=specs, ou...  29.1 us
    all_to_all x3, starting transfers between devices, body(): gathered = lax.all_to_all(spread, 'dom', 0, 0).reshape(hub_total, width)  13.4 us
    ppermute x3, starting transfers between devices, body(): from_core = lax.ppermute(to_core, 'dom', core_pairs)  8.06 us
    all_to_all x3, waiting for transfers between devices, body(): gathered = lax.all_to_all(spread, 'dom', 0, 0).reshape(hub_total, width)  5.34 us
    ppermute x3, starting transfers between devices, body(): from_chip = lax.ppermute(to_chip, 'dom', chip_pairs)  2.04 us
  transfers between devices with their start and end apart: 9, of which 3 were waited for; matrix products, arithmetic and copies ran while one was open for 0% of the time, Pallas kernels for 29%

profile of v3, /device:TPU:0, one launch (start us, length us, event | category | flops | bytes accessed | tf_op | source)
XLA Modules:
  0.0 59.0 jit_solution(5896985481848223925)
XLA Ops:
  0.6 2.2 %prologue.1 = (bf16[256,640]{1,0:T(8,128)(2,1)S(1)}, bf16[256,640]{1,0:T(8,128)(2,1)S(1)}, bf16[32,2,640]{2,1,0:T(2,128)(2,1)}) custom-call(s32[1,2,2]{2,1,0:T(2,128)} %refs_0_.5, s32[1,2]{1,0:T(1,128)} %refs_1_.5, s32[2]{0:T(128)} %refs_2_.5, s32[8,128]{1,0:T(8,128)} %bitcast.6, bf16[1024,512]{1,0:T(8,128)(2,1)} %features_hbm.1, ...), custom_call_target="tpu_custom_call" | custom-call | flops 100000000 | tf_op jit(solution)/shard_map/prologue/pallas_call | solution.py:300
  2.8 0.7 %collective-permute-start = (bf16[256,640]{1,0:T(8,128)(2,1)S(1)}, bf16[256,640]{1,0:T(8,128)(2,1)S(1)}, u32[]{:S(2)}, u32[]{:S(2)}) collective-permute-start(bf16[256,640]{1,0:T(8,128)(2,1)S(1)} %get-tuple-element.34), channel_id=1, source_target_pairs={{1,2},{2,1},{3,4},{4,3},{5,6},{6,5},{7,8},{8,7},{9,10},{10,9},{11,... | collective-permute-start | bytes 983048 | tf_op jit(solution)/shard_map/ppermute | solution.py:332
  3.5 4.4 %collective-permute-start.1 = (bf16[256,640]{1,0:T(8,128)(2,1)S(1)}, bf16[256,640]{1,0:T(8,128)(2,1)S(1)}, u32[]{:S(2)}, u32[]{:S(2)}) collective-permute-start(bf16[256,640]{1,0:T(8,128)(2,1)S(1)} %get-tuple-element.35), channel_id=1, source_target_pairs={{0,1},{1,0},{2,3},{3,2},{4,5},{5,4},{6,7},{7,6},{8,9},{9,8},{10,11... | collective-permute-start | bytes 983048 | tf_op jit(solution)/shard_map/ppermute | solution.py:333
  7.9 4.9 %all-to-all-start = ((bf16[32,2,640]{2,1,0:T(2,128)(2,1)}), bf16[32,2,640]{2,1,0:T(2,128)(2,1)S(1)}, u32[]{:S(2)}, u32[]{:S(2)}) async-start(bf16[32,2,640]{2,1,0:T(2,128)(2,1)} %get-tuple-element.36), calls=%async_computation | async-start | bytes 163840 | tf_op jit(solution)/shard_map/all_to_all | solution.py:334
  12.8 5.2 %bulk0.1 = (f32[1024,640]{1,0:T(8,128)}, f32[528,640]{1,0:T(8,128)}, bf16[1024,576]{1,0:T(8,128)(2,1)}, f32[1024,128]{1,0:T(8,128)}, bf16[528,576]{1,0:T(8,128)(2,1)S(1)}, /*index=5*/f32[528,128]{1,0:T(8,128)S(1)}) custom-call(s32[1,2,2]{2,1,0:T(2,128)} %refs_0_.5, s32[1,2]{1,0:T(1,128)} %refs_1_.5, s32[2]{0:T(128)} %refs_2_.5, s32[4,8]{1,0:T(4,128)} %bitcast.3, ...), custom_call_target="tpu_custom_call" | custom-call | flops 1342177280 | tf_op jit(solution)/shard_map/bulk0/pallas_call | solution.py:300
  18.0 2.4 %all-to-all-done = bf16[32,2,640]{2,1,0:T(2,128)(2,1)S(1)} async-done(((bf16[32,2,640]{2,1,0:T(2,128)(2,1)}), bf16[32,2,640]{2,1,0:T(2,128)(2,1)S(1)}, u32[]{:S(2)}, u32[]{:S(2)}) %all-to-all-start) | async-done | bytes 81952 | tf_op jit(solution)/shard_map/all_to_all | solution.py:334
  20.4 0.0 collective-permute-done.from_chip_ref
  20.5 0.0 collective-permute-done.1.from_core_ref
  20.5 2.8 %edge0.1 = (bf16[256,640]{1,0:T(8,128)(2,1)S(1)}, bf16[256,640]{1,0:T(8,128)(2,1)S(1)}, bf16[32,2,640]{2,1,0:T(2,128)(2,1)}, bf16[576,640]{1,0:T(8,128)(2,1)}) custom-call(f32[528,640]{1,0:T(8,128)} %get-tuple-element.31.own_hbm, bf16[528,576]{1,0:T(8,128)(2,1)S(1)} %get-tuple-element.32.mixed_ref, f32[528,128]{1,0:T(8,128)S(1)} %get-tuple-element.33.dmat_ref, ...), custom_call_target="tpu_custom_call" | custom-call | flops 754974720 | tf_op jit(solution)/shard_map/edge0/pallas_call | solution.py:300
  23.3 0.7 %collective-permute-start.2 = (bf16[256,640]{1,0:T(8,128)(2,1)S(1)}, bf16[256,640]{1,0:T(8,128)(2,1)S(1)}, u32[]{:S(2)}, u32[]{:S(2)}) collective-permute-start(bf16[256,640]{1,0:T(8,128)(2,1)S(1)} %get-tuple-element.40), channel_id=1, source_target_pairs={{1,2},{2,1},{3,4},{4,3},{5,6},{6,5},{7,8},{8,7},{9,10},{10,9},{11,... | collective-permute-start | bytes 983048 | tf_op jit(solution)/shard_map/ppermute | solution.py:332
  24.0 1.8 %collective-permute-start.3 = (bf16[256,640]{1,0:T(8,128)(2,1)S(1)}, bf16[256,640]{1,0:T(8,128)(2,1)S(1)}, u32[]{:S(2)}, u32[]{:S(2)}) collective-permute-start(bf16[256,640]{1,0:T(8,128)(2,1)S(1)} %get-tuple-element.41), channel_id=1, source_target_pairs={{0,1},{1,0},{2,3},{3,2},{4,5},{5,4},{6,7},{7,6},{8,9},{9,8},{10,11... | collective-permute-start | bytes 983048 | tf_op jit(solution)/shard_map/ppermute | solution.py:333
  25.8 3.6 %all-to-all-start.1 = ((bf16[32,2,640]{2,1,0:T(2,128)(2,1)}), bf16[32,2,640]{2,1,0:T(2,128)(2,1)S(1)}, u32[]{:S(2)}, u32[]{:S(2)}) async-start(bf16[32,2,640]{2,1,0:T(2,128)(2,1)} %get-tuple-element.42), calls=%async_computation.1 | async-start | bytes 163840 | tf_op jit(solution)/shard_map/all_to_all | solution.py:334
  29.4 6.3 %bulk1.1 = (bf16[3,1024,512]{2,1,0:T(8,128)(2,1)}, bf16[3,1024,128]{2,1,0:T(8,128)(2,1)}, f32[1024,640]{1,0:T(8,128)}, f32[528,640]{1,0:T(8,128)}) custom-call(s32[1,2,2]{2,1,0:T(2,128)} %refs_0_.5, s32[1,2]{1,0:T(1,128)} %refs_1_.5, s32[2]{0:T(128)} %refs_2_.5, s32[4,8]{1,0:T(4,128)} %bitcast.4, bf16[8,4,128,128]{3,2,1,0:T(8,128)(2,1)} %refs_4_.5, ...), custom_call_target="tpu_custom_call" | custom-call | flops 1342177280 | tf_op jit(solution)/shard_map/bulk1/pallas_call | solution.py:300
  35.7 1.3 %all-to-all-done.1 = bf16[32,2,640]{2,1,0:T(2,128)(2,1)S(1)} async-done(((bf16[32,2,640]{2,1,0:T(2,128)(2,1)}), bf16[32,2,640]{2,1,0:T(2,128)(2,1)S(1)}, u32[]{:S(2)}, u32[]{:S(2)}) %all-to-all-start.1) | async-done | bytes 81952 | tf_op jit(solution)/shard_map/all_to_all | solution.py:334
  37.0 0.0 collective-permute-done.2.from_chip_ref
  37.0 0.0 collective-permute-done.3.from_core_ref
  37.0 2.8 %edge1.1 = (bf16[256,640]{1,0:T(8,128)(2,1)S(1)}, bf16[256,640]{1,0:T(8,128)(2,1)S(1)}, bf16[32,2,640]{2,1,0:T(2,128)(2,1)}, bf16[576,640]{1,0:T(8,128)(2,1)}) custom-call(f32[528,640]{1,0:T(8,128)} %get-tuple-element.39.own_hbm, bf16[528,576]{1,0:T(8,128)(2,1)S(1)} %get-tuple-element.32.mixed_ref, f32[528,128]{1,0:T(8,128)S(1)} %get-tuple-element.33.dmat_ref, ...), custom_call_target="tpu_custom_call" | custom-call | flops 754974720 | tf_op jit(solution)/shard_map/edge1/pallas_call | solution.py:300
  39.9 0.7 %collective-permute-start.4 = (bf16[256,640]{1,0:T(8,128)(2,1)S(1)}, bf16[256,640]{1,0:T(8,128)(2,1)S(1)}, u32[]{:S(2)}, u32[]{:S(2)}) collective-permute-start(bf16[256,640]{1,0:T(8,128)(2,1)S(1)} %get-tuple-element.49), channel_id=1, source_target_pairs={{1,2},{2,1},{3,4},{4,3},{5,6},{6,5},{7,8},{8,7},{9,10},{10,9},{11,... | collective-permute-start | bytes 983048 | tf_op jit(solution)/shard_map/ppermute | solution.py:332
  40.5 1.9 %collective-permute-start.5 = (bf16[256,640]{1,0:T(8,128)(2,1)S(1)}, bf16[256,640]{1,0:T(8,128)(2,1)S(1)}, u32[]{:S(2)}, u32[]{:S(2)}) collective-permute-start(bf16[256,640]{1,0:T(8,128)(2,1)S(1)} %get-tuple-element.50), channel_id=1, source_target_pairs={{0,1},{1,0},{2,3},{3,2},{4,5},{5,4},{6,7},{7,6},{8,9},{9,8},{10,11... | collective-permute-start | bytes 983048 | tf_op jit(solution)/shard_map/ppermute | solution.py:333
  42.4 4.8 %all-to-all-start.2 = ((bf16[32,2,640]{2,1,0:T(2,128)(2,1)}), bf16[32,2,640]{2,1,0:T(2,128)(2,1)S(1)}, u32[]{:S(2)}, u32[]{:S(2)}) async-start(bf16[32,2,640]{2,1,0:T(2,128)(2,1)} %get-tuple-element.51), calls=%async_computation.2 | async-start | bytes 163840 | tf_op jit(solution)/shard_map/all_to_all | solution.py:334
  47.2 5.8 %bulk2.1 = (bf16[3,1024,512]{2,1,0:T(8,128)(2,1)}, bf16[3,1024,128]{2,1,0:T(8,128)(2,1)}, f32[1024,640]{1,0:T(8,128)}, bf16[1024,576]{1,0:T(8,128)(2,1)S(1)}, f32[1024,128]{1,0:T(8,128)S(1)}) custom-call(s32[1,2,2]{2,1,0:T(2,128)} %refs_0_.5, s32[1,2]{1,0:T(1,128)} %refs_1_.5, s32[2]{0:T(128)} %refs_2_.5, ...), custom_call_target="tpu_custom_call", output_to_operand_aliasing={{0}: (9, {}), {1}: (10, {})} | custom-call | flops 1342177280 | tf_op jit(solution)/shard_map/bulk2/pallas_call | solution.py:300
  53.0 1.6 %all-to-all-done.2 = bf16[32,2,640]{2,1,0:T(2,128)(2,1)S(1)} async-done(((bf16[32,2,640]{2,1,0:T(2,128)(2,1)}), bf16[32,2,640]{2,1,0:T(2,128)(2,1)S(1)}, u32[]{:S(2)}, u32[]{:S(2)}) %all-to-all-start.2) | async-done | bytes 81952 | tf_op jit(solution)/shard_map/all_to_all | solution.py:334
  54.7 0.0 collective-permute-done.4.from_chip_ref
  54.7 0.0 collective-permute-done.5.from_core_ref
  54.7 4.1 %final.1 = (bf16[3,1024,512]{2,1,0:T(8,128)(2,1)}, bf16[3,1024,128]{2,1,0:T(8,128)(2,1)}) custom-call(f32[1024,640]{1,0:T(8,128)} %get-tuple-element.46.own_hbm, bf16[1024,576]{1,0:T(8,128)(2,1)S(1)} %get-tuple-element.47.mixed_ref, f32[1024,128]{1,0:T(8,128)S(1)} %get-tuple-element.48.dmat_ref, ...), custom_call_target="tpu_custom_call", output_to_operand_aliasing={{0}: (6, {}), {1}: (7, {})} | custom-call | flops 754974720 | tf_op jit(solution)/shard_map/final/pallas_call | solution.py:300
  (3 shorter events, 0.1 us)
Async XLA Ops:
  2.8 17.6 %collective-permute-start = (bf16[256,640]{1,0:T(8,128)(2,1)S(1)}, bf16[256,640]{1,0:T(8,128)(2,1)S(1)}, u32[]{:S(2)}, u32[]{:S(2)}) collective-permute-start(bf16[256,640]{1,0:T(8,128)(2,1)S(1)} %get-tuple-element.34), channel_id=1, source_target_pairs={{1,2},{2,1},{3,4},{4,3},{5,6},{6,5},{7,8},{8,7},{9,10},{10,9},{11,... | collective-permute-start | bytes 983048 | tf_op jit(solution)/shard_map/ppermute | solution.py:332
  3.5 16.9 %collective-permute-start.1 = (bf16[256,640]{1,0:T(8,128)(2,1)S(1)}, bf16[256,640]{1,0:T(8,128)(2,1)S(1)}, u32[]{:S(2)}, u32[]{:S(2)}) collective-permute-start(bf16[256,640]{1,0:T(8,128)(2,1)S(1)} %get-tuple-element.35), channel_id=1, source_target_pairs={{0,1},{1,0},{2,3},{3,2},{4,5},{5,4},{6,7},{7,6},{8,9},{9,8},{10,11... | collective-permute-start | bytes 983048 | tf_op jit(solution)/shard_map/ppermute | solution.py:333
  7.9 12.5 %all-to-all-start = ((bf16[32,2,640]{2,1,0:T(2,128)(2,1)}), bf16[32,2,640]{2,1,0:T(2,128)(2,1)S(1)}, u32[]{:S(2)}, u32[]{:S(2)}) async-start(bf16[32,2,640]{2,1,0:T(2,128)(2,1)} %get-tuple-element.36), calls=%async_computation | async-start | bytes 163840 | tf_op jit(solution)/shard_map/all_to_all | solution.py:334
  23.3 13.7 %collective-permute-start.2 = (bf16[256,640]{1,0:T(8,128)(2,1)S(1)}, bf16[256,640]{1,0:T(8,128)(2,1)S(1)}, u32[]{:S(2)}, u32[]{:S(2)}) collective-permute-start(bf16[256,640]{1,0:T(8,128)(2,1)S(1)} %get-tuple-element.40), channel_id=1, source_target_pairs={{1,2},{2,1},{3,4},{4,3},{5,6},{6,5},{7,8},{8,7},{9,10},{10,9},{11,... | collective-permute-start | bytes 983048 | tf_op jit(solution)/shard_map/ppermute | solution.py:332
  24.0 13.1 %collective-permute-start.3 = (bf16[256,640]{1,0:T(8,128)(2,1)S(1)}, bf16[256,640]{1,0:T(8,128)(2,1)S(1)}, u32[]{:S(2)}, u32[]{:S(2)}) collective-permute-start(bf16[256,640]{1,0:T(8,128)(2,1)S(1)} %get-tuple-element.41), channel_id=1, source_target_pairs={{0,1},{1,0},{2,3},{3,2},{4,5},{5,4},{6,7},{7,6},{8,9},{9,8},{10,11... | collective-permute-start | bytes 983048 | tf_op jit(solution)/shard_map/ppermute | solution.py:333
  25.8 11.2 %all-to-all-start.1 = ((bf16[32,2,640]{2,1,0:T(2,128)(2,1)}), bf16[32,2,640]{2,1,0:T(2,128)(2,1)S(1)}, u32[]{:S(2)}, u32[]{:S(2)}) async-start(bf16[32,2,640]{2,1,0:T(2,128)(2,1)} %get-tuple-element.42), calls=%async_computation.1 | async-start | bytes 163840 | tf_op jit(solution)/shard_map/all_to_all | solution.py:334
  39.9 14.8 %collective-permute-start.4 = (bf16[256,640]{1,0:T(8,128)(2,1)S(1)}, bf16[256,640]{1,0:T(8,128)(2,1)S(1)}, u32[]{:S(2)}, u32[]{:S(2)}) collective-permute-start(bf16[256,640]{1,0:T(8,128)(2,1)S(1)} %get-tuple-element.49), channel_id=1, source_target_pairs={{1,2},{2,1},{3,4},{4,3},{5,6},{6,5},{7,8},{8,7},{9,10},{10,9},{11,... | collective-permute-start | bytes 983048 | tf_op jit(solution)/shard_map/ppermute | solution.py:332
  40.5 14.1 %collective-permute-start.5 = (bf16[256,640]{1,0:T(8,128)(2,1)S(1)}, bf16[256,640]{1,0:T(8,128)(2,1)S(1)}, u32[]{:S(2)}, u32[]{:S(2)}) collective-permute-start(bf16[256,640]{1,0:T(8,128)(2,1)S(1)} %get-tuple-element.50), channel_id=1, source_target_pairs={{0,1},{1,0},{2,3},{3,2},{4,5},{5,4},{6,7},{7,6},{8,9},{9,8},{10,11... | collective-permute-start | bytes 983048 | tf_op jit(solution)/shard_map/ppermute | solution.py:333
  42.4 12.2 %all-to-all-start.2 = ((bf16[32,2,640]{2,1,0:T(2,128)(2,1)}), bf16[32,2,640]{2,1,0:T(2,128)(2,1)S(1)}, u32[]{:S(2)}, u32[]{:S(2)}) async-start(bf16[32,2,640]{2,1,0:T(2,128)(2,1)} %get-tuple-element.51), calls=%async_computation.2 | async-start | bytes 163840 | tf_op jit(solution)/shard_map/all_to_all | solution.py:334

commit v4 on v3

v4 whole, which is shorter than its diff:
```python
import functools

import jax
import jax.numpy as jnp
from jax import lax
from jax.experimental import pallas as pl
from jax.experimental.pallas import tpu as pltpu
from jax.sharding import PartitionSpec as P

HOPS = 3
VMEM = pltpu.VMEM
SMEM = pltpu.SMEM
BF16 = jnp.bfloat16
F32 = jnp.float32
GROUP = 16


def scale_rows(value, dmat):
    lanes = dmat.shape[1]
    pieces = [value[:, i : i + lanes] * dmat for i in range(0, value.shape[1], lanes)]
    return pieces[0] if len(pieces) == 1 else jnp.concatenate(pieces, axis=1)


def finish(copies):
    for copy in copies:
        copy.wait()


class Copies:
    def __init__(self, sems):
        self.sems, self.used = sems, 0

    def start(self, *pairs):
        begun = []
        for source, target in pairs:
            copy = pltpu.make_async_copy(source, target, self.sems.at[self.used])
            copy.start()
            begun.append(copy)
            self.used += 1
        return begun


def block_rows(index, tile):
    return pl.ds(pl.multiple_of(index * tile, tile), tile)


def one_row(ref, row):
    base = pl.multiple_of(row // GROUP * GROUP, GROUP)
    near = ref[pl.ds(base, GROUP), :].astype(F32)
    at = lax.broadcasted_iota(jnp.int32, near.shape, 0) == row % GROUP
    return jnp.sum(jnp.where(at, near, 0.0), axis=0, keepdims=True)


def lane_to_rows(root):
    return jnp.broadcast_to(root, (root.shape[1], root.shape[1])).T


def roots_of(degree_ref, index):
    return lax.rsqrt(degree_ref[pl.ds(index, 1), :].astype(F32))


def factor_block(degree_ref, index):
    return lane_to_rows(roots_of(degree_ref, index))


def hub_roots(degree_ref, hubs_ref):
    tile = degree_ref.shape[1]
    found = []
    for i in range(hubs_ref.shape[0]):
        roots = roots_of(degree_ref, hubs_ref[i] // tile)
        at = lax.broadcasted_iota(jnp.int32, roots.shape, 1) == hubs_ref[i] % tile
        found.append(jnp.sum(jnp.where(at, roots, 0.0), axis=1, keepdims=True))
    return found


def gather_roots(degree_ref, roots_ref, listed, hubs_ref):
    tile = degree_ref.shape[1]
    rows = [roots_of(degree_ref, index) for index, _ in listed]
    lane = lax.broadcasted_iota(jnp.int32, (1, tile), 1)
    last = jnp.zeros((1, tile), F32)
    for i, root in enumerate(hub_roots(degree_ref, hubs_ref)):
        last = jnp.where(lane == i, jnp.broadcast_to(root, (1, tile)), last)
    roots_ref[...] = jnp.concatenate(rows + [last], axis=0)


def quarters(row_count):
    part = row_count // 4
    return [slice(i, i + part) for i in range(0, row_count, part)]


def slots(blocks_ref, count_ref):
    parity = lax.axis_index("dom") % 2
    send_most = blocks_ref.shape[2]
    return [
        (blocks_ref[0, side, slot], slot < count_ref[0, side])
        for side in (parity, 1 - parity)
        for slot in range(send_most)
    ]


def gather_sent(source_ref, target_ref, listed, hubs_ref):
    tile = (target_ref.shape[0] - GROUP) // len(listed)
    width = source_ref.shape[1]
    for i, (index, live) in enumerate(listed):
        block = source_ref[block_rows(index, tile), :]
        target_ref[i * tile : (i + 1) * tile, :] = jnp.where(live, block, jnp.zeros_like(block))
    rows = [one_row(source_ref, hubs_ref[i]) for i in range(hubs_ref.shape[0])]
    rows.append(jnp.zeros((GROUP - len(rows), width), F32))
    target_ref[len(listed) * tile :, :] = jnp.concatenate(rows, axis=0).astype(target_ref.dtype)


def place_received(from_chip_ref, from_core_ref, gathered_ref, received):
    rim_rows = from_chip_ref.shape[0]
    parity = lax.axis_index("dom") % 2
    received[block_rows(parity, rim_rows), :] = from_chip_ref[...]
    received[block_rows(1 - parity, rim_rows), :] = from_core_ref[...]
    received[2 * rim_rows :, :] = gathered_ref[...]


def spread_rows(rows, spread_ref, spread_hbm, copies):
    spread_ref[...] = jnp.broadcast_to(rows[None], spread_ref.shape)
    return copies.start((spread_ref, spread_hbm))


def prologue_kernel(
    blocks_hbm, count_hbm, hubs_hbm, degree_hbm, features_hbm, embeddings_hbm,
    chip_ref, core_ref, spread_hbm,
    blocks_ref, count_ref, hubs_ref, degree_ref, features_ref, embeddings_ref, spread_ref, sems,
):
    copies = Copies(sems)
    tile = degree_ref.shape[1]
    split = features_ref.shape[1]
    tables = copies.start(
        (blocks_hbm, blocks_ref), (count_hbm, count_ref), (hubs_hbm, hubs_ref), (degree_hbm, degree_ref)
    )
    rows = copies.start((features_hbm, features_ref), (embeddings_hbm, embeddings_ref))
    finish(tables)
    listed = slots(blocks_ref, count_ref)
    factors = [factor_block(degree_ref, index) for index, _ in listed]
    finish(rows)
    hubs = []
    for i, root in enumerate(hub_roots(degree_ref, hubs_ref)):
        row = hubs_ref[i]
        whole = jnp.concatenate([one_row(features_ref, row), one_row(embeddings_ref, row)], axis=1)
        hubs.append(scale_rows(whole, jnp.broadcast_to(root, (1, tile))))
    writes = spread_rows(jnp.concatenate(hubs, axis=0).astype(BF16), spread_ref, spread_hbm, copies)
    half = len(listed) // 2
    for i, (index, live) in enumerate(listed):
        target = (chip_ref, core_ref)[i // half]
        into = slice((i % half) * tile, (i % half + 1) * tile)
        for source, columns in ((features_ref, slice(0, split)), (embeddings_ref, slice(split, None))):
            block = scale_rows(source[block_rows(index, tile), :].astype(F32), factors[i])
            target[into, columns] = jnp.where(live, block, 0.0).astype(BF16)
    finish(writes)


def bulk_kernel(*refs, hop, rim, per_block):
    refs = list(refs)
    take = lambda n: [refs.pop(0) for _ in range(n)]
    blocks_hbm, count_hbm, hubs_hbm, columns_hbm, tiles_hbm = take(5)
    first, last = hop == 0, hop == HOPS - 1
    if first:
        degree_hbm, features_hbm, embeddings_hbm, weight_hbm = take(4)
        own_hbm, own_sent, mixed_out, dmat_out, mixed_sent, roots_sent = take(6)
    else:
        old_own_hbm, mixed_hbm, dmat_hbm, received_hbm = take(4)
        if hop > 1:
            take(2)
        all_features, all_embeddings, own_hbm = take(3)
        if last:
            mixed_ref, dmat_ref = take(2)
        else:
            (own_sent,) = take(1)
    blocks_ref, count_ref, hubs_ref, columns_ref = take(4)
    tiles_ref, z_ref, own_ref, features_ref, embeddings_ref = take(5)
    if not last:
        mixed_ref, dmat_ref = take(2)
    if first:
        degree_ref, weight_ref, sems = refs
    else:
        received, old_own_ref, total_ref, sems = refs
    copies = Copies(sems)
    blocks, _, tile, _ = tiles_ref.shape
    row_count, width = z_ref.shape
    split = features_ref.shape[1]
    every = [slice(b * tile, (b + 1) * tile) for b in range(blocks)]

    tables = copies.start((columns_hbm, columns_ref))
    if not last:
        tables += copies.start((blocks_hbm, blocks_ref), (count_hbm, count_ref), (hubs_hbm, hubs_ref))
    writes = []
    if first:
        finish(copies.start((degree_hbm, degree_ref), (features_hbm, features_ref),
                            (embeddings_hbm, embeddings_ref)))
        late = copies.start((tiles_hbm, tiles_ref), (weight_hbm, weight_ref))
        for b, rows in enumerate(every):
            dmat = factor_block(degree_ref, b)
            dmat_ref[rows, :] = dmat
            z_ref[rows, :split] = scale_rows(features_ref[rows, :].astype(F32), dmat).astype(BF16)
            z_ref[rows, split:] = scale_rows(embeddings_ref[rows, :].astype(F32), dmat).astype(BF16)
    else:
        parts = quarters(row_count)
        finish_first = copies.start((received_hbm, received))
        mixes = [copies.start((mixed_hbm.at[rows, :], mixed_ref.at[rows, :])) for rows in parts]
        rest = copies.start((dmat_hbm, dmat_ref), (old_own_hbm, old_own_ref))
        late = copies.start((tiles_hbm, tiles_ref))
        finish(finish_first)
        for rows, mix in zip(parts, mixes):
            finish(mix)
            total_ref[rows, :] = jnp.dot(mixed_ref[rows, :], received[...], preferred_element_type=F32)
        finish(rest)
        for rows in every:
            dmat = dmat_ref[rows, :]
            fresh = scale_rows(old_own_ref[rows, :].astype(F32) + total_ref[rows, :], dmat).astype(BF16)
            features_ref[rows, :] = fresh[:, :split]
            embeddings_ref[rows, :] = fresh[:, split:]
            z_ref[rows, :] = scale_rows(fresh.astype(F32), dmat).astype(BF16)
        writes += copies.start(
            (features_ref, all_features.at[hop - 1]), (embeddings_ref, all_embeddings.at[hop - 1])
        )
    finish(late + tables)
    for b, rows in enumerate(every):
        columns = [columns_ref[k, b] for k in range(per_block)]
        tiles = [tiles_ref[b, k] for k in range(per_block)]
        values = jnp.concatenate(
            [jnp.where(c < blocks, t, jnp.zeros_like(t)) for c, t in zip(columns, tiles)], axis=1
        )
        picked = jnp.concatenate([z_ref[block_rows(jnp.minimum(c, blocks - 1), tile), :] for c in columns], axis=0)
        own_ref[rows, :] = jnp.dot(values, picked, preferred_element_type=F32).astype(BF16)
        if b % 2:
            pair = slice((b - 1) * tile, (b + 1) * tile)
            writes += copies.start((own_ref.at[pair, :], own_hbm.at[pair, :]))
        if first:
            for slot in range(rim):
                total = jnp.zeros((tile, tile), F32)
                for c, t in zip(columns, tiles):
                    total += jnp.where(c == blocks + slot, t, jnp.zeros_like(t)).astype(F32)
                mixed_ref[rows, slot * tile : (slot + 1) * tile] = total.astype(BF16)
            mixed_ref[rows, rim * tile :] = weight_ref[:, rows].astype(F32).T.astype(BF16)
    if blocks % 2:
        writes += copies.start((own_ref.at[every[-1], :], own_hbm.at[every[-1], :]))
    if first:
        writes += copies.start((mixed_ref, mixed_out), (dmat_ref, dmat_out))
    if not last:
        listed = slots(blocks_ref, count_ref)
        gather_sent(own_ref, own_sent, listed, hubs_ref)
    if first:
        gather_sent(mixed_ref, mixed_sent, listed, hubs_ref)
        gather_roots(degree_ref, roots_sent, listed, hubs_ref)
    finish(writes)


def edge_kernel(
    own_ref, mixed_ref, roots_ref, from_chip_ref, from_core_ref, gathered_ref,
    chip_ref, core_ref, spread_hbm, received_hbm,
    total_ref, received, spread_ref, sems,
):
    copies = Copies(sems)
    rim_rows = chip_ref.shape[0]
    hub_dev = spread_ref.shape[1]
    place_received(from_chip_ref, from_core_ref, gathered_ref, received)
    writes = copies.start((received, received_hbm))
    total_ref[...] = jnp.dot(mixed_ref[...], received[...], preferred_element_type=F32)

    tile = roots_ref.shape[1]

    def fresh(part):
        rows = slice(part * tile, min((part + 1) * tile, total_ref.shape[0]))
        dmat = lane_to_rows(roots_ref[part : part + 1, :])[: rows.stop - rows.start]
        kept = scale_rows(own_ref[rows, :].astype(F32) + total_ref[rows, :], dmat).astype(BF16)
        return scale_rows(kept.astype(F32), dmat).astype(BF16)

    send_most = rim_rows // tile
    hub = fresh(2 * send_most)
    writes += spread_rows(hub[:hub_dev], spread_ref, spread_hbm, copies)
    for slot in range(send_most):
        chip_ref[slot * tile : (slot + 1) * tile, :] = fresh(slot)
        core_ref[slot * tile : (slot + 1) * tile, :] = fresh(send_most + slot)
    finish(writes)


def final_kernel(
    own_hbm, mixed_ref, dmat_ref, from_chip_ref, from_core_ref, gathered_ref, _, __,
    all_features, all_embeddings,
    own_ref, total_ref, features_ref, embeddings_ref, received, sems,
):
    copies = Copies(sems)
    split = features_ref.shape[1]
    row_count = own_ref.shape[0]
    reads = copies.start((own_hbm, own_ref))
    place_received(from_chip_ref, from_core_ref, gathered_ref, received)
    parts = quarters(row_count)

    def multiply(rows):
        total_ref[rows, :] = jnp.dot(mixed_ref[rows, :], received[...], preferred_element_type=F32)

    def store(rows):
        fresh = scale_rows(own_ref[rows, :].astype(F32) + total_ref[rows, :], dmat_ref[rows, :]).astype(BF16)
        features_ref[rows, :] = fresh[:, :split]
        embeddings_ref[rows, :] = fresh[:, split:]
        return copies.start(
            (features_ref.at[rows, :], all_features.at[HOPS - 1, rows, :]),
            (embeddings_ref.at[rows, :], all_embeddings.at[HOPS - 1, rows, :]),
        )

    multiply(parts[0])
    multiply(parts[1])
    finish(reads)
    writes = store(parts[0])
    multiply(parts[2])
    writes += store(parts[1])
    multiply(parts[3])
    writes += store(parts[2])
    writes += store(parts[3])
    finish(writes)


def body(
    features, embeddings, tile_values, tile_columns, send_blocks, send_count, hub_rows, hub_weight, degree,
):
    row_count, split = features.shape
    blocks, per_block, tile, _ = tile_values.shape
    extra = embeddings.shape[1]
    width = split + extra
    send_most = send_blocks.shape[2]
    hub_dev = hub_rows.shape[0]
    hub_total = hub_weight.shape[1]
    count = lax.axis_size("dom")
    rim = 2 * send_most
    deep = rim * tile + hub_total
    sent = rim * tile + GROUP

    vmem = pl.BlockSpec(memory_space=VMEM)
    hbm = pl.BlockSpec(memory_space=pltpu.HBM)
    shape = jax.ShapeDtypeStruct
    int32 = jnp.int32

    def pin(*values):
        return [pltpu.with_memory_space_constraint(value, pltpu.HBM) for value in values]

    def call(kernel, name, flops, out_shape, scratch, sems, in_hbm, operands, aliases={}):
        specs = [hbm] * in_hbm + [vmem] * (len(operands) - in_hbm)
        for source, target in aliases.items():
            if not isinstance(out_shape[target], shape):
                specs[source] = hbm
        return pl.pallas_call(
            kernel,
            name=name,
            out_shape=out_shape,
            in_specs=specs,
            out_specs=[vmem if isinstance(out, shape) else hbm for out in out_shape],
            scratch_shapes=scratch + [pltpu.SemaphoreType.DMA((sems,))],
            input_output_aliases=aliases,
            compiler_params=pltpu.CompilerParams(vmem_limit_bytes=32 * 2**20),
            cost_estimate=pl.CostEstimate(flops=flops, bytes_accessed=0, transcendentals=0),
        )(*operands)

    tables = [SMEM(send_blocks.shape, int32), SMEM(send_count.shape, int32), SMEM(hub_rows.shape, int32)]
    sends = [
        shape((send_most * tile, width), BF16), shape((send_most * tile, width), BF16),
        pltpu.HBM((count, hub_dev, width), BF16),
    ]
    spread_buffer = VMEM((count, hub_dev, width), BF16)
    whole = [pltpu.HBM((HOPS, row_count, split), BF16), pltpu.HBM((HOPS, row_count, extra), BF16)]
    row_buffers = [VMEM((row_count, split), BF16), VMEM((row_count, extra), BF16)]
    lists = pin(send_blocks, send_count, hub_rows)
    rows = pin(degree.reshape(blocks, tile), features, embeddings)
    to_chip, to_core, spread = call(
        prologue_kernel, "prologue", 10**8, sends,
        tables + [VMEM((blocks, tile), int32)] + row_buffers + [spread_buffer], 7, 6, lists + rows,
    )

    core_pairs = [(i, i ^ 1) for i in range(count) if i ^ 1 < count]
    chip_pairs = [p for i in range(1, count - 1, 2) for p in ((i, i + 1), (i + 1, i))]
    fixed = lists + pin(tile_columns.T, tile_values)
    out = []
    for hop in range(HOPS):
        first, last = hop == 0, hop == HOPS - 1
        from_chip = lax.ppermute(to_chip, "dom", chip_pairs)
        from_core = lax.ppermute(to_core, "dom", core_pairs)
        gathered = lax.all_to_all(spread, "dom", 0, 0).reshape(hub_total, width)

        scratch = tables + [
            SMEM((per_block, blocks), int32), VMEM(tile_values.shape, BF16), VMEM((row_count, width), BF16),
            VMEM((row_count, width), BF16),
        ] + row_buffers
        if not last:
            scratch += [VMEM((row_count, deep), BF16), VMEM((row_count, tile), F32)]
        aliases = {}
        full_own = pltpu.HBM((row_count, width), BF16)
        sent_shapes = [shape((sent, width), BF16), shape((sent, deep), BF16)]
        if first:
            operands = fixed + rows + pin(hub_weight.T)
            out_shape = [full_own] + sent_shapes + [shape((rim + 1, tile), F32)]
            out_shape[2:2] = [pltpu.HBM((row_count, deep), BF16), pltpu.HBM((row_count, tile), F32)]
            scratch += [VMEM((blocks, tile), int32), VMEM((hub_total, row_count), BF16)]
        else:
            operands = fixed + pin(own, mixed, dmat, received)
            if out:
                aliases = {len(operands): 0, len(operands) + 1: 1}
                operands += pin(*out)
            out_shape = whole + [full_own]
            out_shape += [shape((row_count, deep), BF16), shape((row_count, tile), F32)] if last else sent_shapes[:1]
            scratch += [VMEM((deep, width), BF16), VMEM((row_count, width), BF16), VMEM((row_count, width), F32)]
        got = call(
            functools.partial(bulk_kernel, hop=hop, rim=rim, per_block=per_block), f"bulk{hop}",
            4 * row_count * per_block * tile * width, out_shape, scratch, 16 + blocks,
            len(operands), operands, aliases,
        )
        if first:
            own, own_sent, mixed, dmat, mixed_sent, roots_sent = got
        else:
            out, (own, *got) = got[:2], got[2:]
            if last:
                mixed_here, dmat_here = got
            else:
                (own_sent,) = got

        flops = 2 * row_count * deep * width
        if last:
            operands = pin(own) + [mixed_here, dmat_here, from_chip, from_core, gathered]
            aliases = {len(operands): 0, len(operands) + 1: 1}
            out = call(
                final_kernel, "final", flops, whole,
                [VMEM((row_count, width), BF16), VMEM((row_count, width), F32)] + row_buffers
                + [VMEM((deep, width), BF16)], 9,
                1, operands + pin(*out), aliases,
            )
        else:
            to_chip, to_core, spread, received = call(
                edge_kernel, f"edge{hop}", flops, sends + [pltpu.HBM((deep, width), BF16)],
                [VMEM((sent, width), F32), VMEM((deep, width), BF16), spread_buffer], 2,
                0, [own_sent, mixed_sent, roots_sent, from_chip, from_core, gathered],
                {3: 0, 4: 1},
            )
    return out[0], out[1]


def solution(mesh):
    placed = (
        P("dom", None),
        P("dom", None),
        P("dom", None, None, None),
        P("dom", None),
        P("dom", None, None),
        P("dom", None),
        P("dom"),
        P("dom", None),
        P("dom"),
    )
    return jax.shard_map(
        body,
        mesh=mesh,
        in_specs=placed,
        out_specs=(P(None, "dom", None), P(None, "dom", None)),
        check_vma=False,
    )
```

time: 59.4 us -> 55.4 us (0.933)
  Pallas kernels: 29.1 us -> 25 us
    pallas_call x7, Pallas kernels: 29.1 us -> 25 us  [call(): pl.pallas_call(kernel, name=name, out_shape=out_shape, in_specs=specs, ou...]
  transfers between devices with their start and end apart: 9 -> 9, of which waited for: 3 -> 3; matrix products, arithmetic and copies ran while one was open for 0% -> 0% of each run, Pallas kernels for 29% -> 31%
where the time goes in v4:
time: 55.4 us; the launch traced here: 55 us
  Pallas kernels  25 us (45%)
  starting transfers between devices  23.3 us (42%)
  waiting for transfers between devices  5.69 us (10%)
  between operations  0.94 us (2%)
    pallas_call x7, Pallas kernels, call(): pl.pallas_call(kernel, name=name, out_shape=out_shape, in_specs=specs, ou...  25 us
    all_to_all x3, starting transfers between devices, body(): gathered = lax.all_to_all(spread, 'dom', 0, 0).reshape(hub_total, width)  13.2 us
    ppermute x3, starting transfers between devices, body(): from_core = lax.ppermute(to_core, 'dom', core_pairs)  7.99 us
    all_to_all x3, waiting for transfers between devices, body(): gathered = lax.all_to_all(spread, 'dom', 0, 0).reshape(hub_total, width)  5.67 us
    ppermute x3, starting transfers between devices, body(): from_chip = lax.ppermute(to_chip, 'dom', chip_pairs)  2.04 us
  transfers between devices with their start and end apart: 9, of which 3 were waited for; matrix products, arithmetic and copies ran while one was open for 0% of the time, Pallas kernels for 31%

profile of v4, /device:TPU:0, one launch (start us, length us, event | category | flops | bytes accessed | tf_op | source)
XLA Modules:
  0.0 55.0 jit_solution(9164262831449252921)
XLA Ops:
  0.6 2.1 %prologue.1 = (bf16[256,640]{1,0:T(8,128)(2,1)S(1)}, bf16[256,640]{1,0:T(8,128)(2,1)S(1)}, bf16[32,2,640]{2,1,0:T(2,128)(2,1)}) custom-call(s32[1,2,2]{2,1,0:T(2,128)} %refs_0_.5, s32[1,2]{1,0:T(1,128)} %refs_1_.5, s32[2]{0:T(128)} %refs_2_.5, s32[8,128]{1,0:T(8,128)} %bitcast.3, bf16[1024,512]{1,0:T(8,128)(2,1)} %features_hbm.1, ...), custom_call_target="tpu_custom_call" | custom-call | flops 100000000 | tf_op jit(solution)/shard_map/prologue/pallas_call | solution.py:346
  2.7 0.7 %collective-permute-start = (bf16[256,640]{1,0:T(8,128)(2,1)S(1)}, bf16[256,640]{1,0:T(8,128)(2,1)S(1)}, u32[]{:S(2)}, u32[]{:S(2)}) collective-permute-start(bf16[256,640]{1,0:T(8,128)(2,1)S(1)} %get-tuple-element.34), channel_id=1, source_target_pairs={{1,2},{2,1},{3,4},{4,3},{5,6},{6,5},{7,8},{8,7},{9,10},{10,9},{11,... | collective-permute-start | bytes 983048 | tf_op jit(solution)/shard_map/ppermute | solution.py:379
  3.4 4.4 %collective-permute-start.1 = (bf16[256,640]{1,0:T(8,128)(2,1)S(1)}, bf16[256,640]{1,0:T(8,128)(2,1)S(1)}, u32[]{:S(2)}, u32[]{:S(2)}) collective-permute-start(bf16[256,640]{1,0:T(8,128)(2,1)S(1)} %get-tuple-element.35), channel_id=1, source_target_pairs={{0,1},{1,0},{2,3},{3,2},{4,5},{5,4},{6,7},{7,6},{8,9},{9,8},{10,11... | collective-permute-start | bytes 983048 | tf_op jit(solution)/shard_map/ppermute | solution.py:380
  7.8 4.9 %all-to-all-start = ((bf16[32,2,640]{2,1,0:T(2,128)(2,1)}), bf16[32,2,640]{2,1,0:T(2,128)(2,1)S(1)}, u32[]{:S(2)}, u32[]{:S(2)}) async-start(bf16[32,2,640]{2,1,0:T(2,128)(2,1)} %get-tuple-element.36), calls=%async_computation | async-start | bytes 163840 | tf_op jit(solution)/shard_map/all_to_all | solution.py:381
  12.7 5.6 %bulk0.1 = (bf16[1024,640]{1,0:T(8,128)(2,1)}, bf16[528,640]{1,0:T(8,128)(2,1)S(1)}, bf16[1024,576]{1,0:T(8,128)(2,1)}, f32[1024,128]{1,0:T(8,128)}, bf16[528,576]{1,0:T(8,128)(2,1)S(1)}, /*index=5*/f32[5,128]{1,0:T(8,128)S(1)}) custom-call(s32[1,2,2]{2,1,0:T(2,128)} %refs_0_.5, s32[1,2]{1,0:T(1,128)} %refs_1_.5, s32[2]{0:T(128)} %refs_2_.5, ...), custom_call_target="tpu_custom_call" | custom-call | flops 1342177280 | tf_op jit(solution)/shard_map/bulk0/pallas_call | solution.py:346
  18.3 2.0 %all-to-all-done = bf16[32,2,640]{2,1,0:T(2,128)(2,1)S(1)} async-done(((bf16[32,2,640]{2,1,0:T(2,128)(2,1)}), bf16[32,2,640]{2,1,0:T(2,128)(2,1)S(1)}, u32[]{:S(2)}, u32[]{:S(2)}) %all-to-all-start) | async-done | bytes 81952 | tf_op jit(solution)/shard_map/all_to_all | solution.py:381
  20.3 0.0 collective-permute-done.from_chip_ref
  20.4 0.0 collective-permute-done.1.from_core_ref
  20.4 1.5 %edge0.1 = (bf16[256,640]{1,0:T(8,128)(2,1)S(1)}, bf16[256,640]{1,0:T(8,128)(2,1)S(1)}, bf16[32,2,640]{2,1,0:T(2,128)(2,1)}, bf16[576,640]{1,0:T(8,128)(2,1)}) custom-call(bf16[528,640]{1,0:T(8,128)(2,1)S(1)} %get-tuple-element.31.own_ref, bf16[528,576]{1,0:T(8,128)(2,1)S(1)} %get-tuple-element.32.mixed_ref, ...), custom_call_target="tpu_custom_call", output_to_operand_aliasing={{0}: (3, {}), {1}: (4, {})} | custom-call | flops 754974720 | tf_op jit(solution)/shard_map/edge0/pallas_call | solution.py:346
  21.9 0.7 %collective-permute-start.2 = (bf16[256,640]{1,0:T(8,128)(2,1)S(1)}, bf16[256,640]{1,0:T(8,128)(2,1)S(1)}, u32[]{:S(2)}, u32[]{:S(2)}) collective-permute-start(bf16[256,640]{1,0:T(8,128)(2,1)S(1)} %get-tuple-element.40), channel_id=1, source_target_pairs={{1,2},{2,1},{3,4},{4,3},{5,6},{6,5},{7,8},{8,7},{9,10},{10,9},{11,... | collective-permute-start | bytes 983048 | tf_op jit(solution)/shard_map/ppermute | solution.py:379
  22.6 1.8 %collective-permute-start.3 = (bf16[256,640]{1,0:T(8,128)(2,1)S(1)}, bf16[256,640]{1,0:T(8,128)(2,1)S(1)}, u32[]{:S(2)}, u32[]{:S(2)}) collective-permute-start(bf16[256,640]{1,0:T(8,128)(2,1)S(1)} %get-tuple-element.41), channel_id=1, source_target_pairs={{0,1},{1,0},{2,3},{3,2},{4,5},{5,4},{6,7},{7,6},{8,9},{9,8},{10,11... | collective-permute-start | bytes 983048 | tf_op jit(solution)/shard_map/ppermute | solution.py:380
  24.4 4.0 %all-to-all-start.1 = ((bf16[32,2,640]{2,1,0:T(2,128)(2,1)}), bf16[32,2,640]{2,1,0:T(2,128)(2,1)S(1)}, u32[]{:S(2)}, u32[]{:S(2)}) async-start(bf16[32,2,640]{2,1,0:T(2,128)(2,1)} %get-tuple-element.42), calls=%async_computation.1 | async-start | bytes 163840 | tf_op jit(solution)/shard_map/all_to_all | solution.py:381
  28.4 5.7 %bulk1.1 = (bf16[3,1024,512]{2,1,0:T(8,128)(2,1)}, bf16[3,1024,128]{2,1,0:T(8,128)(2,1)}, bf16[1024,640]{1,0:T(8,128)(2,1)}, bf16[528,640]{1,0:T(8,128)(2,1)S(1)}) custom-call(s32[1,2,2]{2,1,0:T(2,128)} %refs_0_.5, s32[1,2]{1,0:T(1,128)} %refs_1_.5, s32[2]{0:T(128)} %refs_2_.5, s32[4,8]{1,0:T(4,128)} %bitcast.6, bf16[8,4,128,128]{3,2,1,0:T(8,128)(2,1)} %refs_4_.5, ...), custom_call_target="tpu_custom_call" | custom-call | flops 1342177280 | tf_op jit(solution)/shard_map/bulk1/pallas_call | solution.py:346
  34.1 1.9 %all-to-all-done.1 = bf16[32,2,640]{2,1,0:T(2,128)(2,1)S(1)} async-done(((bf16[32,2,640]{2,1,0:T(2,128)(2,1)}), bf16[32,2,640]{2,1,0:T(2,128)(2,1)S(1)}, u32[]{:S(2)}, u32[]{:S(2)}) %all-to-all-start.1) | async-done | bytes 81952 | tf_op jit(solution)/shard_map/all_to_all | solution.py:381
  36.0 0.0 collective-permute-done.2.from_chip_ref
  36.0 0.0 collective-permute-done.3.from_core_ref
  36.0 1.5 %edge1.1 = (bf16[256,640]{1,0:T(8,128)(2,1)S(1)}, bf16[256,640]{1,0:T(8,128)(2,1)S(1)}, bf16[32,2,640]{2,1,0:T(2,128)(2,1)}, bf16[576,640]{1,0:T(8,128)(2,1)}) custom-call(bf16[528,640]{1,0:T(8,128)(2,1)S(1)} %get-tuple-element.39.own_ref, bf16[528,576]{1,0:T(8,128)(2,1)S(1)} %get-tuple-element.32.mixed_ref, ...), custom_call_target="tpu_custom_call", output_to_operand_aliasing={{0}: (3, {}), {1}: (4, {})} | custom-call | flops 754974720 | tf_op jit(solution)/shard_map/edge1/pallas_call | solution.py:346
  37.6 0.7 %collective-permute-start.4 = (bf16[256,640]{1,0:T(8,128)(2,1)S(1)}, bf16[256,640]{1,0:T(8,128)(2,1)S(1)}, u32[]{:S(2)}, u32[]{:S(2)}) collective-permute-start(bf16[256,640]{1,0:T(8,128)(2,1)S(1)} %get-tuple-element.49), channel_id=1, source_target_pairs={{1,2},{2,1},{3,4},{4,3},{5,6},{6,5},{7,8},{8,7},{9,10},{10,9},{11,... | collective-permute-start | bytes 983048 | tf_op jit(solution)/shard_map/ppermute | solution.py:379
  38.3 1.8 %collective-permute-start.5 = (bf16[256,640]{1,0:T(8,128)(2,1)S(1)}, bf16[256,640]{1,0:T(8,128)(2,1)S(1)}, u32[]{:S(2)}, u32[]{:S(2)}) collective-permute-start(bf16[256,640]{1,0:T(8,128)(2,1)S(1)} %get-tuple-element.50), channel_id=1, source_target_pairs={{0,1},{1,0},{2,3},{3,2},{4,5},{5,4},{6,7},{7,6},{8,9},{9,8},{10,11... | collective-permute-start | bytes 983048 | tf_op jit(solution)/shard_map/ppermute | solution.py:380
  40.1 4.3 %all-to-all-start.2 = ((bf16[32,2,640]{2,1,0:T(2,128)(2,1)}), bf16[32,2,640]{2,1,0:T(2,128)(2,1)S(1)}, u32[]{:S(2)}, u32[]{:S(2)}) async-start(bf16[32,2,640]{2,1,0:T(2,128)(2,1)} %get-tuple-element.51), calls=%async_computation.2 | async-start | bytes 163840 | tf_op jit(solution)/shard_map/all_to_all | solution.py:381
  44.4 5.6 %bulk2.1 = (bf16[3,1024,512]{2,1,0:T(8,128)(2,1)}, bf16[3,1024,128]{2,1,0:T(8,128)(2,1)}, bf16[1024,640]{1,0:T(8,128)(2,1)}, bf16[1024,576]{1,0:T(8,128)(2,1)S(1)}, f32[1024,128]{1,0:T(8,128)S(1)}) custom-call(s32[1,2,2]{2,1,0:T(2,128)} %refs_0_.5, s32[1,2]{1,0:T(1,128)} %refs_1_.5, s32[2]{0:T(128)} %refs_2_.5, ...), custom_call_target="tpu_custom_call", output_to_operand_aliasing={{0}: (9, {}), {1}: (10, {})} | custom-call | flops 1342177280 | tf_op jit(solution)/shard_map/bulk2/pallas_call | solution.py:346
  50.0 1.8 %all-to-all-done.2 = bf16[32,2,640]{2,1,0:T(2,128)(2,1)S(1)} async-done(((bf16[32,2,640]{2,1,0:T(2,128)(2,1)}), bf16[32,2,640]{2,1,0:T(2,128)(2,1)S(1)}, u32[]{:S(2)}, u32[]{:S(2)}) %all-to-all-start.2) | async-done | bytes 81952 | tf_op jit(solution)/shard_map/all_to_all | solution.py:381
  51.8 0.0 collective-permute-done.4.from_chip_ref
  51.8 0.0 collective-permute-done.5.from_core_ref
  51.8 3.0 %final.1 = (bf16[3,1024,512]{2,1,0:T(8,128)(2,1)}, bf16[3,1024,128]{2,1,0:T(8,128)(2,1)}) custom-call(bf16[1024,640]{1,0:T(8,128)(2,1)} %get-tuple-element.46.own_hbm, bf16[1024,576]{1,0:T(8,128)(2,1)S(1)} %get-tuple-element.47.mixed_ref, f32[1024,128]{1,0:T(8,128)S(1)} %get-tuple-element.48.dmat_ref, ...), custom_call_target="tpu_custom_call", output_to_operand_aliasing={{0}: (6, {}), {1}: (7, {})} | custom-call | flops 754974720 | tf_op jit(solution)/shard_map/final/pallas_call | solution.py:346
  (3 shorter events, 0.1 us)
Async XLA Ops:
  2.7 17.6 %collective-permute-start = (bf16[256,640]{1,0:T(8,128)(2,1)S(1)}, bf16[256,640]{1,0:T(8,128)(2,1)S(1)}, u32[]{:S(2)}, u32[]{:S(2)}) collective-permute-start(bf16[256,640]{1,0:T(8,128)(2,1)S(1)} %get-tuple-element.34), channel_id=1, source_target_pairs={{1,2},{2,1},{3,4},{4,3},{5,6},{6,5},{7,8},{8,7},{9,10},{10,9},{11,... | collective-permute-start | bytes 983048 | tf_op jit(solution)/shard_map/ppermute | solution.py:379
  3.4 16.9 %collective-permute-start.1 = (bf16[256,640]{1,0:T(8,128)(2,1)S(1)}, bf16[256,640]{1,0:T(8,128)(2,1)S(1)}, u32[]{:S(2)}, u32[]{:S(2)}) collective-permute-start(bf16[256,640]{1,0:T(8,128)(2,1)S(1)} %get-tuple-element.35), channel_id=1, source_target_pairs={{0,1},{1,0},{2,3},{3,2},{4,5},{5,4},{6,7},{7,6},{8,9},{9,8},{10,11... | collective-permute-start | bytes 983048 | tf_op jit(solution)/shard_map/ppermute | solution.py:380
  7.8 12.5 %all-to-all-start = ((bf16[32,2,640]{2,1,0:T(2,128)(2,1)}), bf16[32,2,640]{2,1,0:T(2,128)(2,1)S(1)}, u32[]{:S(2)}, u32[]{:S(2)}) async-start(bf16[32,2,640]{2,1,0:T(2,128)(2,1)} %get-tuple-element.36), calls=%async_computation | async-start | bytes 163840 | tf_op jit(solution)/shard_map/all_to_all | solution.py:381
  21.9 14.1 %collective-permute-start.2 = (bf16[256,640]{1,0:T(8,128)(2,1)S(1)}, bf16[256,640]{1,0:T(8,128)(2,1)S(1)}, u32[]{:S(2)}, u32[]{:S(2)}) collective-permute-start(bf16[256,640]{1,0:T(8,128)(2,1)S(1)} %get-tuple-element.40), channel_id=1, source_target_pairs={{1,2},{2,1},{3,4},{4,3},{5,6},{6,5},{7,8},{8,7},{9,10},{10,9},{11,... | collective-permute-start | bytes 983048 | tf_op jit(solution)/shard_map/ppermute | solution.py:379
  22.6 13.4 %collective-permute-start.3 = (bf16[256,640]{1,0:T(8,128)(2,1)S(1)}, bf16[256,640]{1,0:T(8,128)(2,1)S(1)}, u32[]{:S(2)}, u32[]{:S(2)}) collective-permute-start(bf16[256,640]{1,0:T(8,128)(2,1)S(1)} %get-tuple-element.41), channel_id=1, source_target_pairs={{0,1},{1,0},{2,3},{3,2},{4,5},{5,4},{6,7},{7,6},{8,9},{9,8},{10,11... | collective-permute-start | bytes 983048 | tf_op jit(solution)/shard_map/ppermute | solution.py:380
  24.4 11.6 %all-to-all-start.1 = ((bf16[32,2,640]{2,1,0:T(2,128)(2,1)}), bf16[32,2,640]{2,1,0:T(2,128)(2,1)S(1)}, u32[]{:S(2)}, u32[]{:S(2)}) async-start(bf16[32,2,640]{2,1,0:T(2,128)(2,1)} %get-tuple-element.42), calls=%async_computation.1 | async-start | bytes 163840 | tf_op jit(solution)/shard_map/all_to_all | solution.py:381
  37.6 14.3 %collective-permute-start.4 = (bf16[256,640]{1,0:T(8,128)(2,1)S(1)}, bf16[256,640]{1,0:T(8,128)(2,1)S(1)}, u32[]{:S(2)}, u32[]{:S(2)}) collective-permute-start(bf16[256,640]{1,0:T(8,128)(2,1)S(1)} %get-tuple-element.49), channel_id=1, source_target_pairs={{1,2},{2,1},{3,4},{4,3},{5,6},{6,5},{7,8},{8,7},{9,10},{10,9},{11,... | collective-permute-start | bytes 983048 | tf_op jit(solution)/shard_map/ppermute | solution.py:379
  38.3 13.6 %collective-permute-start.5 = (bf16[256,640]{1,0:T(8,128)(2,1)S(1)}, bf16[256,640]{1,0:T(8,128)(2,1)S(1)}, u32[]{:S(2)}, u32[]{:S(2)}) collective-permute-start(bf16[256,640]{1,0:T(8,128)(2,1)S(1)} %get-tuple-element.50), channel_id=1, source_target_pairs={{0,1},{1,0},{2,3},{3,2},{4,5},{5,4},{6,7},{7,6},{8,9},{9,8},{10,11... | collective-permute-start | bytes 983048 | tf_op jit(solution)/shard_map/ppermute | solution.py:380
  40.1 11.7 %all-to-all-start.2 = ((bf16[32,2,640]{2,1,0:T(2,128)(2,1)}), bf16[32,2,640]{2,1,0:T(2,128)(2,1)S(1)}, u32[]{:S(2)}, u32[]{:S(2)}) async-start(bf16[32,2,640]{2,1,0:T(2,128)(2,1)} %get-tuple-element.51), calls=%async_computation.2 | async-start | bytes 163840 | tf_op jit(solution)/shard_map/all_to_all | solution.py:381

commit v5 on v4

--- a/solution.py
+++ b/solution.py
@@ -178,7 +178,7 @@
     if first:
         degree_ref, weight_ref, sems = refs
     else:
-        received, old_own_ref, total_ref, sems = refs
+        received, old_own_ref, sems = refs
     copies = Copies(sems)
     blocks, _, tile, _ = tiles_ref.shape
     row_count, width = z_ref.shape
@@ -199,19 +199,19 @@
             z_ref[rows, :split] = scale_rows(features_ref[rows, :].astype(F32), dmat).astype(BF16)
             z_ref[rows, split:] = scale_rows(embeddings_ref[rows, :].astype(F32), dmat).astype(BF16)
     else:
-        parts = quarters(row_count)
-        finish_first = copies.start((received_hbm, received))
-        mixes = [copies.start((mixed_hbm.at[rows, :], mixed_ref.at[rows, :])) for rows in parts]
-        rest = copies.start((dmat_hbm, dmat_ref), (old_own_hbm, old_own_ref))
+        inputs = copies.start((received_hbm, received), (dmat_hbm, dmat_ref))
+        parts = [
+            copies.start((mixed_hbm.at[rows, :], mixed_ref.at[rows, :]), (old_own_hbm.at[rows, :], old_own_ref.at[rows, :]))
+            for rows in quarters(row_count)
+        ]
         late = copies.start((tiles_hbm, tiles_ref))
-        finish(finish_first)
-        for rows, mix in zip(parts, mixes):
-            finish(mix)
-            total_ref[rows, :] = jnp.dot(mixed_ref[rows, :], received[...], preferred_element_type=F32)
-        finish(rest)
-        for rows in every:
+        finish(inputs)
+        for b, rows in enumerate(every):
+            if b * len(parts) % blocks == 0:
+                finish(parts[b * len(parts) // blocks])
+            total = jnp.dot(mixed_ref[rows, :], received[...], preferred_element_type=F32)
             dmat = dmat_ref[rows, :]
-            fresh = scale_rows(old_own_ref[rows, :].astype(F32) + total_ref[rows, :], dmat).astype(BF16)
+            fresh = scale_rows(old_own_ref[rows, :].astype(F32) + total, dmat).astype(BF16)
             features_ref[rows, :] = fresh[:, :split]
             embeddings_ref[rows, :] = fresh[:, split:]
             z_ref[rows, :] = scale_rows(fresh.astype(F32), dmat).astype(BF16)
@@ -253,21 +253,20 @@
 def edge_kernel(
     own_ref, mixed_ref, roots_ref, from_chip_ref, from_core_ref, gathered_ref,
     chip_ref, core_ref, spread_hbm, received_hbm,
-    total_ref, received, spread_ref, sems,
+    received, spread_ref, sems,
 ):
     copies = Copies(sems)
     rim_rows = chip_ref.shape[0]
     hub_dev = spread_ref.shape[1]
     place_received(from_chip_ref, from_core_ref, gathered_ref, received)
     writes = copies.start((received, received_hbm))
-    total_ref[...] = jnp.dot(mixed_ref[...], received[...], preferred_element_type=F32)
-
     tile = roots_ref.shape[1]
 
     def fresh(part):
-        rows = slice(part * tile, min((part + 1) * tile, total_ref.shape[0]))
+        rows = slice(part * tile, min((part + 1) * tile, own_ref.shape[0]))
+        total = jnp.dot(mixed_ref[rows, :], received[...], preferred_element_type=F32)
         dmat = lane_to_rows(roots_ref[part : part + 1, :])[: rows.stop - rows.start]
-        kept = scale_rows(own_ref[rows, :].astype(F32) + total_ref[rows, :], dmat).astype(BF16)
+        kept = scale_rows(own_ref[rows, :].astype(F32) + total, dmat).astype(BF16)
         return scale_rows(kept.astype(F32), dmat).astype(BF16)
 
     send_most = rim_rows // tile
@@ -289,29 +288,25 @@
     row_count = own_ref.shape[0]
     reads = copies.start((own_hbm, own_ref))
     place_received(from_chip_ref, from_core_ref, gathered_ref, received)
-    parts = quarters(row_count)
-
-    def multiply(rows):
+    tile = dmat_ref.shape[1]
+    parts = [slice(at, at + tile) for at in range(0, row_count, tile)]
+    ahead = len(parts) // 2
+    for rows in parts[:ahead]:
         total_ref[rows, :] = jnp.dot(mixed_ref[rows, :], received[...], preferred_element_type=F32)
-
-    def store(rows):
-        fresh = scale_rows(own_ref[rows, :].astype(F32) + total_ref[rows, :], dmat_ref[rows, :]).astype(BF16)
+    finish(reads)
+    writes = []
+    for i, rows in enumerate(parts):
+        if i < ahead:
+            total = total_ref[rows, :]
+        else:
+            total = jnp.dot(mixed_ref[rows, :], received[...], preferred_element_type=F32)
+        fresh = scale_rows(own_ref[rows, :].astype(F32) + total, dmat_ref[rows, :]).astype(BF16)
         features_ref[rows, :] = fresh[:, :split]
         embeddings_ref[rows, :] = fresh[:, split:]
-        return copies.start(
+        writes += copies.start(
             (features_ref.at[rows, :], all_features.at[HOPS - 1, rows, :]),
             (embeddings_ref.at[rows, :], all_embeddings.at[HOPS - 1, rows, :]),
         )
-
-    multiply(parts[0])
-    multiply(parts[1])
-    finish(reads)
-    writes = store(parts[0])
-    multiply(parts[2])
-    writes += store(parts[1])
-    multiply(parts[3])
-    writes += store(parts[2])
-    writes += store(parts[3])
     finish(writes)
 
 
@@ -401,10 +396,10 @@
                 operands += pin(*out)
             out_shape = whole + [full_own]
             out_shape += [shape((row_count, deep), BF16), shape((row_count, tile), F32)] if last else sent_shapes[:1]
-            scratch += [VMEM((deep, width), BF16), VMEM((row_count, width), BF16), VMEM((row_count, width), F32)]
+            scratch += [VMEM((deep, width), BF16), VMEM((row_count, width), BF16)]
         got = call(
             functools.partial(bulk_kernel, hop=hop, rim=rim, per_block=per_block), f"bulk{hop}",
-            4 * row_count * per_block * tile * width, out_shape, scratch, 16 + blocks,
+            4 * row_count * per_block * tile * width, out_shape, scratch, 20 + blocks,
             len(operands), operands, aliases,
         )
         if first:
@@ -423,13 +418,13 @@
             out = call(
                 final_kernel, "final", flops, whole,
                 [VMEM((row_count, width), BF16), VMEM((row_count, width), F32)] + row_buffers
-                + [VMEM((deep, width), BF16)], 9,
+                + [VMEM((deep, width), BF16)], 1 + 2 * blocks,
                 1, operands + pin(*out), aliases,
             )
         else:
             to_chip, to_core, spread, received = call(
                 edge_kernel, f"edge{hop}", flops, sends + [pltpu.HBM((deep, width), BF16)],
-                [VMEM((sent, width), F32), VMEM((deep, width), BF16), spread_buffer], 2,
+                [VMEM((deep, width), BF16), spread_buffer], 2,
                 0, [own_sent, mixed_sent, roots_sent, from_chip, from_core, gathered],
                 {3: 0, 4: 1},
             )

time: 55.4 us -> 54.4 us (0.982)
  Pallas kernels: 25 us -> 23.8 us
    pallas_call x7, Pallas kernels: 25 us -> 23.8 us  [call(): pl.pallas_call(kernel, name=name, out_shape=out_shape, in_specs=specs, ou...]
where the time goes in v5:
time: 54.4 us; the launch traced here: 54 us
  Pallas kernels  23.8 us (44%)
  starting transfers between devices  23.1 us (42%)
  waiting for transfers between devices  6.04 us (11%)
  between operations  0.94 us (2%)
    pallas_call x7, Pallas kernels, call(): pl.pallas_call(kernel, name=name, out_shape=out_shape, in_specs=specs, ou...  23.8 us
    all_to_all x3, starting transfers between devices, body(): gathered = lax.all_to_all(spread, 'dom', 0, 0).reshape(hub_total, width)  13.1 us
    ppermute x3, starting transfers between devices, body(): from_core = lax.ppermute(to_core, 'dom', core_pairs)  7.99 us
    all_to_all x3, waiting for transfers between devices, body(): gathered = lax.all_to_all(spread, 'dom', 0, 0).reshape(hub_total, width)  6.02 us
    ppermute x3, starting transfers between devices, body(): from_chip = lax.ppermute(to_chip, 'dom', chip_pairs)  2.04 us
  transfers between devices with their start and end apart: 9, of which 3 were waited for; matrix products, arithmetic and copies ran while one was open for 0% of the time, Pallas kernels for 31%

profile of v5, /device:TPU:0, one launch (start us, length us, event | category | flops | bytes accessed | tf_op | source)
XLA Modules:
  0.0 54.0 jit_solution(13833906673654476000)
XLA Ops:
  0.6 2.1 %prologue.1 = (bf16[256,640]{1,0:T(8,128)(2,1)S(1)}, bf16[256,640]{1,0:T(8,128)(2,1)S(1)}, bf16[32,2,640]{2,1,0:T(2,128)(2,1)}) custom-call(s32[1,2,2]{2,1,0:T(2,128)} %refs_0_.5, s32[1,2]{1,0:T(1,128)} %refs_1_.5, s32[2]{0:T(128)} %refs_2_.5, s32[8,128]{1,0:T(8,128)} %bitcast.3, bf16[1024,512]{1,0:T(8,128)(2,1)} %features_hbm.1, ...), custom_call_target="tpu_custom_call" | custom-call | flops 100000000 | tf_op jit(solution)/shard_map/prologue/pallas_call | solution.py:341
  2.7 0.7 %collective-permute-start = (bf16[256,640]{1,0:T(8,128)(2,1)S(1)}, bf16[256,640]{1,0:T(8,128)(2,1)S(1)}, u32[]{:S(2)}, u32[]{:S(2)}) collective-permute-start(bf16[256,640]{1,0:T(8,128)(2,1)S(1)} %get-tuple-element.34), channel_id=1, source_target_pairs={{1,2},{2,1},{3,4},{4,3},{5,6},{6,5},{7,8},{8,7},{9,10},{10,9},{11,... | collective-permute-start | bytes 983048 | tf_op jit(solution)/shard_map/ppermute | solution.py:374
  3.4 4.4 %collective-permute-start.1 = (bf16[256,640]{1,0:T(8,128)(2,1)S(1)}, bf16[256,640]{1,0:T(8,128)(2,1)S(1)}, u32[]{:S(2)}, u32[]{:S(2)}) collective-permute-start(bf16[256,640]{1,0:T(8,128)(2,1)S(1)} %get-tuple-element.35), channel_id=1, source_target_pairs={{0,1},{1,0},{2,3},{3,2},{4,5},{5,4},{6,7},{7,6},{8,9},{9,8},{10,11... | collective-permute-start | bytes 983048 | tf_op jit(solution)/shard_map/ppermute | solution.py:375
  7.8 4.9 %all-to-all-start = ((bf16[32,2,640]{2,1,0:T(2,128)(2,1)}), bf16[32,2,640]{2,1,0:T(2,128)(2,1)S(1)}, u32[]{:S(2)}, u32[]{:S(2)}) async-start(bf16[32,2,640]{2,1,0:T(2,128)(2,1)} %get-tuple-element.36), calls=%async_computation | async-start | bytes 163840 | tf_op jit(solution)/shard_map/all_to_all | solution.py:376
  12.7 5.6 %bulk0.1 = (bf16[1024,640]{1,0:T(8,128)(2,1)}, bf16[528,640]{1,0:T(8,128)(2,1)S(1)}, bf16[1024,576]{1,0:T(8,128)(2,1)}, f32[1024,128]{1,0:T(8,128)}, bf16[528,576]{1,0:T(8,128)(2,1)S(1)}, /*index=5*/f32[5,128]{1,0:T(8,128)S(1)}) custom-call(s32[1,2,2]{2,1,0:T(2,128)} %refs_0_.5, s32[1,2]{1,0:T(1,128)} %refs_1_.5, s32[2]{0:T(128)} %refs_2_.5, ...), custom_call_target="tpu_custom_call" | custom-call | flops 1342177280 | tf_op jit(solution)/shard_map/bulk0/pallas_call | solution.py:341
  18.3 2.0 %all-to-all-done = bf16[32,2,640]{2,1,0:T(2,128)(2,1)S(1)} async-done(((bf16[32,2,640]{2,1,0:T(2,128)(2,1)}), bf16[32,2,640]{2,1,0:T(2,128)(2,1)S(1)}, u32[]{:S(2)}, u32[]{:S(2)}) %all-to-all-start) | async-done | bytes 81952 | tf_op jit(solution)/shard_map/all_to_all | solution.py:376
  20.3 0.0 collective-permute-done.from_chip_ref
  20.4 0.0 collective-permute-done.1.from_core_ref
  20.4 1.1 %edge0.1 = (bf16[256,640]{1,0:T(8,128)(2,1)S(1)}, bf16[256,640]{1,0:T(8,128)(2,1)S(1)}, bf16[32,2,640]{2,1,0:T(2,128)(2,1)}, bf16[576,640]{1,0:T(8,128)(2,1)}) custom-call(bf16[528,640]{1,0:T(8,128)(2,1)S(1)} %get-tuple-element.31.own_ref, bf16[528,576]{1,0:T(8,128)(2,1)S(1)} %get-tuple-element.32.mixed_ref, ...), custom_call_target="tpu_custom_call", output_to_operand_aliasing={{0}: (3, {}), {1}: (4, {})} | custom-call | flops 754974720 | tf_op jit(solution)/shard_map/edge0/pallas_call | solution.py:341
  21.4 0.7 %collective-permute-start.2 = (bf16[256,640]{1,0:T(8,128)(2,1)S(1)}, bf16[256,640]{1,0:T(8,128)(2,1)S(1)}, u32[]{:S(2)}, u32[]{:S(2)}) collective-permute-start(bf16[256,640]{1,0:T(8,128)(2,1)S(1)} %get-tuple-element.40), channel_id=1, source_target_pairs={{1,2},{2,1},{3,4},{4,3},{5,6},{6,5},{7,8},{8,7},{9,10},{10,9},{11,... | collective-permute-start | bytes 983048 | tf_op jit(solution)/shard_map/ppermute | solution.py:374
  22.1 1.8 %collective-permute-start.3 = (bf16[256,640]{1,0:T(8,128)(2,1)S(1)}, bf16[256,640]{1,0:T(8,128)(2,1)S(1)}, u32[]{:S(2)}, u32[]{:S(2)}) collective-permute-start(bf16[256,640]{1,0:T(8,128)(2,1)S(1)} %get-tuple-element.41), channel_id=1, source_target_pairs={{0,1},{1,0},{2,3},{3,2},{4,5},{5,4},{6,7},{7,6},{8,9},{9,8},{10,11... | collective-permute-start | bytes 983048 | tf_op jit(solution)/shard_map/ppermute | solution.py:375
  23.9 4.0 %all-to-all-start.1 = ((bf16[32,2,640]{2,1,0:T(2,128)(2,1)}), bf16[32,2,640]{2,1,0:T(2,128)(2,1)S(1)}, u32[]{:S(2)}, u32[]{:S(2)}) async-start(bf16[32,2,640]{2,1,0:T(2,128)(2,1)} %get-tuple-element.42), calls=%async_computation.1 | async-start | bytes 163840 | tf_op jit(solution)/shard_map/all_to_all | solution.py:376
  28.0 5.5 %bulk1.1 = (bf16[3,1024,512]{2,1,0:T(8,128)(2,1)}, bf16[3,1024,128]{2,1,0:T(8,128)(2,1)}, bf16[1024,640]{1,0:T(8,128)(2,1)}, bf16[528,640]{1,0:T(8,128)(2,1)S(1)}) custom-call(s32[1,2,2]{2,1,0:T(2,128)} %refs_0_.5, s32[1,2]{1,0:T(1,128)} %refs_1_.5, s32[2]{0:T(128)} %refs_2_.5, s32[4,8]{1,0:T(4,128)} %bitcast.6, bf16[8,4,128,128]{3,2,1,0:T(8,128)(2,1)} %refs_4_.5, ...), custom_call_target="tpu_custom_call" | custom-call | flops 1342177280 | tf_op jit(solution)/shard_map/bulk1/pallas_call | solution.py:341
  33.5 2.1 %all-to-all-done.1 = bf16[32,2,640]{2,1,0:T(2,128)(2,1)S(1)} async-done(((bf16[32,2,640]{2,1,0:T(2,128)(2,1)}), bf16[32,2,640]{2,1,0:T(2,128)(2,1)S(1)}, u32[]{:S(2)}, u32[]{:S(2)}) %all-to-all-start.1) | async-done | bytes 81952 | tf_op jit(solution)/shard_map/all_to_all | solution.py:376
  35.6 0.0 collective-permute-done.2.from_chip_ref
  35.6 0.0 collective-permute-done.3.from_core_ref
  35.6 1.1 %edge1.1 = (bf16[256,640]{1,0:T(8,128)(2,1)S(1)}, bf16[256,640]{1,0:T(8,128)(2,1)S(1)}, bf16[32,2,640]{2,1,0:T(2,128)(2,1)}, bf16[576,640]{1,0:T(8,128)(2,1)}) custom-call(bf16[528,640]{1,0:T(8,128)(2,1)S(1)} %get-tuple-element.39.own_ref, bf16[528,576]{1,0:T(8,128)(2,1)S(1)} %get-tuple-element.32.mixed_ref, ...), custom_call_target="tpu_custom_call", output_to_operand_aliasing={{0}: (3, {}), {1}: (4, {})} | custom-call | flops 754974720 | tf_op jit(solution)/shard_map/edge1/pallas_call | solution.py:341
  36.7 0.7 %collective-permute-start.4 = (bf16[256,640]{1,0:T(8,128)(2,1)S(1)}, bf16[256,640]{1,0:T(8,128)(2,1)S(1)}, u32[]{:S(2)}, u32[]{:S(2)}) collective-permute-start(bf16[256,640]{1,0:T(8,128)(2,1)S(1)} %get-tuple-element.49), channel_id=1, source_target_pairs={{1,2},{2,1},{3,4},{4,3},{5,6},{6,5},{7,8},{8,7},{9,10},{10,9},{11,... | collective-permute-start | bytes 983048 | tf_op jit(solution)/shard_map/ppermute | solution.py:374
  37.4 1.8 %collective-permute-start.5 = (bf16[256,640]{1,0:T(8,128)(2,1)S(1)}, bf16[256,640]{1,0:T(8,128)(2,1)S(1)}, u32[]{:S(2)}, u32[]{:S(2)}) collective-permute-start(bf16[256,640]{1,0:T(8,128)(2,1)S(1)} %get-tuple-element.50), channel_id=1, source_target_pairs={{0,1},{1,0},{2,3},{3,2},{4,5},{5,4},{6,7},{7,6},{8,9},{9,8},{10,11... | collective-permute-start | bytes 983048 | tf_op jit(solution)/shard_map/ppermute | solution.py:375
  39.2 4.1 %all-to-all-start.2 = ((bf16[32,2,640]{2,1,0:T(2,128)(2,1)}), bf16[32,2,640]{2,1,0:T(2,128)(2,1)S(1)}, u32[]{:S(2)}, u32[]{:S(2)}) async-start(bf16[32,2,640]{2,1,0:T(2,128)(2,1)} %get-tuple-element.51), calls=%async_computation.2 | async-start | bytes 163840 | tf_op jit(solution)/shard_map/all_to_all | solution.py:376
  43.3 5.4 %bulk2.1 = (bf16[3,1024,512]{2,1,0:T(8,128)(2,1)}, bf16[3,1024,128]{2,1,0:T(8,128)(2,1)}, bf16[1024,640]{1,0:T(8,128)(2,1)}, bf16[1024,576]{1,0:T(8,128)(2,1)S(1)}, f32[1024,128]{1,0:T(8,128)S(1)}) custom-call(s32[1,2,2]{2,1,0:T(2,128)} %refs_0_.5, s32[1,2]{1,0:T(1,128)} %refs_1_.5, s32[2]{0:T(128)} %refs_2_.5, ...), custom_call_target="tpu_custom_call", output_to_operand_aliasing={{0}: (9, {}), {1}: (10, {})} | custom-call | flops 1342177280 | tf_op jit(solution)/shard_map/bulk2/pallas_call | solution.py:341
  48.8 2.0 %all-to-all-done.2 = bf16[32,2,640]{2,1,0:T(2,128)(2,1)S(1)} async-done(((bf16[32,2,640]{2,1,0:T(2,128)(2,1)}), bf16[32,2,640]{2,1,0:T(2,128)(2,1)S(1)}, u32[]{:S(2)}, u32[]{:S(2)}) %all-to-all-start.2) | async-done | bytes 81952 | tf_op jit(solution)/shard_map/all_to_all | solution.py:376
  50.8 0.0 collective-permute-done.4.from_chip_ref
  50.8 0.0 collective-permute-done.5.from_core_ref
  50.8 3.0 %final.1 = (bf16[3,1024,512]{2,1,0:T(8,128)(2,1)}, bf16[3,1024,128]{2,1,0:T(8,128)(2,1)}) custom-call(bf16[1024,640]{1,0:T(8,128)(2,1)} %get-tuple-element.46.own_hbm, bf16[1024,576]{1,0:T(8,128)(2,1)S(1)} %get-tuple-element.47.mixed_ref, f32[1024,128]{1,0:T(8,128)S(1)} %get-tuple-element.48.dmat_ref, ...), custom_call_target="tpu_custom_call", output_to_operand_aliasing={{0}: (6, {}), {1}: (7, {})} | custom-call | flops 754974720 | tf_op jit(solution)/shard_map/final/pallas_call | solution.py:341
  (3 shorter events, 0.1 us)
Async XLA Ops:
  2.7 17.6 %collective-permute-start = (bf16[256,640]{1,0:T(8,128)(2,1)S(1)}, bf16[256,640]{1,0:T(8,128)(2,1)S(1)}, u32[]{:S(2)}, u32[]{:S(2)}) collective-permute-start(bf16[256,640]{1,0:T(8,128)(2,1)S(1)} %get-tuple-element.34), channel_id=1, source_target_pairs={{1,2},{2,1},{3,4},{4,3},{5,6},{6,5},{7,8},{8,7},{9,10},{10,9},{11,... | collective-permute-start | bytes 983048 | tf_op jit(solution)/shard_map/ppermute | solution.py:374
  3.4 16.9 %collective-permute-start.1 = (bf16[256,640]{1,0:T(8,128)(2,1)S(1)}, bf16[256,640]{1,0:T(8,128)(2,1)S(1)}, u32[]{:S(2)}, u32[]{:S(2)}) collective-permute-start(bf16[256,640]{1,0:T(8,128)(2,1)S(1)} %get-tuple-element.35), channel_id=1, source_target_pairs={{0,1},{1,0},{2,3},{3,2},{4,5},{5,4},{6,7},{7,6},{8,9},{9,8},{10,11... | collective-permute-start | bytes 983048 | tf_op jit(solution)/shard_map/ppermute | solution.py:375
  7.8 12.5 %all-to-all-start = ((bf16[32,2,640]{2,1,0:T(2,128)(2,1)}), bf16[32,2,640]{2,1,0:T(2,128)(2,1)S(1)}, u32[]{:S(2)}, u32[]{:S(2)}) async-start(bf16[32,2,640]{2,1,0:T(2,128)(2,1)} %get-tuple-element.36), calls=%async_computation | async-start | bytes 163840 | tf_op jit(solution)/shard_map/all_to_all | solution.py:376
  21.4 14.2 %collective-permute-start.2 = (bf16[256,640]{1,0:T(8,128)(2,1)S(1)}, bf16[256,640]{1,0:T(8,128)(2,1)S(1)}, u32[]{:S(2)}, u32[]{:S(2)}) collective-permute-start(bf16[256,640]{1,0:T(8,128)(2,1)S(1)} %get-tuple-element.40), channel_id=1, source_target_pairs={{1,2},{2,1},{3,4},{4,3},{5,6},{6,5},{7,8},{8,7},{9,10},{10,9},{11,... | collective-permute-start | bytes 983048 | tf_op jit(solution)/shard_map/ppermute | solution.py:374
  22.1 13.5 %collective-permute-start.3 = (bf16[256,640]{1,0:T(8,128)(2,1)S(1)}, bf16[256,640]{1,0:T(8,128)(2,1)S(1)}, u32[]{:S(2)}, u32[]{:S(2)}) collective-permute-start(bf16[256,640]{1,0:T(8,128)(2,1)S(1)} %get-tuple-element.41), channel_id=1, source_target_pairs={{0,1},{1,0},{2,3},{3,2},{4,5},{5,4},{6,7},{7,6},{8,9},{9,8},{10,11... | collective-permute-start | bytes 983048 | tf_op jit(solution)/shard_map/ppermute | solution.py:375
  23.9 11.6 %all-to-all-start.1 = ((bf16[32,2,640]{2,1,0:T(2,128)(2,1)}), bf16[32,2,640]{2,1,0:T(2,128)(2,1)S(1)}, u32[]{:S(2)}, u32[]{:S(2)}) async-start(bf16[32,2,640]{2,1,0:T(2,128)(2,1)} %get-tuple-element.42), calls=%async_computation.1 | async-start | bytes 163840 | tf_op jit(solution)/shard_map/all_to_all | solution.py:376
  36.7 14.1 %collective-permute-start.4 = (bf16[256,640]{1,0:T(8,128)(2,1)S(1)}, bf16[256,640]{1,0:T(8,128)(2,1)S(1)}, u32[]{:S(2)}, u32[]{:S(2)}) collective-permute-start(bf16[256,640]{1,0:T(8,128)(2,1)S(1)} %get-tuple-element.49), channel_id=1, source_target_pairs={{1,2},{2,1},{3,4},{4,3},{5,6},{6,5},{7,8},{8,7},{9,10},{10,9},{11,... | collective-permute-start | bytes 983048 | tf_op jit(solution)/shard_map/ppermute | solution.py:374
  37.4 13.4 %collective-permute-start.5 = (bf16[256,640]{1,0:T(8,128)(2,1)S(1)}, bf16[256,640]{1,0:T(8,128)(2,1)S(1)}, u32[]{:S(2)}, u32[]{:S(2)}) collective-permute-start(bf16[256,640]{1,0:T(8,128)(2,1)S(1)} %get-tuple-element.50), channel_id=1, source_target_pairs={{0,1},{1,0},{2,3},{3,2},{4,5},{5,4},{6,7},{7,6},{8,9},{9,8},{10,11... | collective-permute-start | bytes 983048 | tf_op jit(solution)/shard_map/ppermute | solution.py:375
  39.2 11.5 %all-to-all-start.2 = ((bf16[32,2,640]{2,1,0:T(2,128)(2,1)}), bf16[32,2,640]{2,1,0:T(2,128)(2,1)S(1)}, u32[]{:S(2)}, u32[]{:S(2)}) async-start(bf16[32,2,640]{2,1,0:T(2,128)(2,1)} %get-tuple-element.51), calls=%async_computation.2 | async-start | bytes 163840 | tf_op jit(solution)/shard_map/all_to_all | solution.py:376

commit v6 on v5

--- a/solution.py
+++ b/solution.py
@@ -89,11 +89,13 @@
 
 
 def slots(blocks_ref, count_ref):
-    parity = lax.axis_index("dom") % 2
+    index = lax.axis_index("dom")
+    parity = index % 2
     send_most = blocks_ref.shape[2]
+    inner = jnp.logical_and(index > 0, index < lax.axis_size("dom") - 1)
     return [
-        (blocks_ref[0, side, slot], slot < count_ref[0, side])
-        for side in (parity, 1 - parity)
+        (blocks_ref[0, side, slot], jnp.logical_and(slot < count_ref[0, side], real))
+        for side, real in ((parity, inner), (1 - parity, True))
         for slot in range(send_most)
     ]
 
@@ -366,7 +368,7 @@
     )
 
     core_pairs = [(i, i ^ 1) for i in range(count) if i ^ 1 < count]
-    chip_pairs = [p for i in range(1, count - 1, 2) for p in ((i, i + 1), (i + 1, i))]
+    chip_pairs = [p for i in range(1, count, 2) for p in ((i, (i + 1) % count), ((i + 1) % count, i))]
     fixed = lists + pin(tile_columns.T, tile_values)
     out = []
     for hop in range(HOPS):

time: 54.4 us -> 52.8 us (0.971)
  starting transfers between devices: 23.1 us -> 21.6 us
    ppermute x3, starting transfers between devices: 2.04 us -> 13 us  [body(): from_chip = lax.ppermute(to_chip, 'dom', chip_pairs)]
    ppermute x3, starting transfers between devices: 7.99 us -> 0.01 us  [body(): from_core = lax.ppermute(to_core, 'dom', core_pairs)]
    all_to_all x3, starting transfers between devices: 13.1 us -> 8.56 us  [body(): gathered = lax.all_to_all(spread, 'dom', 0, 0).reshape(hub_total, width)]
  transfers between devices with their start and end apart: 9 -> 9, of which waited for: 3 -> 3; matrix products, arithmetic and copies ran while one was open for 0% -> 0% of each run, Pallas kernels for 31% -> 32%
where the time goes in v6:
time: 52.8 us; the launch traced here: 52.4 us
  Pallas kernels  23.8 us (45%)
  starting transfers between devices  21.6 us (41%)
  waiting for transfers between devices  6.04 us (11%)
  between operations  0.92 us (2%)
    pallas_call x7, Pallas kernels, call(): pl.pallas_call(kernel, name=name, out_shape=out_shape, in_specs=specs, ou...  23.8 us
    ppermute x3, starting transfers between devices, body(): from_chip = lax.ppermute(to_chip, 'dom', chip_pairs)  13 us
    all_to_all x3, starting transfers between devices, body(): gathered = lax.all_to_all(spread, 'dom', 0, 0).reshape(hub_total, width)  8.56 us
    all_to_all x3, waiting for transfers between devices, body(): gathered = lax.all_to_all(spread, 'dom', 0, 0).reshape(hub_total, width)  6.02 us
  transfers between devices with their start and end apart: 9, of which 3 were waited for; matrix products, arithmetic and copies ran while one was open for 0% of the time, Pallas kernels for 32%

profile of v6, /device:TPU:0, one launch (start us, length us, event | category | flops | bytes accessed | tf_op | source)
XLA Modules:
  0.0 52.4 jit_solution(14764998438576561452)
XLA Ops:
  0.6 2.1 %prologue.1 = (bf16[256,640]{1,0:T(8,128)(2,1)S(1)}, bf16[256,640]{1,0:T(8,128)(2,1)S(1)}, bf16[32,2,640]{2,1,0:T(2,128)(2,1)}) custom-call(s32[1,2,2]{2,1,0:T(2,128)} %refs_0_.5, s32[1,2]{1,0:T(1,128)} %refs_1_.5, s32[2]{0:T(128)} %refs_2_.5, s32[8,128]{1,0:T(8,128)} %bitcast.3, bf16[1024,512]{1,0:T(8,128)(2,1)} %features_hbm.1, ...), custom_call_target="tpu_custom_call" | custom-call | flops 100000000 | tf_op jit(solution)/shard_map/prologue/pallas_call | solution.py:343
  2.7 6.5 %collective-permute-start = (bf16[256,640]{1,0:T(8,128)(2,1)S(1)}, bf16[256,640]{1,0:T(8,128)(2,1)S(1)}, u32[]{:S(2)}, u32[]{:S(2)}) collective-permute-start(bf16[256,640]{1,0:T(8,128)(2,1)S(1)} %get-tuple-element.34), channel_id=1, source_target_pairs={{1,2},{2,1},{3,4},{4,3},{5,6},{6,5},{7,8},{8,7},{9,10},{10,9},{11,... | collective-permute-start | bytes 983048 | tf_op jit(solution)/shard_map/ppermute | solution.py:376
  9.2 0.0 collective-permute-start.1
  9.2 2.6 %all-to-all-start = ((bf16[32,2,640]{2,1,0:T(2,128)(2,1)}), bf16[32,2,640]{2,1,0:T(2,128)(2,1)S(1)}, u32[]{:S(2)}, u32[]{:S(2)}) async-start(bf16[32,2,640]{2,1,0:T(2,128)(2,1)} %get-tuple-element.36), calls=%async_computation | async-start | bytes 163840 | tf_op jit(solution)/shard_map/all_to_all | solution.py:378
  11.8 5.6 %bulk0.1 = (bf16[1024,640]{1,0:T(8,128)(2,1)}, bf16[528,640]{1,0:T(8,128)(2,1)S(1)}, bf16[1024,576]{1,0:T(8,128)(2,1)}, f32[1024,128]{1,0:T(8,128)}, bf16[528,576]{1,0:T(8,128)(2,1)S(1)}, /*index=5*/f32[5,128]{1,0:T(8,128)S(1)}) custom-call(s32[1,2,2]{2,1,0:T(2,128)} %refs_0_.5, s32[1,2]{1,0:T(1,128)} %refs_1_.5, s32[2]{0:T(128)} %refs_2_.5, ...), custom_call_target="tpu_custom_call" | custom-call | flops 1342177280 | tf_op jit(solution)/shard_map/bulk0/pallas_call | solution.py:343
  17.4 2.0 %all-to-all-done = bf16[32,2,640]{2,1,0:T(2,128)(2,1)S(1)} async-done(((bf16[32,2,640]{2,1,0:T(2,128)(2,1)}), bf16[32,2,640]{2,1,0:T(2,128)(2,1)S(1)}, u32[]{:S(2)}, u32[]{:S(2)}) %all-to-all-start) | async-done | bytes 81952 | tf_op jit(solution)/shard_map/all_to_all | solution.py:378
  19.4 0.0 collective-permute-done.from_chip_ref
  19.4 0.0 collective-permute-done.1.from_core_ref
  19.4 1.1 %edge0.1 = (bf16[256,640]{1,0:T(8,128)(2,1)S(1)}, bf16[256,640]{1,0:T(8,128)(2,1)S(1)}, bf16[32,2,640]{2,1,0:T(2,128)(2,1)}, bf16[576,640]{1,0:T(8,128)(2,1)}) custom-call(bf16[528,640]{1,0:T(8,128)(2,1)S(1)} %get-tuple-element.31.own_ref, bf16[528,576]{1,0:T(8,128)(2,1)S(1)} %get-tuple-element.32.mixed_ref, ...), custom_call_target="tpu_custom_call", output_to_operand_aliasing={{0}: (3, {}), {1}: (4, {})} | custom-call | flops 754974720 | tf_op jit(solution)/shard_map/edge0/pallas_call | solution.py:343
  20.5 3.3 %collective-permute-start.2 = (bf16[256,640]{1,0:T(8,128)(2,1)S(1)}, bf16[256,640]{1,0:T(8,128)(2,1)S(1)}, u32[]{:S(2)}, u32[]{:S(2)}) collective-permute-start(bf16[256,640]{1,0:T(8,128)(2,1)S(1)} %get-tuple-element.40), channel_id=1, source_target_pairs={{1,2},{2,1},{3,4},{4,3},{5,6},{6,5},{7,8},{8,7},{9,10},{10,9},{11,... | collective-permute-start | bytes 983048 | tf_op jit(solution)/shard_map/ppermute | solution.py:376
  23.8 0.0 collective-permute-start.3
  23.8 2.9 %all-to-all-start.1 = ((bf16[32,2,640]{2,1,0:T(2,128)(2,1)}), bf16[32,2,640]{2,1,0:T(2,128)(2,1)S(1)}, u32[]{:S(2)}, u32[]{:S(2)}) async-start(bf16[32,2,640]{2,1,0:T(2,128)(2,1)} %get-tuple-element.42), calls=%async_computation.1 | async-start | bytes 163840 | tf_op jit(solution)/shard_map/all_to_all | solution.py:378
  26.7 5.5 %bulk1.1 = (bf16[3,1024,512]{2,1,0:T(8,128)(2,1)}, bf16[3,1024,128]{2,1,0:T(8,128)(2,1)}, bf16[1024,640]{1,0:T(8,128)(2,1)}, bf16[528,640]{1,0:T(8,128)(2,1)S(1)}) custom-call(s32[1,2,2]{2,1,0:T(2,128)} %refs_0_.5, s32[1,2]{1,0:T(1,128)} %refs_1_.5, s32[2]{0:T(128)} %refs_2_.5, s32[4,8]{1,0:T(4,128)} %bitcast.6, bf16[8,4,128,128]{3,2,1,0:T(8,128)(2,1)} %refs_4_.5, ...), custom_call_target="tpu_custom_call" | custom-call | flops 1342177280 | tf_op jit(solution)/shard_map/bulk1/pallas_call | solution.py:343
  32.2 2.1 %all-to-all-done.1 = bf16[32,2,640]{2,1,0:T(2,128)(2,1)S(1)} async-done(((bf16[32,2,640]{2,1,0:T(2,128)(2,1)}), bf16[32,2,640]{2,1,0:T(2,128)(2,1)S(1)}, u32[]{:S(2)}, u32[]{:S(2)}) %all-to-all-start.1) | async-done | bytes 81952 | tf_op jit(solution)/shard_map/all_to_all | solution.py:378
  34.3 0.0 collective-permute-done.2.from_chip_ref
  34.3 0.0 collective-permute-done.3.from_core_ref
  34.3 1.1 %edge1.1 = (bf16[256,640]{1,0:T(8,128)(2,1)S(1)}, bf16[256,640]{1,0:T(8,128)(2,1)S(1)}, bf16[32,2,640]{2,1,0:T(2,128)(2,1)}, bf16[576,640]{1,0:T(8,128)(2,1)}) custom-call(bf16[528,640]{1,0:T(8,128)(2,1)S(1)} %get-tuple-element.39.own_ref, bf16[528,576]{1,0:T(8,128)(2,1)S(1)} %get-tuple-element.32.mixed_ref, ...), custom_call_target="tpu_custom_call", output_to_operand_aliasing={{0}: (3, {}), {1}: (4, {})} | custom-call | flops 754974720 | tf_op jit(solution)/shard_map/edge1/pallas_call | solution.py:343
  35.4 3.2 %collective-permute-start.4 = (bf16[256,640]{1,0:T(8,128)(2,1)S(1)}, bf16[256,640]{1,0:T(8,128)(2,1)S(1)}, u32[]{:S(2)}, u32[]{:S(2)}) collective-permute-start(bf16[256,640]{1,0:T(8,128)(2,1)S(1)} %get-tuple-element.49), channel_id=1, source_target_pairs={{1,2},{2,1},{3,4},{4,3},{5,6},{6,5},{7,8},{8,7},{9,10},{10,9},{11,... | collective-permute-start | bytes 983048 | tf_op jit(solution)/shard_map/ppermute | solution.py:376
  38.6 0.0 collective-permute-start.5
  38.6 3.1 %all-to-all-start.2 = ((bf16[32,2,640]{2,1,0:T(2,128)(2,1)}), bf16[32,2,640]{2,1,0:T(2,128)(2,1)S(1)}, u32[]{:S(2)}, u32[]{:S(2)}) async-start(bf16[32,2,640]{2,1,0:T(2,128)(2,1)} %get-tuple-element.51), calls=%async_computation.2 | async-start | bytes 163840 | tf_op jit(solution)/shard_map/all_to_all | solution.py:378
  41.8 5.4 %bulk2.1 = (bf16[3,1024,512]{2,1,0:T(8,128)(2,1)}, bf16[3,1024,128]{2,1,0:T(8,128)(2,1)}, bf16[1024,640]{1,0:T(8,128)(2,1)}, bf16[1024,576]{1,0:T(8,128)(2,1)S(1)}, f32[1024,128]{1,0:T(8,128)S(1)}) custom-call(s32[1,2,2]{2,1,0:T(2,128)} %refs_0_.5, s32[1,2]{1,0:T(1,128)} %refs_1_.5, s32[2]{0:T(128)} %refs_2_.5, ...), custom_call_target="tpu_custom_call", output_to_operand_aliasing={{0}: (9, {}), {1}: (10, {})} | custom-call | flops 1342177280 | tf_op jit(solution)/shard_map/bulk2/pallas_call | solution.py:343
  47.2 2.0 %all-to-all-done.2 = bf16[32,2,640]{2,1,0:T(2,128)(2,1)S(1)} async-done(((bf16[32,2,640]{2,1,0:T(2,128)(2,1)}), bf16[32,2,640]{2,1,0:T(2,128)(2,1)S(1)}, u32[]{:S(2)}, u32[]{:S(2)}) %all-to-all-start.2) | async-done | bytes 81952 | tf_op jit(solution)/shard_map/all_to_all | solution.py:378
  49.2 0.0 collective-permute-done.4.from_chip_ref
  49.2 0.0 collective-permute-done.5.from_core_ref
  49.2 3.0 %final.1 = (bf16[3,1024,512]{2,1,0:T(8,128)(2,1)}, bf16[3,1024,128]{2,1,0:T(8,128)(2,1)}) custom-call(bf16[1024,640]{1,0:T(8,128)(2,1)} %get-tuple-element.46.own_hbm, bf16[1024,576]{1,0:T(8,128)(2,1)S(1)} %get-tuple-element.47.mixed_ref, f32[1024,128]{1,0:T(8,128)S(1)} %get-tuple-element.48.dmat_ref, ...), custom_call_target="tpu_custom_call", output_to_operand_aliasing={{0}: (6, {}), {1}: (7, {})} | custom-call | flops 754974720 | tf_op jit(solution)/shard_map/final/pallas_call | solution.py:343
  (3 shorter events, 0.1 us)
Async XLA Ops:
  2.7 16.7 %collective-permute-start = (bf16[256,640]{1,0:T(8,128)(2,1)S(1)}, bf16[256,640]{1,0:T(8,128)(2,1)S(1)}, u32[]{:S(2)}, u32[]{:S(2)}) collective-permute-start(bf16[256,640]{1,0:T(8,128)(2,1)S(1)} %get-tuple-element.34), channel_id=1, source_target_pairs={{1,2},{2,1},{3,4},{4,3},{5,6},{6,5},{7,8},{8,7},{9,10},{10,9},{11,... | collective-permute-start | bytes 983048 | tf_op jit(solution)/shard_map/ppermute | solution.py:376
  9.2 10.2 %collective-permute-start.1 = (bf16[256,640]{1,0:T(8,128)(2,1)S(1)}, bf16[256,640]{1,0:T(8,128)(2,1)S(1)}, u32[]{:S(2)}, u32[]{:S(2)}) collective-permute-start(bf16[256,640]{1,0:T(8,128)(2,1)S(1)} %get-tuple-element.35), channel_id=1, source_target_pairs={{0,1},{1,0},{2,3},{3,2},{4,5},{5,4},{6,7},{7,6},{8,9},{9,8},{10,11... | collective-permute-start | bytes 983048 | tf_op jit(solution)/shard_map/ppermute | solution.py:377
  9.2 10.2 %all-to-all-start = ((bf16[32,2,640]{2,1,0:T(2,128)(2,1)}), bf16[32,2,640]{2,1,0:T(2,128)(2,1)S(1)}, u32[]{:S(2)}, u32[]{:S(2)}) async-start(bf16[32,2,640]{2,1,0:T(2,128)(2,1)} %get-tuple-element.36), calls=%async_computation | async-start | bytes 163840 | tf_op jit(solution)/shard_map/all_to_all | solution.py:378
  20.5 13.8 %collective-permute-start.2 = (bf16[256,640]{1,0:T(8,128)(2,1)S(1)}, bf16[256,640]{1,0:T(8,128)(2,1)S(1)}, u32[]{:S(2)}, u32[]{:S(2)}) collective-permute-start(bf16[256,640]{1,0:T(8,128)(2,1)S(1)} %get-tuple-element.40), channel_id=1, source_target_pairs={{1,2},{2,1},{3,4},{4,3},{5,6},{6,5},{7,8},{8,7},{9,10},{10,9},{11,... | collective-permute-start | bytes 983048 | tf_op jit(solution)/shard_map/ppermute | solution.py:376
  23.8 10.5 %collective-permute-start.3 = (bf16[256,640]{1,0:T(8,128)(2,1)S(1)}, bf16[256,640]{1,0:T(8,128)(2,1)S(1)}, u32[]{:S(2)}, u32[]{:S(2)}) collective-permute-start(bf16[256,640]{1,0:T(8,128)(2,1)S(1)} %get-tuple-element.41), channel_id=1, source_target_pairs={{0,1},{1,0},{2,3},{3,2},{4,5},{5,4},{6,7},{7,6},{8,9},{9,8},{10,11... | collective-permute-start | bytes 983048 | tf_op jit(solution)/shard_map/ppermute | solution.py:377
  23.8 10.4 %all-to-all-start.1 = ((bf16[32,2,640]{2,1,0:T(2,128)(2,1)}), bf16[32,2,640]{2,1,0:T(2,128)(2,1)S(1)}, u32[]{:S(2)}, u32[]{:S(2)}) async-start(bf16[32,2,640]{2,1,0:T(2,128)(2,1)} %get-tuple-element.42), calls=%async_computation.1 | async-start | bytes 163840 | tf_op jit(solution)/shard_map/all_to_all | solution.py:378
  35.4 13.8 %collective-permute-start.4 = (bf16[256,640]{1,0:T(8,128)(2,1)S(1)}, bf16[256,640]{1,0:T(8,128)(2,1)S(1)}, u32[]{:S(2)}, u32[]{:S(2)}) collective-permute-start(bf16[256,640]{1,0:T(8,128)(2,1)S(1)} %get-tuple-element.49), channel_id=1, source_target_pairs={{1,2},{2,1},{3,4},{4,3},{5,6},{6,5},{7,8},{8,7},{9,10},{10,9},{11,... | collective-permute-start | bytes 983048 | tf_op jit(solution)/shard_map/ppermute | solution.py:376
  38.6 10.6 %collective-permute-start.5 = (bf16[256,640]{1,0:T(8,128)(2,1)S(1)}, bf16[256,640]{1,0:T(8,128)(2,1)S(1)}, u32[]{:S(2)}, u32[]{:S(2)}) collective-permute-start(bf16[256,640]{1,0:T(8,128)(2,1)S(1)} %get-tuple-element.50), channel_id=1, source_target_pairs={{0,1},{1,0},{2,3},{3,2},{4,5},{5,4},{6,7},{7,6},{8,9},{9,8},{10,11... | collective-permute-start | bytes 983048 | tf_op jit(solution)/shard_map/ppermute | solution.py:377
  38.6 10.5 %all-to-all-start.2 = ((bf16[32,2,640]{2,1,0:T(2,128)(2,1)}), bf16[32,2,640]{2,1,0:T(2,128)(2,1)S(1)}, u32[]{:S(2)}, u32[]{:S(2)}) async-start(bf16[32,2,640]{2,1,0:T(2,128)(2,1)} %get-tuple-element.51), calls=%async_computation.2 | async-start | bytes 163840 | tf_op jit(solution)/shard_map/all_to_all | solution.py:378

commit v7 on v6

--- a/solution.py
+++ b/solution.py
@@ -13,6 +13,7 @@
 BF16 = jnp.bfloat16
 F32 = jnp.float32
 GROUP = 16
+KEPT = 2
 
 
 def scale_rows(value, dmat):
@@ -163,16 +164,17 @@
     first, last = hop == 0, hop == HOPS - 1
     if first:
         degree_hbm, features_hbm, embeddings_hbm, weight_hbm = take(4)
-        own_hbm, own_sent, mixed_out, dmat_out, mixed_sent, roots_sent = take(6)
+        own_hbm, own_tail, own_sent, mixed_out, dmat_out, mixed_sent, roots_sent = take(7)
     else:
         old_own_hbm, mixed_hbm, dmat_hbm, received_hbm = take(4)
         if hop > 1:
             take(2)
+        (old_tail,) = take(1)
         all_features, all_embeddings, own_hbm = take(3)
         if last:
             mixed_ref, dmat_ref = take(2)
         else:
-            (own_sent,) = take(1)
+            own_tail, own_sent = take(2)
     blocks_ref, count_ref, hubs_ref, columns_ref = take(4)
     tiles_ref, z_ref, own_ref, features_ref, embeddings_ref = take(5)
     if not last:
@@ -201,19 +203,23 @@
             z_ref[rows, :split] = scale_rows(features_ref[rows, :].astype(F32), dmat).astype(BF16)
             z_ref[rows, split:] = scale_rows(embeddings_ref[rows, :].astype(F32), dmat).astype(BF16)
     else:
-        inputs = copies.start((received_hbm, received), (dmat_hbm, dmat_ref))
-        parts = [
-            copies.start((mixed_hbm.at[rows, :], mixed_ref.at[rows, :]), (old_own_hbm.at[rows, :], old_own_ref.at[rows, :]))
-            for rows in quarters(row_count)
-        ]
+        inputs = copies.start((received_hbm, received))
+        held = old_own_ref.shape[0]
+        parts = []
+        for rows in every:
+            pairs = [(mixed_hbm.at[rows, :], mixed_ref.at[rows, :]), (dmat_hbm.at[rows, :], dmat_ref.at[rows, :])]
+            if rows.stop <= held:
+                pairs.append((old_own_hbm.at[rows, :], old_own_ref.at[rows, :]))
+            parts.append(copies.start(*pairs))
         late = copies.start((tiles_hbm, tiles_ref))
         finish(inputs)
         for b, rows in enumerate(every):
-            if b * len(parts) % blocks == 0:
-                finish(parts[b * len(parts) // blocks])
+            if b % 4 == 0:
+                finish([copy for part in parts[b : b + 4] for copy in part])
             total = jnp.dot(mixed_ref[rows, :], received[...], preferred_element_type=F32)
             dmat = dmat_ref[rows, :]
-            fresh = scale_rows(old_own_ref[rows, :].astype(F32) + total, dmat).astype(BF16)
+            old = old_own_ref[rows, :] if rows.stop <= held else old_tail[rows.start - held : rows.stop - held, :]
+            fresh = scale_rows(old.astype(F32) + total, dmat).astype(BF16)
             features_ref[rows, :] = fresh[:, :split]
             embeddings_ref[rows, :] = fresh[:, split:]
             z_ref[rows, :] = scale_rows(fresh.astype(F32), dmat).astype(BF16)
@@ -228,10 +234,12 @@
             [jnp.where(c < blocks, t, jnp.zeros_like(t)) for c, t in zip(columns, tiles)], axis=1
         )
         picked = jnp.concatenate([z_ref[block_rows(jnp.minimum(c, blocks - 1), tile), :] for c in columns], axis=0)
-        own_ref[rows, :] = jnp.dot(values, picked, preferred_element_type=F32).astype(BF16)
-        if b % 2:
-            pair = slice((b - 1) * tile, (b + 1) * tile)
-            writes += copies.start((own_ref.at[pair, :], own_hbm.at[pair, :]))
+        own = jnp.dot(values, picked, preferred_element_type=F32).astype(BF16)
+        own_ref[rows, :] = own
+        if rows.stop <= own_hbm.shape[0]:
+            writes += copies.start((own_ref.at[rows, :], own_hbm.at[rows, :]))
+        else:
+            own_tail[rows.start - own_hbm.shape[0] : rows.stop - own_hbm.shape[0], :] = own
         if first:
             for slot in range(rim):
                 total = jnp.zeros((tile, tile), F32)
@@ -239,8 +247,6 @@
                     total += jnp.where(c == blocks + slot, t, jnp.zeros_like(t)).astype(F32)
                 mixed_ref[rows, slot * tile : (slot + 1) * tile] = total.astype(BF16)
             mixed_ref[rows, rim * tile :] = weight_ref[:, rows].astype(F32).T.astype(BF16)
-    if blocks % 2:
-        writes += copies.start((own_ref.at[every[-1], :], own_hbm.at[every[-1], :]))
     if first:
         writes += copies.start((mixed_ref, mixed_out), (dmat_ref, dmat_out))
     if not last:
@@ -288,16 +294,22 @@
     copies = Copies(sems)
     split = features_ref.shape[1]
     row_count = own_ref.shape[0]
-    reads = copies.start((own_hbm, own_ref))
+    half = row_count // 2
+    reads = [
+        copies.start((own_hbm.at[rows, :], own_ref.at[rows, :]))
+        for rows in (slice(0, half), slice(half, row_count))
+    ]
     place_received(from_chip_ref, from_core_ref, gathered_ref, received)
     tile = dmat_ref.shape[1]
     parts = [slice(at, at + tile) for at in range(0, row_count, tile)]
     ahead = len(parts) // 2
     for rows in parts[:ahead]:
         total_ref[rows, :] = jnp.dot(mixed_ref[rows, :], received[...], preferred_element_type=F32)
-    finish(reads)
+    finish(reads[0])
     writes = []
     for i, rows in enumerate(parts):
+        if i == ahead:
+            finish(reads[1])
         if i < ahead:
             total = total_ref[rows, :]
         else:
@@ -384,34 +396,36 @@
         if not last:
             scratch += [VMEM((row_count, deep), BF16), VMEM((row_count, tile), F32)]
         aliases = {}
-        full_own = pltpu.HBM((row_count, width), BF16)
-        sent_shapes = [shape((sent, width), BF16), shape((sent, deep), BF16)]
+        tail = 0 if last else KEPT * tile
+        full_own = pltpu.HBM((row_count - tail, width), BF16)
+        sent_shapes = [shape((tail, width), BF16), shape((sent, width), BF16), shape((sent, deep), BF16)]
         if first:
             operands = fixed + rows + pin(hub_weight.T)
             out_shape = [full_own] + sent_shapes + [shape((rim + 1, tile), F32)]
-            out_shape[2:2] = [pltpu.HBM((row_count, deep), BF16), pltpu.HBM((row_count, tile), F32)]
+            out_shape[3:3] = [pltpu.HBM((row_count, deep), BF16), pltpu.HBM((row_count, tile), F32)]
             scratch += [VMEM((blocks, tile), int32), VMEM((hub_total, row_count), BF16)]
         else:
             operands = fixed + pin(own, mixed, dmat, received)
             if out:
                 aliases = {len(operands): 0, len(operands) + 1: 1}
                 operands += pin(*out)
+            operands += [own_tail]
             out_shape = whole + [full_own]
-            out_shape += [shape((row_count, deep), BF16), shape((row_count, tile), F32)] if last else sent_shapes[:1]
-            scratch += [VMEM((deep, width), BF16), VMEM((row_count, width), BF16)]
+            out_shape += [shape((row_count, deep), BF16), shape((row_count, tile), F32)] if last else sent_shapes[:2]
+            scratch += [VMEM((deep, width), BF16), VMEM((row_count - KEPT * tile, width), BF16)]
         got = call(
             functools.partial(bulk_kernel, hop=hop, rim=rim, per_block=per_block), f"bulk{hop}",
-            4 * row_count * per_block * tile * width, out_shape, scratch, 20 + blocks,
-            len(operands), operands, aliases,
+            4 * row_count * per_block * tile * width, out_shape, scratch, 12 + 4 * blocks,
+            len(operands) - (not first), operands, aliases,
         )
         if first:
-            own, own_sent, mixed, dmat, mixed_sent, roots_sent = got
+            own, own_tail, own_sent, mixed, dmat, mixed_sent, roots_sent = got
         else:
             out, (own, *got) = got[:2], got[2:]
             if last:
                 mixed_here, dmat_here = got
             else:
-                (own_sent,) = got
+                own_tail, own_sent = got
 
         flops = 2 * row_count * deep * width
         if last:
@@ -420,7 +434,7 @@
             out = call(
                 final_kernel, "final", flops, whole,
                 [VMEM((row_count, width), BF16), VMEM((row_count, width), F32)] + row_buffers
-                + [VMEM((deep, width), BF16)], 1 + 2 * blocks,
+                + [VMEM((deep, width), BF16)], 2 + 2 * blocks,
                 1, operands + pin(*out), aliases,
             )
         else:

time: 52.8 us -> 52.6 us (level)
  Pallas kernels: 23.8 us -> 23.1 us
    pallas_call x7, Pallas kernels: 23.8 us -> 23.1 us  [call(): pl.pallas_call(kernel, name=name, out_shape=out_shape, in_specs=specs, ou...]
  transfers between devices with their start and end apart: 9 -> 9, of which waited for: 3 -> 3; matrix products, arithmetic and copies ran while one was open for 0% -> 0% of each run, Pallas kernels for 32% -> 31%
where the time goes in v7:
time: 52.6 us; the launch traced here: 52.2 us
  Pallas kernels  23.1 us (44%)
  starting transfers between devices  21.6 us (41%)
  waiting for transfers between devices  6.53 us (12%)
  between operations  0.92 us (2%)
    pallas_call x7, Pallas kernels, call(): pl.pallas_call(kernel, name=name, out_shape=out_shape, in_specs=specs, ou...  23.1 us
    ppermute x3, starting transfers between devices, body(): from_chip = lax.ppermute(to_chip, 'dom', chip_pairs)  12.6 us
    all_to_all x3, starting transfers between devices, body(): gathered = lax.all_to_all(spread, 'dom', 0, 0).reshape(hub_total, width)  8.9 us
    all_to_all x3, waiting for transfers between devices, body(): gathered = lax.all_to_all(spread, 'dom', 0, 0).reshape(hub_total, width)  6.51 us
  transfers between devices with their start and end apart: 9, of which 3 were waited for; matrix products, arithmetic and copies ran while one was open for 0% of the time, Pallas kernels for 31%

profile of v7, /device:TPU:0, one launch (start us, length us, event | category | flops | bytes accessed | tf_op | source)
XLA Modules:
  0.0 52.2 jit_solution(13723407452443907254)
XLA Ops:
  0.6 2.1 %prologue.1 = (bf16[256,640]{1,0:T(8,128)(2,1)S(1)}, bf16[256,640]{1,0:T(8,128)(2,1)S(1)}, bf16[32,2,640]{2,1,0:T(2,128)(2,1)}) custom-call(s32[1,2,2]{2,1,0:T(2,128)} %refs_0_.5, s32[1,2]{1,0:T(1,128)} %refs_1_.5, s32[2]{0:T(128)} %refs_2_.5, s32[8,128]{1,0:T(8,128)} %bitcast.3, bf16[1024,512]{1,0:T(8,128)(2,1)} %features_hbm.1, ...), custom_call_target="tpu_custom_call" | custom-call | flops 100000000 | tf_op jit(solution)/shard_map/prologue/pallas_call | solution.py:355
  2.7 6.5 %collective-permute-start = (bf16[256,640]{1,0:T(8,128)(2,1)S(1)}, bf16[256,640]{1,0:T(8,128)(2,1)S(1)}, u32[]{:S(2)}, u32[]{:S(2)}) collective-permute-start(bf16[256,640]{1,0:T(8,128)(2,1)S(1)} %get-tuple-element.36), channel_id=1, source_target_pairs={{1,2},{2,1},{3,4},{4,3},{5,6},{6,5},{7,8},{8,7},{9,10},{10,9},{11,... | collective-permute-start | bytes 983048 | tf_op jit(solution)/shard_map/ppermute | solution.py:388
  9.2 0.0 collective-permute-start.1
  9.2 2.6 %all-to-all-start = ((bf16[32,2,640]{2,1,0:T(2,128)(2,1)}), bf16[32,2,640]{2,1,0:T(2,128)(2,1)S(1)}, u32[]{:S(2)}, u32[]{:S(2)}) async-start(bf16[32,2,640]{2,1,0:T(2,128)(2,1)} %get-tuple-element.38), calls=%async_computation | async-start | bytes 163840 | tf_op jit(solution)/shard_map/all_to_all | solution.py:390
  11.8 5.7 %bulk0.1 = (bf16[768,640]{1,0:T(8,128)(2,1)}, bf16[256,640]{1,0:T(8,128)(2,1)S(1)}, bf16[528,640]{1,0:T(8,128)(2,1)S(1)}, bf16[1024,576]{1,0:T(8,128)(2,1)}, f32...) custom-call(s32[1,2,2]{2,1,0:T(2,128)} %refs_0_.5, s32[1,2]{1,0:T(1,128)} %refs_1_.5, ...), custom_call_target="tpu_custom_call" | custom-call | flops 1342177280 | tf_op jit(solution)/shard_map/bulk0/pallas_call | solution.py:355
  17.5 1.9 %all-to-all-done = bf16[32,2,640]{2,1,0:T(2,128)(2,1)S(1)} async-done(((bf16[32,2,640]{2,1,0:T(2,128)(2,1)}), bf16[32,2,640]{2,1,0:T(2,128)(2,1)S(1)}, u32[]{:S(2)}, u32[]{:S(2)}) %all-to-all-start) | async-done | bytes 81952 | tf_op jit(solution)/shard_map/all_to_all | solution.py:390
  19.4 0.0 collective-permute-done.from_chip_ref
  19.4 0.0 collective-permute-done.1.from_core_ref
  19.4 1.1 %edge0.1 = (bf16[256,640]{1,0:T(8,128)(2,1)S(1)}, bf16[256,640]{1,0:T(8,128)(2,1)S(1)}, bf16[32,2,640]{2,1,0:T(2,128)(2,1)}, bf16[576,640]{1,0:T(8,128)(2,1)}) custom-call(bf16[528,640]{1,0:T(8,128)(2,1)S(1)} %get-tuple-element.33.own_ref, bf16[528,576]{1,0:T(8,128)(2,1)S(1)} %get-tuple-element.34.mixed_ref, ...), custom_call_target="tpu_custom_call", output_to_operand_aliasing={{0}: (3, {}), {1}: (4, {})} | custom-call | flops 754974720 | tf_op jit(solution)/shard_map/edge0/pallas_call | solution.py:355
  20.5 3.4 %collective-permute-start.2 = (bf16[256,640]{1,0:T(8,128)(2,1)S(1)}, bf16[256,640]{1,0:T(8,128)(2,1)S(1)}, u32[]{:S(2)}, u32[]{:S(2)}) collective-permute-start(bf16[256,640]{1,0:T(8,128)(2,1)S(1)} %get-tuple-element.43), channel_id=1, source_target_pairs={{1,2},{2,1},{3,4},{4,3},{5,6},{6,5},{7,8},{8,7},{9,10},{10,9},{11,... | collective-permute-start | bytes 983048 | tf_op jit(solution)/shard_map/ppermute | solution.py:388
  23.9 0.0 collective-permute-start.3
  23.9 2.8 %all-to-all-start.1 = ((bf16[32,2,640]{2,1,0:T(2,128)(2,1)}), bf16[32,2,640]{2,1,0:T(2,128)(2,1)S(1)}, u32[]{:S(2)}, u32[]{:S(2)}) async-start(bf16[32,2,640]{2,1,0:T(2,128)(2,1)} %get-tuple-element.45), calls=%async_computation.1 | async-start | bytes 163840 | tf_op jit(solution)/shard_map/all_to_all | solution.py:390
  26.7 5.1 %bulk1.1 = (bf16[3,1024,512]{2,1,0:T(8,128)(2,1)}, bf16[3,1024,128]{2,1,0:T(8,128)(2,1)}, bf16[768,640]{1,0:T(8,128)(2,1)}, bf16[256,640]{1,0:T(8,128)(2,1)S(1)}, bf16[528,640]{1,0:T(8,128)(2,1)S(1)}) custom-call(s32[1,2,2]{2,1,0:T(2,128)} %refs_0_.5, s32[1,2]{1,0:T(1,128)} %refs_1_.5, s32[2]{0:T(128)} %refs_2_.5, s32[4,8]{1,0:T(4,128)} %bitcast.6, ...), custom_call_target="tpu_custom_call" | custom-call | flops 1342177280 | tf_op jit(solution)/shard_map/bulk1/pallas_call | solution.py:355
  31.7 2.5 %all-to-all-done.1 = bf16[32,2,640]{2,1,0:T(2,128)(2,1)S(1)} async-done(((bf16[32,2,640]{2,1,0:T(2,128)(2,1)}), bf16[32,2,640]{2,1,0:T(2,128)(2,1)S(1)}, u32[]{:S(2)}, u32[]{:S(2)}) %all-to-all-start.1) | async-done | bytes 81952 | tf_op jit(solution)/shard_map/all_to_all | solution.py:390
  34.3 0.0 collective-permute-done.2.from_chip_ref
  34.3 0.0 collective-permute-done.3.from_core_ref
  34.3 1.1 %edge1.1 = (bf16[256,640]{1,0:T(8,128)(2,1)S(1)}, bf16[256,640]{1,0:T(8,128)(2,1)S(1)}, bf16[32,2,640]{2,1,0:T(2,128)(2,1)}, bf16[576,640]{1,0:T(8,128)(2,1)}) custom-call(bf16[528,640]{1,0:T(8,128)(2,1)S(1)} %get-tuple-element.42.own_ref, bf16[528,576]{1,0:T(8,128)(2,1)S(1)} %get-tuple-element.34.mixed_ref, ...), custom_call_target="tpu_custom_call", output_to_operand_aliasing={{0}: (3, {}), {1}: (4, {})} | custom-call | flops 754974720 | tf_op jit(solution)/shard_map/edge1/pallas_call | solution.py:355
  35.4 2.8 %collective-permute-start.4 = (bf16[256,640]{1,0:T(8,128)(2,1)S(1)}, bf16[256,640]{1,0:T(8,128)(2,1)S(1)}, u32[]{:S(2)}, u32[]{:S(2)}) collective-permute-start(bf16[256,640]{1,0:T(8,128)(2,1)S(1)} %get-tuple-element.53), channel_id=1, source_target_pairs={{1,2},{2,1},{3,4},{4,3},{5,6},{6,5},{7,8},{8,7},{9,10},{10,9},{11,... | collective-permute-start | bytes 983048 | tf_op jit(solution)/shard_map/ppermute | solution.py:388
  38.1 0.0 collective-permute-start.5
  38.2 3.6 %all-to-all-start.2 = ((bf16[32,2,640]{2,1,0:T(2,128)(2,1)}), bf16[32,2,640]{2,1,0:T(2,128)(2,1)S(1)}, u32[]{:S(2)}, u32[]{:S(2)}) async-start(bf16[32,2,640]{2,1,0:T(2,128)(2,1)} %get-tuple-element.55), calls=%async_computation.2 | async-start | bytes 163840 | tf_op jit(solution)/shard_map/all_to_all | solution.py:390
  41.7 5.3 %bulk2.1 = (bf16[3,1024,512]{2,1,0:T(8,128)(2,1)}, bf16[3,1024,128]{2,1,0:T(8,128)(2,1)}, bf16[1024,640]{1,0:T(8,128)(2,1)}, bf16[1024,576]{1,0:T(8,128)(2,1)S(1)}, f32[1024,128]{1,0:T(8,128)S(1)}) custom-call(s32[1,2,2]{2,1,0:T(2,128)} %refs_0_.5, s32[1,2]{1,0:T(1,128)} %refs_1_.5, s32[2]{0:T(128)} %refs_2_.5, ...), custom_call_target="tpu_custom_call", output_to_operand_aliasing={{0}: (9, {}), {1}: (10, {})} | custom-call | flops 1342177280 | tf_op jit(solution)/shard_map/bulk2/pallas_call | solution.py:355
  47.0 2.1 %all-to-all-done.2 = bf16[32,2,640]{2,1,0:T(2,128)(2,1)S(1)} async-done(((bf16[32,2,640]{2,1,0:T(2,128)(2,1)}), bf16[32,2,640]{2,1,0:T(2,128)(2,1)S(1)}, u32[]{:S(2)}, u32[]{:S(2)}) %all-to-all-start.2) | async-done | bytes 81952 | tf_op jit(solution)/shard_map/all_to_all | solution.py:390
  49.2 0.0 collective-permute-done.4.from_chip_ref
  49.2 0.0 collective-permute-done.5.from_core_ref
  49.2 2.9 %final.1 = (bf16[3,1024,512]{2,1,0:T(8,128)(2,1)}, bf16[3,1024,128]{2,1,0:T(8,128)(2,1)}) custom-call(bf16[1024,640]{1,0:T(8,128)(2,1)} %get-tuple-element.50.own_hbm, bf16[1024,576]{1,0:T(8,128)(2,1)S(1)} %get-tuple-element.51.mixed_ref, f32[1024,128]{1,0:T(8,128)S(1)} %get-tuple-element.52.dmat_ref, ...), custom_call_target="tpu_custom_call", output_to_operand_aliasing={{0}: (6, {}), {1}: (7, {})} | custom-call | flops 754974720 | tf_op jit(solution)/shard_map/final/pallas_call | solution.py:355
  (3 shorter events, 0.1 us)
Async XLA Ops:
  2.7 16.7 %collective-permute-start = (bf16[256,640]{1,0:T(8,128)(2,1)S(1)}, bf16[256,640]{1,0:T(8,128)(2,1)S(1)}, u32[]{:S(2)}, u32[]{:S(2)}) collective-permute-start(bf16[256,640]{1,0:T(8,128)(2,1)S(1)} %get-tuple-element.36), channel_id=1, source_target_pairs={{1,2},{2,1},{3,4},{4,3},{5,6},{6,5},{7,8},{8,7},{9,10},{10,9},{11,... | collective-permute-start | bytes 983048 | tf_op jit(solution)/shard_map/ppermute | solution.py:388
  9.2 10.2 %collective-permute-start.1 = (bf16[256,640]{1,0:T(8,128)(2,1)S(1)}, bf16[256,640]{1,0:T(8,128)(2,1)S(1)}, u32[]{:S(2)}, u32[]{:S(2)}) collective-permute-start(bf16[256,640]{1,0:T(8,128)(2,1)S(1)} %get-tuple-element.37), channel_id=1, source_target_pairs={{0,1},{1,0},{2,3},{3,2},{4,5},{5,4},{6,7},{7,6},{8,9},{9,8},{10,11... | collective-permute-start | bytes 983048 | tf_op jit(solution)/shard_map/ppermute | solution.py:389
  9.2 10.2 %all-to-all-start = ((bf16[32,2,640]{2,1,0:T(2,128)(2,1)}), bf16[32,2,640]{2,1,0:T(2,128)(2,1)S(1)}, u32[]{:S(2)}, u32[]{:S(2)}) async-start(bf16[32,2,640]{2,1,0:T(2,128)(2,1)} %get-tuple-element.38), calls=%async_computation | async-start | bytes 163840 | tf_op jit(solution)/shard_map/all_to_all | solution.py:390
  20.5 13.8 %collective-permute-start.2 = (bf16[256,640]{1,0:T(8,128)(2,1)S(1)}, bf16[256,640]{1,0:T(8,128)(2,1)S(1)}, u32[]{:S(2)}, u32[]{:S(2)}) collective-permute-start(bf16[256,640]{1,0:T(8,128)(2,1)S(1)} %get-tuple-element.43), channel_id=1, source_target_pairs={{1,2},{2,1},{3,4},{4,3},{5,6},{6,5},{7,8},{8,7},{9,10},{10,9},{11,... | collective-permute-start | bytes 983048 | tf_op jit(solution)/shard_map/ppermute | solution.py:388
  23.9 10.4 %collective-permute-start.3 = (bf16[256,640]{1,0:T(8,128)(2,1)S(1)}, bf16[256,640]{1,0:T(8,128)(2,1)S(1)}, u32[]{:S(2)}, u32[]{:S(2)}) collective-permute-start(bf16[256,640]{1,0:T(8,128)(2,1)S(1)} %get-tuple-element.44), channel_id=1, source_target_pairs={{0,1},{1,0},{2,3},{3,2},{4,5},{5,4},{6,7},{7,6},{8,9},{9,8},{10,11... | collective-permute-start | bytes 983048 | tf_op jit(solution)/shard_map/ppermute | solution.py:389
  23.9 10.4 %all-to-all-start.1 = ((bf16[32,2,640]{2,1,0:T(2,128)(2,1)}), bf16[32,2,640]{2,1,0:T(2,128)(2,1)S(1)}, u32[]{:S(2)}, u32[]{:S(2)}) async-start(bf16[32,2,640]{2,1,0:T(2,128)(2,1)} %get-tuple-element.45), calls=%async_computation.1 | async-start | bytes 163840 | tf_op jit(solution)/shard_map/all_to_all | solution.py:390
  35.4 13.8 %collective-permute-start.4 = (bf16[256,640]{1,0:T(8,128)(2,1)S(1)}, bf16[256,640]{1,0:T(8,128)(2,1)S(1)}, u32[]{:S(2)}, u32[]{:S(2)}) collective-permute-start(bf16[256,640]{1,0:T(8,128)(2,1)S(1)} %get-tuple-element.53), channel_id=1, source_target_pairs={{1,2},{2,1},{3,4},{4,3},{5,6},{6,5},{7,8},{8,7},{9,10},{10,9},{11,... | collective-permute-start | bytes 983048 | tf_op jit(solution)/shard_map/ppermute | solution.py:388
  38.1 11.0 %collective-permute-start.5 = (bf16[256,640]{1,0:T(8,128)(2,1)S(1)}, bf16[256,640]{1,0:T(8,128)(2,1)S(1)}, u32[]{:S(2)}, u32[]{:S(2)}) collective-permute-start(bf16[256,640]{1,0:T(8,128)(2,1)S(1)} %get-tuple-element.54), channel_id=1, source_target_pairs={{0,1},{1,0},{2,3},{3,2},{4,5},{5,4},{6,7},{7,6},{8,9},{9,8},{10,11... | collective-permute-start | bytes 983048 | tf_op jit(solution)/shard_map/ppermute | solution.py:389
  38.2 11.0 %all-to-all-start.2 = ((bf16[32,2,640]{2,1,0:T(2,128)(2,1)}), bf16[32,2,640]{2,1,0:T(2,128)(2,1)S(1)}, u32[]{:S(2)}, u32[]{:S(2)}) async-start(bf16[32,2,640]{2,1,0:T(2,128)(2,1)} %get-tuple-element.55), calls=%async_computation.2 | async-start | bytes 163840 | tf_op jit(solution)/shard_map/all_to_all | solution.py:390

commit v8 on v7

--- a/solution.py
+++ b/solution.py
@@ -140,12 +140,13 @@
     finish(tables)
     listed = slots(blocks_ref, count_ref)
     factors = [factor_block(degree_ref, index) for index, _ in listed]
+    hub_factors = [jnp.broadcast_to(root, (1, tile)) for root in hub_roots(degree_ref, hubs_ref)]
     finish(rows)
     hubs = []
-    for i, root in enumerate(hub_roots(degree_ref, hubs_ref)):
+    for i, factor in enumerate(hub_factors):
         row = hubs_ref[i]
         whole = jnp.concatenate([one_row(features_ref, row), one_row(embeddings_ref, row)], axis=1)
-        hubs.append(scale_rows(whole, jnp.broadcast_to(root, (1, tile))))
+        hubs.append(scale_rows(whole, factor))
     writes = spread_rows(jnp.concatenate(hubs, axis=0).astype(BF16), spread_ref, spread_hbm, copies)
     half = len(listed) // 2
     for i, (index, live) in enumerate(listed):

time: 52.6 us -> 52.5 us (level)
  no operation moved by 1% of the time
where the time goes in v8:
time: 52.5 us; the launch traced here: 52.2 us
  Pallas kernels  23.1 us (44%)
  starting transfers between devices  21.6 us (41%)
  waiting for transfers between devices  6.52 us (12%)
  between operations  0.92 us (2%)
    pallas_call x7, Pallas kernels, call(): pl.pallas_call(kernel, name=name, out_shape=out_shape, in_specs=specs, ou...  23.1 us
    ppermute x3, starting transfers between devices, body(): from_chip = lax.ppermute(to_chip, 'dom', chip_pairs)  12.6 us
    all_to_all x3, starting transfers between devices, body(): gathered = lax.all_to_all(spread, 'dom', 0, 0).reshape(hub_total, width)  8.9 us
    all_to_all x3, waiting for transfers between devices, body(): gathered = lax.all_to_all(spread, 'dom', 0, 0).reshape(hub_total, width)  6.51 us
  transfers between devices with their start and end apart: 9, of which 3 were waited for; matrix products, arithmetic and copies ran while one was open for 0% of the time, Pallas kernels for 31%

profile of v8, /device:TPU:0, one launch (start us, length us, event | category | flops | bytes accessed | tf_op | source)
XLA Modules:
  0.0 52.2 jit_solution(279562005859659565)
XLA Ops:
  0.6 2.0 %prologue.1 = (bf16[256,640]{1,0:T(8,128)(2,1)S(1)}, bf16[256,640]{1,0:T(8,128)(2,1)S(1)}, bf16[32,2,640]{2,1,0:T(2,128)(2,1)}) custom-call(s32[1,2,2]{2,1,0:T(2,128)} %refs_0_.5, s32[1,2]{1,0:T(1,128)} %refs_1_.5, s32[2]{0:T(128)} %refs_2_.5, s32[8,128]{1,0:T(8,128)} %bitcast.3, bf16[1024,512]{1,0:T(8,128)(2,1)} %features_hbm.1, ...), custom_call_target="tpu_custom_call" | custom-call | flops 100000000 | tf_op jit(solution)/shard_map/prologue/pallas_call | solution.py:356
  2.7 6.5 %collective-permute-start = (bf16[256,640]{1,0:T(8,128)(2,1)S(1)}, bf16[256,640]{1,0:T(8,128)(2,1)S(1)}, u32[]{:S(2)}, u32[]{:S(2)}) collective-permute-start(bf16[256,640]{1,0:T(8,128)(2,1)S(1)} %get-tuple-element.36), channel_id=1, source_target_pairs={{1,2},{2,1},{3,4},{4,3},{5,6},{6,5},{7,8},{8,7},{9,10},{10,9},{11,... | collective-permute-start | bytes 983048 | tf_op jit(solution)/shard_map/ppermute | solution.py:389
  9.1 0.0 collective-permute-start.1
  9.1 2.6 %all-to-all-start = ((bf16[32,2,640]{2,1,0:T(2,128)(2,1)}), bf16[32,2,640]{2,1,0:T(2,128)(2,1)S(1)}, u32[]{:S(2)}, u32[]{:S(2)}) async-start(bf16[32,2,640]{2,1,0:T(2,128)(2,1)} %get-tuple-element.38), calls=%async_computation | async-start | bytes 163840 | tf_op jit(solution)/shard_map/all_to_all | solution.py:391
  11.7 5.7 %bulk0.1 = (bf16[768,640]{1,0:T(8,128)(2,1)}, bf16[256,640]{1,0:T(8,128)(2,1)S(1)}, bf16[528,640]{1,0:T(8,128)(2,1)S(1)}, bf16[1024,576]{1,0:T(8,128)(2,1)}, f32...) custom-call(s32[1,2,2]{2,1,0:T(2,128)} %refs_0_.5, s32[1,2]{1,0:T(1,128)} %refs_1_.5, ...), custom_call_target="tpu_custom_call" | custom-call | flops 1342177280 | tf_op jit(solution)/shard_map/bulk0/pallas_call | solution.py:356
  17.4 1.9 %all-to-all-done = bf16[32,2,640]{2,1,0:T(2,128)(2,1)S(1)} async-done(((bf16[32,2,640]{2,1,0:T(2,128)(2,1)}), bf16[32,2,640]{2,1,0:T(2,128)(2,1)S(1)}, u32[]{:S(2)}, u32[]{:S(2)}) %all-to-all-start) | async-done | bytes 81952 | tf_op jit(solution)/shard_map/all_to_all | solution.py:391
  19.3 0.0 collective-permute-done.from_chip_ref
  19.3 0.0 collective-permute-done.1.from_core_ref
  19.4 1.1 %edge0.1 = (bf16[256,640]{1,0:T(8,128)(2,1)S(1)}, bf16[256,640]{1,0:T(8,128)(2,1)S(1)}, bf16[32,2,640]{2,1,0:T(2,128)(2,1)}, bf16[576,640]{1,0:T(8,128)(2,1)}) custom-call(bf16[528,640]{1,0:T(8,128)(2,1)S(1)} %get-tuple-element.33.own_ref, bf16[528,576]{1,0:T(8,128)(2,1)S(1)} %get-tuple-element.34.mixed_ref, ...), custom_call_target="tpu_custom_call", output_to_operand_aliasing={{0}: (3, {}), {1}: (4, {})} | custom-call | flops 754974720 | tf_op jit(solution)/shard_map/edge0/pallas_call | solution.py:356
  20.4 3.4 %collective-permute-start.2 = (bf16[256,640]{1,0:T(8,128)(2,1)S(1)}, bf16[256,640]{1,0:T(8,128)(2,1)S(1)}, u32[]{:S(2)}, u32[]{:S(2)}) collective-permute-start(bf16[256,640]{1,0:T(8,128)(2,1)S(1)} %get-tuple-element.43), channel_id=1, source_target_pairs={{1,2},{2,1},{3,4},{4,3},{5,6},{6,5},{7,8},{8,7},{9,10},{10,9},{11,... | collective-permute-start | bytes 983048 | tf_op jit(solution)/shard_map/ppermute | solution.py:389
  23.8 0.0 collective-permute-start.3
  23.8 2.8 %all-to-all-start.1 = ((bf16[32,2,640]{2,1,0:T(2,128)(2,1)}), bf16[32,2,640]{2,1,0:T(2,128)(2,1)S(1)}, u32[]{:S(2)}, u32[]{:S(2)}) async-start(bf16[32,2,640]{2,1,0:T(2,128)(2,1)} %get-tuple-element.45), calls=%async_computation.1 | async-start | bytes 163840 | tf_op jit(solution)/shard_map/all_to_all | solution.py:391
  26.6 5.1 %bulk1.1 = (bf16[3,1024,512]{2,1,0:T(8,128)(2,1)}, bf16[3,1024,128]{2,1,0:T(8,128)(2,1)}, bf16[768,640]{1,0:T(8,128)(2,1)}, bf16[256,640]{1,0:T(8,128)(2,1)S(1)}, bf16[528,640]{1,0:T(8,128)(2,1)S(1)}) custom-call(s32[1,2,2]{2,1,0:T(2,128)} %refs_0_.5, s32[1,2]{1,0:T(1,128)} %refs_1_.5, s32[2]{0:T(128)} %refs_2_.5, s32[4,8]{1,0:T(4,128)} %bitcast.6, ...), custom_call_target="tpu_custom_call" | custom-call | flops 1342177280 | tf_op jit(solution)/shard_map/bulk1/pallas_call | solution.py:356
  31.7 2.5 %all-to-all-done.1 = bf16[32,2,640]{2,1,0:T(2,128)(2,1)S(1)} async-done(((bf16[32,2,640]{2,1,0:T(2,128)(2,1)}), bf16[32,2,640]{2,1,0:T(2,128)(2,1)S(1)}, u32[]{:S(2)}, u32[]{:S(2)}) %all-to-all-start.1) | async-done | bytes 81952 | tf_op jit(solution)/shard_map/all_to_all | solution.py:391
  34.2 0.0 collective-permute-done.2.from_chip_ref
  34.2 0.0 collective-permute-done.3.from_core_ref
  34.2 1.1 %edge1.1 = (bf16[256,640]{1,0:T(8,128)(2,1)S(1)}, bf16[256,640]{1,0:T(8,128)(2,1)S(1)}, bf16[32,2,640]{2,1,0:T(2,128)(2,1)}, bf16[576,640]{1,0:T(8,128)(2,1)}) custom-call(bf16[528,640]{1,0:T(8,128)(2,1)S(1)} %get-tuple-element.42.own_ref, bf16[528,576]{1,0:T(8,128)(2,1)S(1)} %get-tuple-element.34.mixed_ref, ...), custom_call_target="tpu_custom_call", output_to_operand_aliasing={{0}: (3, {}), {1}: (4, {})} | custom-call | flops 754974720 | tf_op jit(solution)/shard_map/edge1/pallas_call | solution.py:356
  35.3 2.8 %collective-permute-start.4 = (bf16[256,640]{1,0:T(8,128)(2,1)S(1)}, bf16[256,640]{1,0:T(8,128)(2,1)S(1)}, u32[]{:S(2)}, u32[]{:S(2)}) collective-permute-start(bf16[256,640]{1,0:T(8,128)(2,1)S(1)} %get-tuple-element.53), channel_id=1, source_target_pairs={{1,2},{2,1},{3,4},{4,3},{5,6},{6,5},{7,8},{8,7},{9,10},{10,9},{11,... | collective-permute-start | bytes 983048 | tf_op jit(solution)/shard_map/ppermute | solution.py:389
  38.1 0.0 collective-permute-start.5
  38.1 3.6 %all-to-all-start.2 = ((bf16[32,2,640]{2,1,0:T(2,128)(2,1)}), bf16[32,2,640]{2,1,0:T(2,128)(2,1)S(1)}, u32[]{:S(2)}, u32[]{:S(2)}) async-start(bf16[32,2,640]{2,1,0:T(2,128)(2,1)} %get-tuple-element.55), calls=%async_computation.2 | async-start | bytes 163840 | tf_op jit(solution)/shard_map/all_to_all | solution.py:391
  41.7 5.3 %bulk2.1 = (bf16[3,1024,512]{2,1,0:T(8,128)(2,1)}, bf16[3,1024,128]{2,1,0:T(8,128)(2,1)}, bf16[1024,640]{1,0:T(8,128)(2,1)}, bf16[1024,576]{1,0:T(8,128)(2,1)S(1)}, f32[1024,128]{1,0:T(8,128)S(1)}) custom-call(s32[1,2,2]{2,1,0:T(2,128)} %refs_0_.5, s32[1,2]{1,0:T(1,128)} %refs_1_.5, s32[2]{0:T(128)} %refs_2_.5, ...), custom_call_target="tpu_custom_call", output_to_operand_aliasing={{0}: (9, {}), {1}: (10, {})} | custom-call | flops 1342177280 | tf_op jit(solution)/shard_map/bulk2/pallas_call | solution.py:356
  46.9 2.1 %all-to-all-done.2 = bf16[32,2,640]{2,1,0:T(2,128)(2,1)S(1)} async-done(((bf16[32,2,640]{2,1,0:T(2,128)(2,1)}), bf16[32,2,640]{2,1,0:T(2,128)(2,1)S(1)}, u32[]{:S(2)}, u32[]{:S(2)}) %all-to-all-start.2) | async-done | bytes 81952 | tf_op jit(solution)/shard_map/all_to_all | solution.py:391
  49.1 0.0 collective-permute-done.4.from_chip_ref
  49.1 0.0 collective-permute-done.5.from_core_ref
  49.1 2.9 %final.1 = (bf16[3,1024,512]{2,1,0:T(8,128)(2,1)}, bf16[3,1024,128]{2,1,0:T(8,128)(2,1)}) custom-call(bf16[1024,640]{1,0:T(8,128)(2,1)} %get-tuple-element.50.own_hbm, bf16[1024,576]{1,0:T(8,128)(2,1)S(1)} %get-tuple-element.51.mixed_ref, f32[1024,128]{1,0:T(8,128)S(1)} %get-tuple-element.52.dmat_ref, ...), custom_call_target="tpu_custom_call", output_to_operand_aliasing={{0}: (6, {}), {1}: (7, {})} | custom-call | flops 754974720 | tf_op jit(solution)/shard_map/final/pallas_call | solution.py:356
  (3 shorter events, 0.1 us)
Async XLA Ops:
  2.7 16.7 %collective-permute-start = (bf16[256,640]{1,0:T(8,128)(2,1)S(1)}, bf16[256,640]{1,0:T(8,128)(2,1)S(1)}, u32[]{:S(2)}, u32[]{:S(2)}) collective-permute-start(bf16[256,640]{1,0:T(8,128)(2,1)S(1)} %get-tuple-element.36), channel_id=1, source_target_pairs={{1,2},{2,1},{3,4},{4,3},{5,6},{6,5},{7,8},{8,7},{9,10},{10,9},{11,... | collective-permute-start | bytes 983048 | tf_op jit(solution)/shard_map/ppermute | solution.py:389
  9.1 10.2 %collective-permute-start.1 = (bf16[256,640]{1,0:T(8,128)(2,1)S(1)}, bf16[256,640]{1,0:T(8,128)(2,1)S(1)}, u32[]{:S(2)}, u32[]{:S(2)}) collective-permute-start(bf16[256,640]{1,0:T(8,128)(2,1)S(1)} %get-tuple-element.37), channel_id=1, source_target_pairs={{0,1},{1,0},{2,3},{3,2},{4,5},{5,4},{6,7},{7,6},{8,9},{9,8},{10,11... | collective-permute-start | bytes 983048 | tf_op jit(solution)/shard_map/ppermute | solution.py:390
  9.1 10.2 %all-to-all-start = ((bf16[32,2,640]{2,1,0:T(2,128)(2,1)}), bf16[32,2,640]{2,1,0:T(2,128)(2,1)S(1)}, u32[]{:S(2)}, u32[]{:S(2)}) async-start(bf16[32,2,640]{2,1,0:T(2,128)(2,1)} %get-tuple-element.38), calls=%async_computation | async-start | bytes 163840 | tf_op jit(solution)/shard_map/all_to_all | solution.py:391
  20.4 13.8 %collective-permute-start.2 = (bf16[256,640]{1,0:T(8,128)(2,1)S(1)}, bf16[256,640]{1,0:T(8,128)(2,1)S(1)}, u32[]{:S(2)}, u32[]{:S(2)}) collective-permute-start(bf16[256,640]{1,0:T(8,128)(2,1)S(1)} %get-tuple-element.43), channel_id=1, source_target_pairs={{1,2},{2,1},{3,4},{4,3},{5,6},{6,5},{7,8},{8,7},{9,10},{10,9},{11,... | collective-permute-start | bytes 983048 | tf_op jit(solution)/shard_map/ppermute | solution.py:389
  23.8 10.4 %collective-permute-start.3 = (bf16[256,640]{1,0:T(8,128)(2,1)S(1)}, bf16[256,640]{1,0:T(8,128)(2,1)S(1)}, u32[]{:S(2)}, u32[]{:S(2)}) collective-permute-start(bf16[256,640]{1,0:T(8,128)(2,1)S(1)} %get-tuple-element.44), channel_id=1, source_target_pairs={{0,1},{1,0},{2,3},{3,2},{4,5},{5,4},{6,7},{7,6},{8,9},{9,8},{10,11... | collective-permute-start | bytes 983048 | tf_op jit(solution)/shard_map/ppermute | solution.py:390
  23.8 10.3 %all-to-all-start.1 = ((bf16[32,2,640]{2,1,0:T(2,128)(2,1)}), bf16[32,2,640]{2,1,0:T(2,128)(2,1)S(1)}, u32[]{:S(2)}, u32[]{:S(2)}) async-start(bf16[32,2,640]{2,1,0:T(2,128)(2,1)} %get-tuple-element.45), calls=%async_computation.1 | async-start | bytes 163840 | tf_op jit(solution)/shard_map/all_to_all | solution.py:391
  35.3 13.8 %collective-permute-start.4 = (bf16[256,640]{1,0:T(8,128)(2,1)S(1)}, bf16[256,640]{1,0:T(8,128)(2,1)S(1)}, u32[]{:S(2)}, u32[]{:S(2)}) collective-permute-start(bf16[256,640]{1,0:T(8,128)(2,1)S(1)} %get-tuple-element.53), channel_id=1, source_target_pairs={{1,2},{2,1},{3,4},{4,3},{5,6},{6,5},{7,8},{8,7},{9,10},{10,9},{11,... | collective-permute-start | bytes 983048 | tf_op jit(solution)/shard_map/ppermute | solution.py:389
  38.1 11.0 %collective-permute-start.5 = (bf16[256,640]{1,0:T(8,128)(2,1)S(1)}, bf16[256,640]{1,0:T(8,128)(2,1)S(1)}, u32[]{:S(2)}, u32[]{:S(2)}) collective-permute-start(bf16[256,640]{1,0:T(8,128)(2,1)S(1)} %get-tuple-element.54), channel_id=1, source_target_pairs={{0,1},{1,0},{2,3},{3,2},{4,5},{5,4},{6,7},{7,6},{8,9},{9,8},{10,11... | collective-permute-start | bytes 983048 | tf_op jit(solution)/shard_map/ppermute | solution.py:390
  38.1 11.0 %all-to-all-start.2 = ((bf16[32,2,640]{2,1,0:T(2,128)(2,1)}), bf16[32,2,640]{2,1,0:T(2,128)(2,1)S(1)}, u32[]{:S(2)}, u32[]{:S(2)}) async-start(bf16[32,2,640]{2,1,0:T(2,128)(2,1)} %get-tuple-element.55), calls=%async_computation.2 | async-start | bytes 163840 | tf_op jit(solution)/shard_map/all_to_all | solution.py:391
